TPU v7x, 512 devices: a whole 4x8x8 slice. The times are simulated.
512 devices in a mesh: tile: 128 (over y, z, core), shell: 4 (over x).
Axes of the slice: x: 4, y: 8, z: 8, core: 2. Of those that a mesh axis runs over, the one named last changes fastest.
Arguments:
- particles: bfloat16 [4096, 2, 32768], P('tile', None, 'shell'), may hold values from -40 to 40
- projections: bfloat16 [4096, 2, 32768], P('tile', None, 'shell'), may hold values from -6 to 6
- noise_weight: float32 [32768], P('shell'), may hold values from 0.001 to 0.012
- tile_list: int32 [4096, 4], P('tile'), may hold values from 0 to 127, all different within a row; in each aligned block of 32 rows (0 to 31, 32 to 63, ...) at most 2 rows name the same one
- ori_start: int32 [4096, 4], P('tile'), may hold values from 0 to 31
- shifts: int32 [4096, 2], P('tile'), may hold values from -8 to 8
- defocus_bin: int32 [4096], P('tile'), may hold values from 0 to 15
Outputs:
- posterior: float32 [4096, 9, 64], P('tile')
- log_evidence: float32 [4096], P('tile')
Inputs may be any that keep to these rules, and one draw needn't show every extreme that they name: `tile_list`: the 4 tiles of one particle differ, and among the particles of one index of tile no tile is named more than 2 times, a count reached.
All inputs are finite; a program needn't handle non-finite values.
Results may differ from a plain program's by a relative error of at most 0.0035.
Values may be sent and summed in bfloat16 or wider, within the bound.
No kernel may reach another device: no remote copies, remote signals or barrier semaphores. Data moves between devices by JAX's collectives and lax.ppermute only.
A program may use at most 128 MiB of HBM per device.

v0:
```python
import math

import jax
import jax.numpy as jnp
from jax import lax
from jax.sharding import Mesh
from jax.sharding import PartitionSpec as P

BOX = 256
NBIN = 16
TSIDE = 3
TILE = ("tile_0", "tile_1", "tile_2")


wave_length = 0.0197
aberration = 27000000.0
amplitude = 0.1
b_factor = 20.0
defocus_base = 5000.0
defocus_step = 500.0


def split_up(array, dim, size):
    before, after = (array.shape[:dim], array.shape[dim + 1 :])
    return jnp.moveaxis(array.reshape(*before, size, -1, *after), dim, 0)


def joined_along(tiles, dim):
    shape = list(tiles.shape[1:])
    shape[dim] *= tiles.shape[0]
    return jnp.moveaxis(tiles, 0, dim).reshape(shape)


def moved_by_axis(tiles, axes, turns):
    shape = [lax.axis_size(a) for a in axes]
    tiles = tiles.reshape(*shape, *tiles.shape[1:])
    for k in turns:
        tiles = lax.all_to_all(tiles, axes[k], split_axis=k, concat_axis=k, tiled=True)
    return tiles.reshape(-1, *tiles.shape[len(axes) :])


def core_and_chips(array, groups, turns, split_dim, concat_dim):
    size = lax.axis_size(groups[0]) * lax.axis_size(groups[1])
    tiles = split_up(array, split_dim, size)
    return joined_along(moved_by_axis(tiles, groups, turns), concat_dim)


def copy_for_each(array, axis):
    copies = jnp.broadcast_to(array, (lax.axis_size(axis), *array.shape))
    return lax.all_to_all(copies, axis, split_axis=0, concat_axis=0, tiled=True)


def taken_together(array, axis):
    everything = copy_for_each(array, axis)
    return jnp.sum(everything, axis=0)


def together(arrays, axis):
    vector, at, outs = (jnp.concatenate([a.reshape(-1) for a in arrays]), 0, [])
    total = taken_together(vector, axis)
    for a in arrays:
        outs.append(total[at : at + a.size].reshape(a.shape))
        at += a.size
    return tuple(outs)


def frequencies(first_index, span_count):
    flat_index = first_index + jnp.arange(span_count, dtype=jnp.int32)
    freq_x = flat_index // BOX
    freq_y = flat_index % BOX - BOX // 2
    return (freq_x, freq_y)


def ctf_table(freq_x, freq_y, bins_count):
    scaled_x = freq_x.astype(jnp.float32) / BOX
    scaled_y = freq_y.astype(jnp.float32) / BOX
    radius_sq = scaled_x * scaled_x + scaled_y * scaled_y
    defocus = defocus_base + defocus_step * jnp.arange(bins_count, dtype=jnp.float32)[:, None]
    aberr_phase = (
        math.pi * wave_length * defocus * radius_sq[None, :]
        - 0.5 * math.pi * aberration * wave_length**3 * radius_sq[None, :] ** 2
    )
    envelope = jnp.exp(-0.25 * b_factor * radius_sq)[None, :]
    return (
        -(math.sqrt(1.0 - amplitude**2) * jnp.sin(aberr_phase) + amplitude * jnp.cos(aberr_phase))
        * envelope
    )


def rotation(freq_x, freq_y, mult_x, mult_y):
    phase_turns = jnp.mod(freq_x * mult_x + freq_y * mult_y, BOX)
    angles = phase_turns.astype(jnp.float32) * (2.0 * math.pi / BOX)
    return (jnp.cos(angles), jnp.sin(angles))


def pick_rows(bin_index, lookup):
    one_hot = (bin_index[:, None] == jnp.arange(lookup.shape[0], dtype=jnp.int32)[None, :]).astype(
        jnp.float32
    )
    return jnp.dot(
        one_hot, lookup, precision=lax.Precision.HIGHEST, preferred_element_type=jnp.float32
    )


def prepare(particles, weight, ctf_rows, shifts, freq_x, freq_y):
    values = particles.astype(jnp.float32)
    real_part = values[:, 0]
    imag_part = values[:, 1]
    cosine, sine_value = rotation(freq_x[None, :], freq_y[None, :], shifts[:, 0:1], shifts[:, 1:2])
    moved_real = real_part * cosine + imag_part * sine_value
    moved_imag = imag_part * cosine - real_part * sine_value
    factor = weight[None, :] * ctf_rows
    weighted = jnp.stack([factor * moved_real, factor * moved_imag], axis=1).astype(jnp.bfloat16)
    energy = jnp.sum(weight[None, :] * (real_part * real_part + imag_part * imag_part), axis=1)
    return (weighted, energy)


def shifted_tables(projections, freq_x, freq_y):
    offsets = jnp.arange(TSIDE, dtype=jnp.int32) - TSIDE // 2
    mult_x = jnp.repeat(offsets, TSIDE)[:, None]
    mult_y = jnp.tile(offsets, TSIDE)[:, None]
    cosine, sine_value = rotation(freq_x[None, :], freq_y[None, :], mult_x, mult_y)
    cosine = cosine[:, None, :]
    sine_value = sine_value[:, None, :]
    proj_real = projections[:, 0].astype(jnp.float32)[None, :, :]
    proj_imag = projections[:, 1].astype(jnp.float32)[None, :, :]
    moved_real = proj_real * cosine - proj_imag * sine_value
    moved_imag = proj_imag * cosine + proj_real * sine_value
    stacked = jnp.stack([moved_real, moved_imag], axis=2).astype(jnp.bfloat16)
    return stacked.reshape(TSIDE * TSIDE * projections.shape[0], -1)


def slot_scores(slot_rows, bin_index, projections, weight, ctf, freq_x, freq_y):
    orient_count = projections.shape[0]
    lookup = shifted_tables(projections, freq_x, freq_y)
    cross_term = lax.dot_general(
        slot_rows, lookup, (((1,), (1,)), ((), ())), preferred_element_type=jnp.float32
    )
    cross_term = cross_term.reshape(slot_rows.shape[0], TSIDE * TSIDE, orient_count)
    proj_values = projections.astype(jnp.float32)
    magnitude = proj_values[:, 0] * proj_values[:, 0] + proj_values[:, 1] * proj_values[:, 1]
    weighted_ctf = weight[None, :] * ctf * ctf
    power = lax.dot_general(
        weighted_ctf,
        magnitude,
        (((1,), (1,)), ((), ())),
        precision=lax.Precision.HIGHEST,
        preferred_element_type=jnp.float32,
    )
    power_rows = pick_rows(bin_index, power)
    return cross_term - 0.5 * power_rows[:, None, :]


def window(scores, starts, orient_count):
    orient_index = jnp.mod(
        starts[:, None] + jnp.arange(orient_count // 2, dtype=jnp.int32)[None, :], orient_count
    )
    return jnp.take_along_axis(scores, orient_index[:, None, :], axis=2)


def slot_layout(tile_ids, tile_count, capacity):
    positions = jnp.arange(tile_ids.shape[0], dtype=jnp.int32)
    earlier_same = (tile_ids[:, None] == tile_ids[None, :]) & (
        positions[None, :] < positions[:, None]
    )
    slot_rank = jnp.sum(earlier_same.astype(jnp.int32), axis=1)
    slot_index = tile_ids * capacity + slot_rank
    matches = slot_index[None, :] == jnp.arange(tile_count * capacity, dtype=jnp.int32)[:, None]
    slot_owner = jnp.sum(jnp.where(matches, positions[None, :] + 1, 0), axis=1) - 1
    return (slot_index, slot_owner)


def finish(scores, energy_sum):
    scored = scores - 0.5 * energy_sum[:, None, None]
    row_peak = jnp.max(scored, axis=(1, 2))
    log_total = row_peak + jnp.log(jnp.sum(jnp.exp(scored - row_peak[:, None, None]), axis=(1, 2)))
    posterior = jnp.exp(scored - log_total[:, None, None])
    return (posterior, log_total)


def per_device(particles, projections, noise_weight, tile_list, ori_start, shifts, defocus_bin):
    tile_count = lax.axis_size(TILE)
    band_index = lax.axis_index("shell")
    local_count = particles.shape[0]
    window_count = tile_list.shape[1]
    band_width = particles.shape[2]
    orient_count = projections.shape[0]
    capacity = max(2, (2 * local_count * window_count + tile_count - 1) // tile_count)
    freq_x, freq_y = frequencies(band_index * band_width, band_width)
    ctf = ctf_table(freq_x, freq_y, NBIN)
    weighted, energy = prepare(
        particles, noise_weight, pick_rows(defocus_bin, ctf), shifts, freq_x, freq_y
    )
    weighted = weighted.reshape(local_count, 2 * band_width)
    slot_index, slot_owner = slot_layout(tile_list.reshape(-1), tile_count, capacity)
    occupied = slot_owner >= 0
    item_index = jnp.maximum(slot_owner, 0)
    particle = item_index // window_count
    starts_flat = ori_start.reshape(-1)
    send_rows = jnp.where(
        occupied[:, None], jnp.take(weighted, particle, axis=0), jnp.zeros((), jnp.bfloat16)
    )
    send_rows = send_rows.reshape(tile_count, capacity, 2 * band_width)
    send_labels = jnp.stack(
        [jnp.take(defocus_bin, particle), jnp.take(starts_flat, item_index)], axis=1
    )
    send_labels = send_labels.astype(jnp.bfloat16).reshape(tile_count, capacity, 2)
    payload = lax.all_to_all(send_rows, TILE, split_axis=0, concat_axis=0, tiled=True)
    labels = lax.all_to_all(send_labels, TILE, split_axis=0, concat_axis=0, tiled=True)
    source_count = payload.shape[0]
    slot_count = payload.shape[1]
    slot_rows = payload.reshape(source_count * slot_count, payload.shape[2])
    label_ints = labels.reshape(source_count * slot_count, 2).astype(jnp.int32)
    partial_value = slot_scores(
        slot_rows, label_ints[:, 0], projections, noise_weight, ctf, freq_x, freq_y
    )
    partial_value = partial_value.reshape(
        source_count, slot_count, partial_value.shape[1], partial_value.shape[2]
    )
    returned = core_and_chips(partial_value, (("tile_0", "tile_1"), "tile_2"), (1, 0), 0, 0)
    candidates = returned.shape[2]
    returned = jnp.take(
        returned.reshape(tile_count * capacity, candidates, returned.shape[3]), slot_index, axis=0
    )
    returned = window(returned, starts_flat, orient_count)
    kept = returned.shape[2]
    returned = returned.reshape(local_count, window_count, candidates, kept)
    scores = jnp.transpose(returned, (0, 2, 1, 3)).reshape(
        local_count, candidates, window_count * kept
    )
    scores, energy_sum = together((scores, energy), "shell")
    return finish(scores, energy_sum)


def solution(mesh):
    split = Mesh(
        mesh.devices.reshape(8, 8, 2, mesh.shape["shell"]), ("tile_0", "tile_1", "tile_2", "shell")
    )
    in_specs = (
        P(TILE, None, "shell"),
        P(TILE, None, "shell"),
        P("shell"),
        P(TILE, None),
        P(TILE, None),
        P(TILE, None),
        P(TILE),
    )
    out_specs = (P(TILE, None, None), P(TILE))
    return jax.shard_map(
        per_device, mesh=split, in_specs=in_specs, out_specs=out_specs, check_vma=False
    )
```

profile of v0, /device:TPU:1, one launch (start us, length us, event | category | flops | bytes accessed | tf_op | source)
XLA Modules:
  0.0 453.4 jit_solution(7667772477958521209)
XLA Ops:
  0.6 0.8 copy.85
  1.9 2.1 fusion.54
  3.9 1.8 fusion.55
  5.8 0.8 copy.84
  6.7 1.9 gather_fusion.1
  8.9 20.1 %compare_select_fusion.7 = s32[256]{0:T(256)S(1)} fusion(s32[256]{0:T(256)S(1)} %bitcast.118, s32[]{:T(128)} %bitcast.10, s32[]{:T(128)} %bitcast.11, s32[]{:T(128)} %bitcast.12, s32[]{:T(128)} %bitcast.13, s32[]{:T(128)} %bitcast.14, s32[]{:T(128)} %bitcast.15, s32[]{:T(128)} %bitcast.16, s32[]{:T(128)} %bitcast.17, s32[]{:T(128)} %bitcast.18, ...), kind=kLoop, calls=%fused_computation.123 | loop fusion | flops 15872 | bytes 2176 | tf_op jit(solution)/shard_map/jit(_take)/gather | solution.py:205
  29.3 0.7 copy.91
  30.0 18.7 %all-to-all-start.1 = ((bf16[128,2,2]{1,2,0:T(2,128)(2,1)}), bf16[128,2,2]{1,2,0:T(2,128)(2,1)S(1)}, u32[]{:S(2)}, u32[]{:S(2)}) async-start(bf16[128,2,2]{1,2,0:T(2,128)(2,1)} %copy.91), calls=%async_computation.1 | async-start | bytes 131072 | tf_op jit(solution)/shard_map/all_to_all | solution.py:209
  49.2 0.8 slice_bitcast_fusion.5
  50.0 1.8 copy_convert_fusion
  51.8 8.2 %fusion.12 = (bf16[32,1,8192]{2,0,1:T(8,128)(2,1)S(1)}, bf16[32,1,8192]{2,0,1:T(8,128)(2,1)S(1)}, f32[32]{0:T(128)S(1)}) fusion(f32[32,2,8192]{2,0,1:T(8,128)S(1)} %copy_convert_fusion, s32[32]{0:T(128)S(1)} %get-tuple-element.30, s32[8192]{0:T(1024)S(1)} %get-tuple-element.64, s32[32]{0:T(128)S(1)} %get-tuple-element.29, s32[8192]{0:T(1024)S(1)} %get-tuple-element.63, ...), kind=kOutput, calls=%fused_computation.40 | convolution fusion | flops 59638240 | bytes 3342912 | tf_op jit(solution)/shard_map/dot_general | solution.py:100
  60.2 9.0 %gather_fusion = bf16[256,16384]{1,0:T(8,128)(2,1)} fusion(bf16[32,16384]{1,0:T(8,128)(2,1)S(1)} %bitcast.108, s32[1024]{0:T(1024)S(1)} %pad_clamp_fusion.2), kind=kCustom, calls=%fused_computation | custom fusion | bytes 16778240 | tf_op jit(solution)/shard_map/jit(_take)/gather | solution.py:201
  69.2 14.0 %gather.27 = bf16[128,2,16384]{2,1,0:T(2,128)(2,1)} reshape(bf16[256,16384]{1,0:T(8,128)(2,1)} %gather_fusion) | data formatting | bytes 16777216 | tf_op jit(solution)/shard_map/jit(_take)/gather | solution.py:201
  83.5 11.6 %broadcast_select_fusion.1 = bf16[128,2,16384]{2,1,0:T(2,128)(2,1)} fusion(pred[128,2]{1,0:T(8,128)(4,1)S(1)} %ge.64, bf16[128,2,16384]{2,1,0:T(2,128)(2,1)} %gather.27, pred[128,2]{1,0:T(8,128)(4,1)S(1)} %compare_and_fusion), kind=kLoop, calls=%fused_computation.5 | loop fusion | flops 8388608 | bytes 16777728 | tf_op jit(solution)/shard_map/jit(_where)/select_n | solution.py:200
  95.1 14.7 %all-to-all-start = ((bf16[128,2,16384]{2,1,0:T(2,128)(2,1)}), bf16[128,2,16384]{2,1,0:T(2,128)(2,1)}, u32[]{:S(2)}, u32[]{:S(2)}) async-start(bf16[128,2,16384]{2,1,0:T(2,128)(2,1)} %broadcast_select_fusion.1), calls=%async_computation | async-start | bytes 16777216 | tf_op jit(solution)/shard_map/all_to_all | solution.py:208
  110.1 2.1 fusion.17
  112.2 0.7 copy_convert_fusion.1
  113.0 21.1 %subtract_convert_fusion = (bf16[9,32,1,8192]{3,2,1,0:T(2,128)(2,1)}, bf16[9,32,1,8192]{3,2,1,0:T(2,128)(2,1)}) fusion(f32[9,8192]{1,0:T(8,128)S(1)} %get-tuple-element.24, f32[32,8192]{1,0:T(8,128)S(1)} %get-tuple-element.22, f32[9,8192]{1,0:T(8,128)S(1)} %get-tuple-element.23, f32[32,8192]{1,0:T(8,128)S(1)} %get-tuple-element.21), kind=kLoop, calls=%fused_computation.8 | loop fusion | flops 18874368 | bytes 12124160 | tf_op jit(solution)/shard_map/convert.8
  134.2 24.0 %pad_maximum_fusion = bf16[9,32,2,8192]{3,2,1,0:T(2,128)(2,1)} fusion(bf16[9,32,1,8192]{3,2,1,0:T(2,128)(2,1)} %get-tuple-element.17, bf16[9,32,1,8192]{3,2,1,0:T(2,128)(2,1)} %get-tuple-element.16), kind=kLoop, calls=%fused_computation.6 | loop fusion | flops 18874368 | bytes 18874368 | tf_op jit(solution)/shard_map/stack | solution.py:129
  158.2 16.6 %convert_element_type.104 = bf16[9,32,16384]{2,1,0:T(8,128)(2,1)} reshape(bf16[9,32,2,8192]{3,2,1,0:T(2,128)(2,1)} %pad_maximum_fusion) | data formatting | bytes 18874368 | tf_op jit(solution)/shard_map/convert_element_type | solution.py:129
  174.9 3.0 fusion.5
  178.4 169.6 %all-to-all-done = bf16[128,2,16384]{2,1,0:T(2,128)(2,1)} async-done(((bf16[128,2,16384]{2,1,0:T(2,128)(2,1)}), bf16[128,2,16384]{2,1,0:T(2,128)(2,1)}, u32[]{:S(2)}, u32[]{:S(2)}) %all-to-all-start) | async-done | bytes 8388640 | tf_op jit(solution)/shard_map/all_to_all | solution.py:208
  348.1 13.1 %reshape.701 = bf16[256,16384,1]{1,0,2:T(8,128)(2,1)} reshape(bf16[128,2,16384]{2,1,0:T(2,128)(2,1)} %all-to-all-done) | data formatting | bytes 16777216 | tf_op jit(solution)/shard_map/reshape | solution.py:212
  361.2 10.7 %convolution_subtract_fusion = f32[256,9,32]{0,2,1:T(8,128)S(1)} fusion(bf16[256,16384,1]{1,0,2:T(8,128)(2,1)} %reshape.701, bf16[9,32,16384]{2,1,0:T(8,128)(2,1)} %convert_element_type.104, f32[256,32]{0,1:T(8,128)S(1)} %convolution_multiply_fusion.1), kind=kOutput, calls=%fused_computation.13 | convolution fusion | flops 2415992832 | bytes 18153472 | tf_op jit(solution)/shard_map/dot_general | solution.py:136
  372.3 1.1 copy.95
  373.4 0.4 reshape.706
  373.8 3.6 all_to_all.26
  377.4 0.5 broadcast.1183
  377.9 1.6 reduce.1
  379.4 0.4 reshape.707
  379.8 0.8 copy.96
  380.6 1.9 reshape.708
  382.5 22.5 %all-to-all-start.3 = ((f32[64,1,1152]{2,1,0:T(1,128)}), f32[64,1,1152]{2,1,0:T(1,128)S(1)}, u32[]{:S(2)}, u32[]{:S(2)}) async-start(f32[64,1,1152]{2,1,0:T(1,128)} %reshape.708), calls=%async_computation.3 | async-start | bytes 589824 | tf_op jit(solution)/shard_map/all_to_all | solution.py:38
  405.6 13.2 %all-to-all-done.3 = f32[64,1,1152]{2,1,0:T(1,128)S(1)} async-done(((f32[64,1,1152]{2,1,0:T(1,128)}), f32[64,1,1152]{2,1,0:T(1,128)S(1)}, u32[]{:S(2)}, u32[]{:S(2)}) %all-to-all-start.3) | async-done | bytes 294944 | tf_op jit(solution)/shard_map/all_to_all | solution.py:38
  418.8 1.4 reduce.2
  420.1 0.9 reshape.709
  421.1 0.5 copy.97
  421.5 0.7 copy.99
  422.3 1.7 gather_fusion.2
  424.0 1.4 broadcast_select_fusion.2
  425.5 0.8 copy.100
  426.3 13.0 %gather_fusion.3 = f32[2048,9]{1,0:T(8,128)S(1)} fusion(f32[128,9,32]{1,2,0:T(8,128)S(1)} %copy.100, s32[2048]{0:T(1024)S(1)} %reshape.684), kind=kCustom, calls=%fused_computation.3 | custom fusion | bytes 163840 | tf_op jit(solution)/shard_map/jit(take_along_axis)/gather | solution.py:158
  439.3 0.9 copy.101
  440.5 0.4 reshape_reshape.3
  441.1 9.5 %all_to_all.27 = f32[4,1,18464]{2,1,0:T(1,128)S(1)} all-to-all(f32[4,1,18464]{2,1,0:T(1,128)S(1)} %broadcast_in_dim.113), channel_id=1, replica_groups=mesh['tile_0'=8,'tile_1'=8,'tile_2'=2,'shell'=4] {'shell'}, dimensions={0} | all-to-all | bytes 590848 | tf_op jit(solution)/shard_map/all_to_all | solution.py:50
  451.0 0.5 subtract_reduce_fusion
  451.5 0.6 exponential_reduce_fusion
  452.3 0.7 copy.104
  (66 shorter events, 4.8 us)
Async XLA Ops:
  30.0 65.1 %all-to-all-start.1 = ((bf16[128,2,2]{1,2,0:T(2,128)(2,1)}), bf16[128,2,2]{1,2,0:T(2,128)(2,1)S(1)}, u32[]{:S(2)}, u32[]{:S(2)}) async-start(bf16[128,2,2]{1,2,0:T(2,128)(2,1)} %copy.91), calls=%async_computation.1 | async-start | bytes 131072 | tf_op jit(solution)/shard_map/all_to_all | solution.py:209
  95.1 17.2 %copy-start = (bf16[32,2,8192]{2,1,0:T(2,128)(2,1)S(1)}, bf16[32,2,8192]{2,1,0:T(2,128)(2,1)}, u32[]{:S(2)}) copy-start(bf16[32,2,8192]{2,1,0:T(2,128)(2,1)} %param.8) | copy-start | bytes 3145732
  95.1 253.0 %all-to-all-start = ((bf16[128,2,16384]{2,1,0:T(2,128)(2,1)}), bf16[128,2,16384]{2,1,0:T(2,128)(2,1)}, u32[]{:S(2)}, u32[]{:S(2)}) async-start(bf16[128,2,16384]{2,1,0:T(2,128)(2,1)} %broadcast_select_fusion.1), calls=%async_computation | async-start | bytes 16777216 | tf_op jit(solution)/shard_map/all_to_all | solution.py:208
  158.2 16.8 %copy-start.3 = (f32[8192]{0:T(1024)S(1)}, f32[8192]{0:T(1024)}, u32[]{:S(2)}) copy-start(f32[8192]{0:T(1024)} %param.9) | copy-start | bytes 98308
  371.9 33.2 %copy-start.1 = (s32[32,4]{0,1:T(4,128)S(1)}, s32[32,4]{0,1:T(4,128)}, u32[]{:S(2)}) copy-start(s32[32,4]{0,1:T(4,128)} %param.10) | copy-start | bytes 1540
  382.5 36.2 %all-to-all-start.3 = ((f32[64,1,1152]{2,1,0:T(1,128)}), f32[64,1,1152]{2,1,0:T(1,128)S(1)}, u32[]{:S(2)}, u32[]{:S(2)}) async-start(f32[64,1,1152]{2,1,0:T(1,128)} %reshape.708), calls=%async_computation.3 | async-start | bytes 589824 | tf_op jit(solution)/shard_map/all_to_all | solution.py:38
  452.1 0.9 copy-start.2
where the time goes:
time: 460 us; the launch traced here: 453 us
  waiting for transfers between devices  183 us (40%)
  local copies, waits for them, and re-layouts  89.1 us (19%)
  other arithmetic  88.6 us (19%)
  starting transfers between devices  56 us (12%)
  matrix products  22.2 us (5%)
  blocking collectives  13.1 us (3%)
    all_to_all x1, waiting for transfers between devices, per_device(): lax.all_to_all(send_rows, TILE, split_axis=0, concat_axis=0, tiled=True)  170 us
    another operation x1, other arithmetic, shifted_tables(): stacked = jnp.stack([moved_real, moved_imag], axis=2).astype(jnp.bfloat16)  24 us
    gather x2, local copies, waits for them, and re-layouts, per_device(): jnp.take(weighted, particle, axis=0)  23.1 us
    all_to_all x1, starting transfers between devices, moved_by_axis(): lax.all_to_all(tiles, axes[k], split_axis=k, concat_axis=k, tiled=True)  22.5 us
    another operation x3, other arithmetic  21.2 us
    gather x1, other arithmetic, per_device(): jnp.take(defocus_bin, particle)  20.1 us
    all_to_all x1, starting transfers between devices, per_device(): lax.all_to_all(send_labels, TILE, split_axis=0, concat_axis=0, tiled=True)  18.7 us
    convert_element_type x1, local copies, waits for them, and re-layouts, shifted_tables(): stacked = jnp.stack([moved_real, moved_imag], axis=2).astype(jnp.bfloat16)  16.6 us
  transfers between devices with their start and end apart: 3, of which 2 were waited for; matrix products, arithmetic and copies ran while one was open for 25% of the time, Pallas kernels for 0%

commit v1 on v0

v1 whole, which is shorter than its diff:
```python
import functools
import math

import jax
import jax.numpy as jnp
from jax import lax
from jax.experimental import pallas as pl
from jax.experimental.pallas import tpu as pltpu
from jax.sharding import Mesh
from jax.sharding import PartitionSpec as P

BOX = 256
NBIN = 16
TSIDE = 3
NT = TSIDE * TSIDE
TILE = ("tile_0", "tile_1", "tile_2")

wave_length = 0.0197
aberration = 27000000.0
amplitude = 0.1
b_factor = 20.0
defocus_base = 5000.0
defocus_step = 500.0

META = 128
CHUNK = 512
PAIRS = ((5, 3, 0, 1), (7, 1, 1, 0), (8, 0, 1, 1), (6, 2, 1, -1))


def ring_offsets(n):
    offs = [0]
    for s in range(1, n // 2):
        offs += [s, -s]
    return offs + [n // 2]


def frequencies(first_index, span_count):
    flat_index = first_index + jnp.arange(span_count, dtype=jnp.int32)
    freq_x = flat_index // BOX
    freq_y = flat_index % BOX - BOX // 2
    return (freq_x, freq_y)


def ctf_table(freq_x, freq_y, bins_count):
    scaled_x = freq_x.astype(jnp.float32) / BOX
    scaled_y = freq_y.astype(jnp.float32) / BOX
    radius_sq = scaled_x * scaled_x + scaled_y * scaled_y
    defocus = defocus_base + defocus_step * jnp.arange(bins_count, dtype=jnp.float32)[:, None]
    aberr_phase = (
        math.pi * wave_length * defocus * radius_sq[None, :]
        - 0.5 * math.pi * aberration * wave_length**3 * radius_sq[None, :] ** 2
    )
    envelope = jnp.exp(-0.25 * b_factor * radius_sq)[None, :]
    return (
        -(math.sqrt(1.0 - amplitude**2) * jnp.sin(aberr_phase) + amplitude * jnp.cos(aberr_phase))
        * envelope
    )


def turn(m):
    angles = jnp.mod(m, BOX).astype(jnp.float32) * (2.0 * math.pi / BOX)
    return (jnp.cos(angles), jnp.sin(angles))


def split3(v):
    hi = v.astype(jnp.bfloat16)
    rest = v - hi.astype(jnp.float32)
    mid = rest.astype(jnp.bfloat16)
    lo = (rest - mid.astype(jnp.float32)).astype(jnp.bfloat16)
    return hi, mid, lo


NT_DIMS = (((1,), (1,)), ((), ()))


def prep_kernel(c_ref, xr, xi, qr, qi, w, ctf, binc, cx, sx, cy, sy, meta, out, energy, wc2_s, mag_s):
    n, width = xr.shape
    half = width // 2
    c = c_ref[0]
    bins = binc[...]
    acc = jnp.zeros((n, BOX), jnp.float32)
    cyv = cy[...]
    syv = sy[...]
    for g in range(width // BOX):
        sl = pl.ds(g * BOX, BOX)
        wv = w[:, sl]
        table = ctf[:, sl]
        wc2_s[:, sl] = wv * table * table
        rows = jnp.zeros((n, BOX), jnp.float32)
        for b in range(NBIN):
            rows = jnp.where(bins == b, table[b : b + 1, :], rows)
        re = xr[:, sl].astype(jnp.float32)
        im = xi[:, sl].astype(jnp.float32)
        cxv = cx[:, g : g + 1]
        sxv = sx[:, g : g + 1]
        co = cxv * cyv - sxv * syv
        si = sxv * cyv + cxv * syv
        factor = wv * rows
        h = (g * BOX) // half
        at = g * BOX - h * half
        place = (at // CHUNK) * 2 * CHUNK + at % CHUNK
        d = (h + c) % 2
        out[d, 0:n, pl.ds(place, BOX)] = (factor * (re * co + im * si)).astype(jnp.bfloat16)
        out[d, 0:n, pl.ds(place + CHUNK, BOX)] = (factor * (im * co - re * si)).astype(jnp.bfloat16)
        acc = acc + wv * (re * re + im * im)
        pr = qr[:, sl]
        pi = qi[:, sl]
        out[d, n : 2 * n, pl.ds(place, BOX)] = pr
        out[d, n : 2 * n, pl.ds(place + CHUNK, BOX)] = pi
        prf = pr.astype(jnp.float32)
        pif = pi.astype(jnp.float32)
        mag_s[:, sl] = prf * prf + pif * pif
    energy[...] = jnp.broadcast_to(jnp.sum(acc, axis=1, keepdims=True), (n, META))
    power = lax.dot_general(
        mag_s[...], wc2_s[...], NT_DIMS, precision=lax.Precision.HIGHEST, preferred_element_type=jnp.float32
    )
    lane = lax.broadcasted_iota(jnp.int32, (NBIN, META), 1)
    row = lax.broadcasted_iota(jnp.int32, (NBIN, META), 0)
    placed = jnp.zeros((n, META), jnp.float32)
    for k, part in enumerate(split3(power)):
        spot = jnp.where(lane == row + k * NBIN, 1.0, 0.0).astype(jnp.bfloat16)
        placed = placed + jnp.dot(part, spot, preferred_element_type=jnp.float32)
    for d in range(2):
        out[d, 0:n, pl.ds(width, META)] = meta[...]
        out[d, n : 2 * n, pl.ds(width, META)] = placed.astype(jnp.bfloat16)


def prepare(c, xr, xi, qr, qi, w, ctf, binc, cx, sx, cy, sy, meta):
    n, width = xr.shape
    vm = pl.BlockSpec(memory_space=pltpu.VMEM)
    return pl.pallas_call(
        prep_kernel,
        out_shape=(
            jax.ShapeDtypeStruct((2, 2 * n, width + META), jnp.bfloat16),
            jax.ShapeDtypeStruct((n, META), jnp.float32),
        ),
        in_specs=[pl.BlockSpec(memory_space=pltpu.SMEM)] + [vm] * 12,
        out_specs=(vm, vm),
        scratch_shapes=[pltpu.VMEM((NBIN, width), jnp.float32), pltpu.VMEM((n, width), jnp.float32)],
        name="prep",
    )(c, xr, xi, qr, qi, w, ctf, binc, cx, sx, cy, sy, meta)


def score_kernel(n_y, n_z, ids, *refs):
    yb = refs[: n_y + 1]
    zb = refs[n_y + 1 : n_y + n_z + 2]
    tables, meta_y, meta_z, out, part_s, proj_s, rot_s, acc, w_s = refs[n_y + n_z + 2 :]
    step = pl.program_id(0)
    steps = pl.num_programs(0)
    rows = yb[0].shape[0]
    half_rows = rows // 2
    np_ = n_y * rows
    offs_y = ring_offsets(n_y)
    offs_z = ring_offsets(n_z)

    for k in range(n_y - 1):
        part_s[k * rows : (k + 1) * rows, :] = yb[k][...]
    part_s[(n_y - 1) * rows : (n_y - 1) * rows + half_rows, :] = yb[n_y - 1][...]
    part_s[(n_y - 1) * rows + half_rows : n_y * rows, :] = yb[n_y][...]
    for k in range(n_z - 1):
        proj_s[k] = zb[k][...]
    proj_s[n_z - 1, 0:half_rows, :] = zb[n_z - 1][...]
    proj_s[n_z - 1, half_rows:rows, :] = zb[n_z][...]

    def rotate(b, slot):
        for s in range(rows // 16):
            sl = slice(s * 16, s * 16 + 16)
            for q in range(CHUNK // 256):
                la = slice(q * 256, q * 256 + 256)
                lb = slice(CHUNK + q * 256, CHUNK + q * 256 + 256)
                reb = proj_s[b, sl, la]
                imb = proj_s[b, sl, lb]
                re = reb.astype(jnp.float32)
                im = imb.astype(jnp.float32)
                base = 4 * rows + s * 16
                rot_s[slot, base : base + 16, la] = reb
                rot_s[slot, base : base + 16, lb] = imb
                for k, (t1, t2, _, _) in enumerate(PAIRS):
                    co = tables[k : k + 1, la]
                    si = tables[4 + k : 5 + k, la]
                    rc = re * co
                    is_ = im * si
                    ic = im * co
                    rs = re * si
                    b1 = t1 * rows + s * 16
                    b2 = t2 * rows + s * 16
                    rot_s[slot, b1 : b1 + 16, la] = (rc - is_).astype(jnp.bfloat16)
                    rot_s[slot, b1 : b1 + 16, lb] = (ic + rs).astype(jnp.bfloat16)
                    rot_s[slot, b2 : b2 + 16, la] = (rc + is_).astype(jnp.bfloat16)
                    rot_s[slot, b2 : b2 + 16, lb] = (ic - rs).astype(jnp.bfloat16)

    @pl.when(step == 0)
    def _():
        acc[...] = jnp.zeros_like(acc)

    rotate(0, 0)

    def body(b, carry):
        acc[b] += lax.dot_general(
            rot_s[b % 2], part_s[...], NT_DIMS, preferred_element_type=jnp.float32
        )
        rotate(jnp.minimum(b + 1, n_z - 1), (b + 1) % 2)
        return carry

    lax.fori_loop(0, n_z, body, 0)

    @pl.when(step == steps - 1)
    def _():
        my_y = ids[0]
        my_z = ids[1]
        my_c = ids[2]
        info = jnp.transpose(meta_y[...].astype(jnp.float32)).astype(jnp.int32)
        bins = info[8:9, :]
        r = lax.broadcasted_iota(jnp.int32, (META, np_), 0)
        spot = jnp.where((r % NBIN == bins) & (r < 3 * NBIN), -0.25, 0.0).astype(jnp.bfloat16)
        power = jnp.dot(meta_z[...], spot, preferred_element_type=jnp.float32)
        for lt in range(np_ // 128):
            la = slice(lt * 128, lt * 128 + 128)
            for t in range(NT):
                sums = [jnp.zeros((half_rows, 128), jnp.float32) for _ in range(4)]
                for k in range(n_z):
                    z_abs = (my_z - offs_z[k] + n_z) % n_z
                    for u in range(2):
                        tile = (my_y * n_z + z_abs) * 2 + (my_c + u) % 2
                        lo = t * rows + u * half_rows
                        val = acc[k, lo : lo + half_rows, la]
                        lo = k * rows + u * half_rows
                        val = val + power[lo : lo + half_rows, la]
                        for j in range(4):
                            sums[j] = jnp.where(info[j : j + 1, la] // 2 == tile, val, sums[j])
                for j in range(4):
                    x = sums[j]
                    start = info[4 + j : 5 + j, la]
                    for bit in (16, 8, 4, 2, 1):
                        x = jnp.where((start & bit) != 0, pltpu.roll(x, half_rows - bit, 0), x)
                    w_s[j, t * 16 : t * 16 + 16, la] = x[0:16]
        lane = lax.broadcasted_iota(jnp.int32, (1, np_), 1)
        k_of = lane // rows
        c_of = ((lane // half_rows) + my_c) % 2
        y_of = jnp.zeros((1, np_), jnp.int32)
        for k in range(n_y):
            y_of = jnp.where(k_of == k, (my_y - offs_y[k] + n_y) % n_y, y_of)
        per_row = 4 * n_z
        n_slots = out.shape[0]
        slot_row = lax.broadcasted_iota(jnp.int32, (n_slots, np_), 0)
        total = jnp.zeros(out.shape, jnp.float32)
        for j in range(4):
            local = info[j : j + 1, :] - my_y * per_row
            fits = (local >= 0) & (local < per_row)
            slot = jnp.where(fits, (y_of * 2 + c_of) * per_row + local, -1)
            pick = jnp.where(slot_row == slot, 1.0, 0.0).astype(jnp.bfloat16)
            for piece in split3(w_s[j]):
                total = total + lax.dot_general(pick, piece, NT_DIMS, preferred_element_type=jnp.float32)
        out[...] = total


def score(ids, y_blocks, z_blocks, tables, meta_y, meta_z):
    n_y = len(y_blocks) - 1
    n_z = len(z_blocks) - 1
    rows = y_blocks[0].shape[0]
    width = y_blocks[0].shape[1] - META
    steps = width // (2 * CHUNK)
    span = 2 * CHUNK
    blocks = [
        pl.BlockSpec((a.shape[0], span), lambda i, s: (0, i)) for a in list(y_blocks) + list(z_blocks)
    ]
    full = lambda a: pl.BlockSpec(a.shape, lambda i, s: (0, 0))
    n_slots = 2 * n_y * 4 * n_z
    flops = 2 * NT * rows * n_z * rows * n_y * width
    return pl.pallas_call(
        functools.partial(score_kernel, n_y, n_z),
        out_shape=jax.ShapeDtypeStruct((n_slots, NT * 16), jnp.float32),
        grid_spec=pltpu.PrefetchScalarGridSpec(
            num_scalar_prefetch=1,
            grid=(steps,),
            in_specs=blocks
            + [pl.BlockSpec((8, CHUNK), lambda i, s: (0, i)), full(meta_y), full(meta_z)],
            out_specs=pl.BlockSpec((n_slots, NT * 16), lambda i, s: (0, 0)),
            scratch_shapes=[
                pltpu.VMEM((n_y * rows, span), jnp.bfloat16),
                pltpu.VMEM((n_z, rows, span), jnp.bfloat16),
                pltpu.VMEM((2, NT * rows, span), jnp.bfloat16),
                pltpu.VMEM((n_z, NT * rows, n_y * rows), jnp.float32),
                pltpu.VMEM((4, NT * 16, n_y * rows), jnp.float32),
            ],
        ),
        compiler_params=pltpu.CompilerParams(
            dimension_semantics=("arbitrary",), vmem_limit_bytes=60 * 1024 * 1024
        ),
        cost_estimate=pl.CostEstimate(flops=flops, transcendentals=0, bytes_accessed=17 * 1024 * 1024),
        name="score",
    )(ids, *y_blocks, *z_blocks, tables, meta_y, meta_z)


def both_rings(a, axis_a, b, axis_b):
    found = {0: [a], 1: [b]}
    axes = (axis_a, axis_b)
    sizes = [lax.axis_size(x) for x in axes]
    ahead = [a, b]
    back = [a, b]

    def shift(v, k, d):
        n = sizes[k]
        return lax.ppermute(v, axes[k], [(i, (i + d) % n) for i in range(n)])

    for s in range(1, max(sizes) // 2 + 1):
        for k in range(2):
            n = sizes[k]
            if s < n // 2:
                ahead[k] = shift(ahead[k], k, 1)
                back[k] = shift(back[k], k, -1)
                found[k] += [ahead[k], back[k]]
            elif s == n // 2:
                h = a.shape[0] // 2
                found[k] += [shift(ahead[k][:h], k, 1), shift(back[k][h:], k, -1)]
    return found[0], found[1]


def slot_rank(tile_ids):
    positions = jnp.arange(tile_ids.shape[0], dtype=jnp.int32)
    earlier_same = (tile_ids[:, None] == tile_ids[None, :]) & (
        positions[None, :] < positions[:, None]
    )
    return jnp.sum(earlier_same.astype(jnp.int32), axis=1)


def finish(scored):
    row_peak = jnp.max(scored, axis=(1, 2))
    log_total = row_peak + jnp.log(jnp.sum(jnp.exp(scored - row_peak[:, None, None]), axis=(1, 2)))
    posterior = jnp.exp(scored - log_total[:, None, None])
    return (posterior, log_total)


def per_device(particles, projections, noise_weight, tile_list, ori_start, shifts, defocus_bin):
    band = lax.axis_index("shell")
    my_y = lax.axis_index(TILE[0])
    my_z = lax.axis_index(TILE[1])
    my_c = lax.axis_index(TILE[2])
    count, _, width = particles.shape
    windows = tile_list.shape[1]
    half = width // 2
    freq_x, freq_y = frequencies(band * width, width)
    ctf = ctf_table(freq_x, freq_y, NBIN)
    first_x = (band * width) // BOX
    span_x = first_x + jnp.arange(width // BOX, dtype=jnp.int32)
    span_y = jnp.arange(BOX, dtype=jnp.int32) - BOX // 2
    cx, sx = turn(span_x[None, :] * shifts[:, 0:1])
    cy, sy = turn(span_y[None, :] * shifts[:, 1:2])
    key = tile_list * 2 + slot_rank(tile_list.reshape(-1)).reshape(count, windows)
    meta = jnp.concatenate([key, ori_start, defocus_bin[:, None]], axis=1)
    meta = jnp.pad(meta, ((0, 0), (0, META - meta.shape[1]))).astype(jnp.bfloat16)
    sides, energy = prepare(
        my_c.reshape(1).astype(jnp.int32),
        particles[:, 0],
        particles[:, 1],
        projections[:, 0],
        projections[:, 1],
        noise_weight[None, :],
        ctf,
        defocus_bin[:, None],
        cx,
        sx,
        cy,
        sy,
        meta,
    )
    kept = sides[0]
    got = lax.ppermute(sides[1], TILE[2], [(0, 1), (1, 0)])
    y_own = jnp.concatenate([kept[:count], got[:count]], axis=0)
    z_own = jnp.concatenate([kept[count:], got[count:]], axis=0)
    y_blocks, z_blocks = both_rings(y_own, TILE[0], z_own, TILE[1])
    mult = jnp.array([[a, b] for _, _, a, b in PAIRS], jnp.int32)
    fx = lax.dynamic_slice_in_dim(freq_x, my_c * half, half)
    fy = lax.dynamic_slice_in_dim(freq_y, my_c * half, half)
    co, si = turn(mult[:, 0:1] * fx[None, :] + mult[:, 1:2] * fy[None, :])
    tables = jnp.concatenate([co, si], axis=0)
    meta_y = jnp.concatenate([b[:, half * 2 :] for b in y_blocks], axis=0)
    meta_z = jnp.concatenate([b[:, half * 2 :] for b in z_blocks], axis=0)
    ids = jnp.stack([my_y, my_z, my_c]).astype(jnp.int32)
    slots = score(ids, y_blocks, z_blocks, tables, meta_y, meta_z)
    n_y = lax.axis_size(TILE[0])
    slots = slots.reshape(2 * n_y, -1, NT * 16)
    slots = lax.all_to_all(slots, (TILE[0], TILE[2]), split_axis=0, concat_axis=0, tiled=True)
    slots = jnp.sum(slots.reshape(n_y, 2, -1, NT * 16), axis=1).reshape(-1, NT * 16)
    items = jnp.take(slots, key.reshape(-1), axis=0)
    items = items.reshape(count, windows * NT * 16) - 0.5 * energy[:, 0:1]
    n_x = lax.axis_size("shell")
    copies = jnp.broadcast_to(items, (n_x, *items.shape))
    items = jnp.sum(lax.all_to_all(copies, "shell", split_axis=0, concat_axis=0, tiled=True), axis=0)
    scores = items.reshape(count, windows, NT, 16).transpose(0, 2, 1, 3).reshape(count, NT, windows * 16)
    return finish(scores)


def solution(mesh):
    split = Mesh(
        mesh.devices.reshape(8, 8, 2, mesh.shape["shell"]), ("tile_0", "tile_1", "tile_2", "shell")
    )
    in_specs = (
        P(TILE, None, "shell"),
        P(TILE, None, "shell"),
        P("shell"),
        P(TILE, None),
        P(TILE, None),
        P(TILE, None),
        P(TILE),
    )
    out_specs = (P(TILE, None, None), P(TILE))
    return jax.shard_map(
        per_device, mesh=split, in_specs=in_specs, out_specs=out_specs, check_vma=False
    )
```

time: 460 us -> 268 us (0.58); the launches traced: 453 us -> 267 us
  waiting for transfers between devices: 183 us -> 61.5 us
  Pallas kernels: 0 us -> 82.9 us
  other arithmetic: 88.6 us -> 9.93 us
  local copies, waits for them, and re-layouts: 89.1 us -> 26.9 us
  matrix products: 22.2 us -> 0 us
  starting transfers between devices: 56 us -> 73.5 us
    all_to_all x3 -> x1, waiting for transfers between devices: 183 us -> 16.7 us  [per_device(): lax.all_to_all(slots, (TILE[0], TILE[2]), split_axis=0, concat_axis=0, ti...]
    pallas_call x0 -> x2, Pallas kernels: none -> 82.9 us  [the longest x1 77.2 us: score(): pl.pallas_call(functools.partial(score_kernel, n_y, n_z), out_shape=jax.S...]
    ppermute x0 -> x17, starting transfers between devices: none -> 62.1 us  [the longest x16 53.3 us: shift(): return lax.ppermute(v, axes[k], [(i, (i + d) % n) for i in range(n)])]
    ppermute x0 -> x17, waiting for transfers between devices: none -> 44.8 us  [the longest x16 42.6 us: shift(): return lax.ppermute(v, axes[k], [(i, (i + d) % n) for i in range(n)])]
    all_to_all x3 -> x1, starting transfers between devices: 56 us -> 11.4 us  [per_device(): lax.all_to_all(slots, (TILE[0], TILE[2]), split_axis=0, concat_axis=0, ti...]
    another operation x5 -> x4, other arithmetic: 45.2 us -> 0.67 us  [the longest x1 0.65 us: per_device(): ids = jnp.stack([my_y, my_z, my_c]).astype(jnp.int32)]
    gather x10 -> x2, local copies, waits for them, and re-layouts: 44.7 us -> 0.87 us  [per_device(): items = jnp.take(slots, key.reshape(-1), axis=0)]
    dot_general x4 -> x0, matrix products: 22.2 us -> none  [the longest x1 10.7 us: slot_scores(): lax.dot_general(slot_rows, lookup, (((1,), (1,)), ((), ())), preferred_el...]
  transfers between devices with their start and end apart: 3 -> 18, of which waited for: 2 -> 11; matrix products, arithmetic and copies ran while one was open for 25% -> 4% of each run, Pallas kernels for 0% -> 0%
where the time goes in v1:
time: 268 us; the launch traced here: 267 us
  Pallas kernels  82.9 us (31%)
  starting transfers between devices  73.5 us (27%)
  waiting for transfers between devices  61.5 us (23%)
  local copies, waits for them, and re-layouts  26.9 us (10%)
  blocking collectives  11 us (4%)
  other arithmetic  9.93 us (4%)
    pallas_call x1, Pallas kernels, score(): pl.pallas_call(functools.partial(score_kernel, n_y, n_z), out_shape=jax.S...  77.2 us
    ppermute x16, starting transfers between devices, shift(): return lax.ppermute(v, axes[k], [(i, (i + d) % n) for i in range(n)])  53.3 us
    ppermute x16, waiting for transfers between devices, shift(): return lax.ppermute(v, axes[k], [(i, (i + d) % n) for i in range(n)])  42.6 us
    all_to_all x1, waiting for transfers between devices, per_device(): lax.all_to_all(slots, (TILE[0], TILE[2]), split_axis=0, concat_axis=0, ti...  16.7 us
    all_to_all x1, starting transfers between devices, per_device(): lax.all_to_all(slots, (TILE[0], TILE[2]), split_axis=0, concat_axis=0, ti...  11.4 us
    all_to_all x1, blocking collectives, per_device(): lax.all_to_all(copies, 'shell', split_axis=0, concat_axis=0, tiled=True)  11 us
    unnamed x54, local copies, waits for them, and re-layouts  8.97 us
    ppermute x1, starting transfers between devices, per_device(): got = lax.ppermute(sides[1], TILE[2], [(0, 1), (1, 0)])  8.75 us
  transfers between devices with their start and end apart: 18, of which 11 were waited for; matrix products, arithmetic and copies ran while one was open for 4% of the time, Pallas kernels for 0%

profile of v1, /device:TPU:1, one launch (start us, length us, event | category | flops | bytes accessed | tf_op | source)
XLA Modules:
  0.0 266.8 jit_solution(10977462012104936824)
XLA Ops:
  0.8 0.8 copy.45
  2.2 0.8 slice_bitcast_fusion.3
  3.0 5.1 %fusion.33 = (bf16[32,1,8192]{2,1,0:T(2,128)(2,1)S(1)}, bf16[32,1,8192]{2,1,0:T(2,128)(2,1)}) fusion(bf16[32,2,8192]{2,1,0:T(2,128)(2,1)} %param.9), kind=kLoop, calls=%fused_computation.111 | loop fusion | bytes 2097152 | tf_op jit(solution)/shard_map/slice | solution.py:357
  8.1 2.3 fusion.34
  11.7 0.8 fusion.28
  12.5 3.3 %copy_bitcast_fusion = (bf16[32,8192]{1,0:T(8,128)(2,1)}, bf16[32,8192]{1,0:T(8,128)(2,1)}) fusion(bf16[32,1,8192]{2,1,0:T(2,128)(2,1)S(1)} %get-tuple-element.18, bf16[32,1,8192]{2,1,0:T(2,128)(2,1)} %get-tuple-element.19), kind=kLoop, calls=%fused_computation.10 | loop fusion | bytes 2097152 | tf_op jit(solution)/shard_map/squeeze | solution.py:357
  15.8 2.1 copy_bitcast_fusion.2
  17.9 0.8 fusion.24
  19.5 3.0 %negate_multiply_fusion.ctf = f32[16,8192]{1,0:T(8,128)} fusion(f32[8192]{0:T(1024)S(1)} %get-tuple-element.36, f32[8192]{0:T(1024)S(1)} %get-tuple-element.37, f32[8192]{0:T(1024)S(1)} %multiply_add_fusion, f32[16]{0:T(128)S(1)} %add_multiply_fusion), kind=kLoop, calls=%fused_computation.15 | loop fusion | flops 917504 | bytes 622656 | tf_op jit(solution)/shard_map/mul | solution.py:55
  22.5 5.7 %prep.1 = (bf16[2,64,8320]{2,1,0:T(8,128)(2,1)}, f32[32,128]{1,0:T(8,128)}) custom-call(s32[1]{0:T(128)} %bitcast.2.c_ref, bf16[32,8192]{1,0:T(8,128)(2,1)} %get-tuple-element.31.xr, bf16[32,8192]{1,0:T(8,128)(2,1)} %get-tuple-element.30.xi, bf16[32,8192]{1,0:T(8,128)(2,1)} %get-tuple-element.33.qr, bf16[32,8192]{1,0:T(8,128)(2,1)} %get-tuple-element.32.qi, ...), custom_call_target="tpu_custom_call" | custom-call | tf_op jit(solution)/shard_map/prep/pallas_call | solution.py:131
  28.2 1.5 slice_bitcast_fusion
  29.7 8.7 %collective-permute-start = (bf16[64,8320]{1,0:T(8,128)(2,1)S(1)}, bf16[64,8320]{1,0:T(8,128)(2,1)S(1)}, u32[]{:S(2)}, u32[]{:S(2)}) collective-permute-start(bf16[64,8320]{1,0:T(8,128)(2,1)S(1)} %slice_bitcast_fusion), channel_id=1, source_target_pairs={{0,4},{4,0},{1,5},{5,1},{2,6},{6,2},{3,7},{7,3},{8,12},{12,8},{9,1... | collective-permute-start | bytes 3194888 | tf_op jit(solution)/shard_map/ppermute | solution.py:368
  38.5 2.2 collective-permute-done
  40.9 1.9 collective-permute-start.9
  42.8 5.3 %collective-permute-start.10 = (bf16[64,8320]{1,0:T(8,128)(2,1)S(1)}, bf16[64,8320]{1,0:T(8,128)(2,1)}, u32[]{:S(2)}, u32[]{:S(2)}) collective-permute-start(bf16[64,8320]{1,0:T(8,128)(2,1)S(1)} %pad_maximum_fusion.1.refs_9_), channel_id=1, source_target_pairs={{0,56},{8,0},{16,8},{24,16},{32,24},{40,32},{48,40},{56,48},{1,57}... | collective-permute-start | bytes 3194888 | tf_op jit(solution)/shard_map/ppermute | solution.py:304
  48.1 1.1 pad_maximum_fusion.refs_0_
  49.2 3.2 %collective-permute-start.1 = (bf16[64,8320]{1,0:T(8,128)(2,1)}, bf16[64,8320]{1,0:T(8,128)(2,1)}, u32[]{:S(2)}, u32[]{:S(2)}) collective-permute-start(bf16[64,8320]{1,0:T(8,128)(2,1)} %pad_maximum_fusion.refs_0_), channel_id=1, source_target_pairs={{0,64},{64,128},{128,192},{192,256},{256,320},{320,384},{384,448},... | collective-permute-start | bytes 3194888 | tf_op jit(solution)/shard_map/ppermute | solution.py:304
  52.4 3.8 %collective-permute-start.2 = (bf16[64,8320]{1,0:T(8,128)(2,1)}, bf16[64,8320]{1,0:T(8,128)(2,1)}, u32[]{:S(2)}, u32[]{:S(2)}) collective-permute-start(bf16[64,8320]{1,0:T(8,128)(2,1)} %pad_maximum_fusion.refs_0_), channel_id=1, source_target_pairs={{0,448},{64,0},{128,64},{192,128},{256,192},{320,256},{384,320},{4... | collective-permute-start | bytes 3194888 | tf_op jit(solution)/shard_map/ppermute | solution.py:304
  56.9 12.9 %collective-permute-done.9.refs_10_ = bf16[64,8320]{1,0:T(8,128)(2,1)} collective-permute-done((bf16[64,8320]{1,0:T(8,128)(2,1)S(1)}, bf16[64,8320]{1,0:T(8,128)(2,1)}, u32[]{:S(2)}, u32[]{:S(2)}) %collective-permute-start.9) | collective-permute-done | bytes 1064992 | tf_op jit(solution)/shard_map/ppermute | solution.py:304
  69.8 1.9 collective-permute-start.11
  71.7 4.6 %collective-permute-start.12 = (bf16[64,8320]{1,0:T(8,128)(2,1)}, bf16[64,8320]{1,0:T(8,128)(2,1)}, u32[]{:S(2)}, u32[]{:S(2)}) collective-permute-start(bf16[64,8320]{1,0:T(8,128)(2,1)} %collective-permute-done.10.refs_11_), channel_id=1, source_target_pairs={{0,56},{8,0},{16,8},{24,16},{32,24},{40,32},{48,40},{56,48},{1,57}... | collective-permute-start | bytes 3194888 | tf_op jit(solution)/shard_map/ppermute | solution.py:304
  76.3 1.5 collective-permute-done.1.refs_1_
  77.8 1.9 collective-permute-start.3
  79.8 4.6 %collective-permute-start.4 = (bf16[64,8320]{1,0:T(8,128)(2,1)}, bf16[64,8320]{1,0:T(8,128)(2,1)}, u32[]{:S(2)}, u32[]{:S(2)}) collective-permute-start(bf16[64,8320]{1,0:T(8,128)(2,1)} %collective-permute-done.2.refs_2_), channel_id=1, source_target_pairs={{0,448},{64,0},{128,64},{192,128},{256,192},{320,256},{384,320},{4... | collective-permute-start | bytes 3194888 | tf_op jit(solution)/shard_map/ppermute | solution.py:304
  87.1 0.7 constant_dynamic-update-slice_fusion.7
  87.9 9.5 %collective-permute-done.11.refs_12_ = bf16[64,8320]{1,0:T(8,128)(2,1)} collective-permute-done((bf16[64,8320]{1,0:T(8,128)(2,1)}, bf16[64,8320]{1,0:T(8,128)(2,1)}, u32[]{:S(2)}, u32[]{:S(2)}) %collective-permute-start.11) | collective-permute-done | bytes 1064992 | tf_op jit(solution)/shard_map/ppermute | solution.py:304
  97.3 1.9 collective-permute-start.13
  99.3 4.6 %collective-permute-start.14 = (bf16[64,8320]{1,0:T(8,128)(2,1)}, bf16[64,8320]{1,0:T(8,128)(2,1)S(1)}, u32[]{:S(2)}, u32[]{:S(2)}) collective-permute-start(bf16[64,8320]{1,0:T(8,128)(2,1)} %collective-permute-done.12.refs_13_), channel_id=1, source_target_pairs={{0,56},{8,0},{16,8},{24,16},{32,24},{40,32},{48,40},{56,48},{1,57}... | collective-permute-start | bytes 3194888 | tf_op jit(solution)/shard_map/ppermute | solution.py:304
  103.8 1.3 collective-permute-done.3.refs_3_
  105.1 2.0 collective-permute-start.5
  107.1 4.5 %collective-permute-start.6 = (bf16[64,8320]{1,0:T(8,128)(2,1)}, bf16[64,8320]{1,0:T(8,128)(2,1)S(1)}, u32[]{:S(2)}, u32[]{:S(2)}) collective-permute-start(bf16[64,8320]{1,0:T(8,128)(2,1)} %collective-permute-done.4.refs_4_), channel_id=1, source_target_pairs={{0,448},{64,0},{128,64},{192,128},{256,192},{320,256},{384,320},{4... | collective-permute-start | bytes 3194888 | tf_op jit(solution)/shard_map/ppermute | solution.py:304
  111.6 0.7 constant_dynamic-update-slice_fusion.6
  112.3 0.7 constant_dynamic-update-slice_fusion.14
  115.2 8.7 %collective-permute-done.13.refs_14_ = bf16[64,8320]{1,0:T(8,128)(2,1)S(1)} collective-permute-done((bf16[64,8320]{1,0:T(8,128)(2,1)}, bf16[64,8320]{1,0:T(8,128)(2,1)S(1)}, u32[]{:S(2)}, u32[]{:S(2)}) %collective-permute-start.13) | collective-permute-done | bytes 1064992 | tf_op jit(solution)/shard_map/ppermute | solution.py:304
  123.9 1.9 collective-permute-start.15
  125.9 4.6 %collective-permute-start.16 = (bf16[32,8320]{1,0:T(8,128)(2,1)S(1)}, bf16[32,8320]{1,0:T(8,128)(2,1)S(1)}, u32[]{:S(2)}, u32[]{:S(2)}) collective-permute-start(bf16[32,8320]{1,0:T(8,128)(2,1)S(1)} %slice.162), channel_id=1, source_target_pairs={{0,56},{8,0},{16,8},{24,16},{32,24},{40,32},{48,40},{56,48},{1,57}... | collective-permute-start | bytes 1597448 | tf_op jit(solution)/shard_map/ppermute | solution.py:304
  130.5 0.9 collective-permute-done.5.refs_5_
  131.4 2.4 collective-permute-start.7
  133.9 4.3 %collective-permute-start.8 = (bf16[32,8320]{1,0:T(8,128)(2,1)S(1)}, bf16[32,8320]{1,0:T(8,128)(2,1)S(1)}, u32[]{:S(2)}, u32[]{:S(2)}) collective-permute-start(bf16[32,8320]{1,0:T(8,128)(2,1)S(1)} %slice.159), channel_id=1, source_target_pairs={{0,448},{64,0},{128,64},{192,128},{256,192},{320,256},{384,320},{4... | collective-permute-start | bytes 1597448 | tf_op jit(solution)/shard_map/ppermute | solution.py:304
  139.0 6.2 %collective-permute-done.7.refs_7_ = bf16[32,8320]{1,0:T(8,128)(2,1)S(1)} collective-permute-done((bf16[32,8320]{1,0:T(8,128)(2,1)S(1)}, bf16[32,8320]{1,0:T(8,128)(2,1)S(1)}, u32[]{:S(2)}, u32[]{:S(2)}) %collective-permute-start.7) | collective-permute-done | bytes 532512 | tf_op jit(solution)/shard_map/ppermute | solution.py:304
  145.3 1.0 collective-permute-done.8.refs_8_
  146.2 0.8 copy-done.18
  147.7 77.2 %score.1 = f32[512,144]{1,0:T(8,128)} custom-call(s32[3]{0:T(128)} %pad_add_fusion.ids, bf16[64,8320]{1,0:T(8,128)(2,1)} %pad_maximum_fusion.refs_0_, bf16[64,8320]{1,0:T(8,128)(2,1)} %collective-permute-done.1.refs_1_, bf16[64,8320]{1,0:T(8,128)(2,1)} %collective-permute-done.2.refs_2_, bf16[64,8320]{1,0:T(8,128)(2,1)} %collective-permute-done.3.refs_3_, ...), custom_call_target="tpu_custom_call" | custom-call | flops 38654705664 | bytes 17825792 | tf_op jit(solution)/shard_map/score/pallas_call | solution.py:270
  224.9 11.4 %all-to-all-start = ((f32[16,32,144]{2,1,0:T(8,128)}), f32[16,32,144]{2,1,0:T(8,128)S(1)}, u32[]{:S(2)}, u32[]{:S(2)}) async-start(f32[16,32,144]{2,1,0:T(8,128)} %bitcast.40), calls=%async_computation | async-start | bytes 1048576 | tf_op jit(solution)/shard_map/all_to_all | solution.py:383
  236.8 16.7 %all-to-all-done = f32[16,32,144]{2,1,0:T(8,128)S(1)} async-done(((f32[16,32,144]{2,1,0:T(8,128)}), f32[16,32,144]{2,1,0:T(8,128)S(1)}, u32[]{:S(2)}, u32[]{:S(2)}) %all-to-all-start) | async-done | bytes 294944 | tf_op jit(solution)/shard_map/all_to_all | solution.py:383
  253.5 0.8 gather_fusion
  254.5 11.0 %all_to_all.10 = f32[4,32,576]{2,1,0:T(8,128)S(1)} all-to-all(f32[4,32,576]{2,1,0:T(8,128)S(1)} %broadcast_in_dim.39), channel_id=1, replica_groups=mesh['tile_0'=8,'tile_1'=8,'tile_2'=2,'shell'=4] {'shell'}, dimensions={0} | all-to-all | bytes 589824 | tf_op jit(solution)/shard_map/all_to_all | solution.py:389
  266.0 0.8 copy.56
  (108 shorter events, 11.6 us)
Async XLA Ops:
  3.0 5.1 %copy-start = (bf16[32,2,8192]{2,1,0:T(2,128)(2,1)S(1)}, bf16[32,2,8192]{2,1,0:T(2,128)(2,1)}, u32[]{:S(2)}) copy-start(bf16[32,2,8192]{2,1,0:T(2,128)(2,1)} %param.8) | copy-start | bytes 3145732
  8.1 2.8 %copy-start.10 = (s32[32,4]{0,1:T(4,128)S(1)}, s32[32,4]{0,1:T(4,128)}, u32[]{:S(2)}) copy-start(s32[32,4]{0,1:T(4,128)} %param.12) | copy-start | bytes 1540
  8.1 2.9 %copy-start.13 = (s32[32]{0:T(128)S(1)}, s32[32]{0:T(128)}, u32[]{:S(2)}) copy-start(s32[32]{0:T(128)} %param.14) | copy-start | bytes 388
  28.2 10.2 %copy-start.1 = (bf16[2,64,8320]{2,1,0:T(8,128)(2,1)S(1)}, bf16[2,64,8320]{2,1,0:T(8,128)(2,1)}, u32[]{:S(2)}) copy-start(bf16[2,64,8320]{2,1,0:T(8,128)(2,1)} %get-tuple-element.4) | copy-start | bytes 6389764
  29.7 11.0 %collective-permute-start = (bf16[64,8320]{1,0:T(8,128)(2,1)S(1)}, bf16[64,8320]{1,0:T(8,128)(2,1)S(1)}, u32[]{:S(2)}, u32[]{:S(2)}) collective-permute-start(bf16[64,8320]{1,0:T(8,128)(2,1)S(1)} %slice_bitcast_fusion), channel_id=1, source_target_pairs={{0,4},{4,0},{1,5},{5,1},{2,6},{6,2},{3,7},{7,3},{8,12},{12,8},{9,1... | collective-permute-start | bytes 3194888 | tf_op jit(solution)/shard_map/ppermute | solution.py:368
  40.9 8.4 %copy-start.2 = (bf16[64,8320]{1,0:T(8,128)(2,1)}, bf16[64,8320]{1,0:T(8,128)(2,1)S(1)}, u32[]{:S(2)}) copy-start(bf16[64,8320]{1,0:T(8,128)(2,1)S(1)} %pad_maximum_fusion.1.refs_9_) | copy-start | bytes 3194884
  40.9 28.9 %collective-permute-start.9 = (bf16[64,8320]{1,0:T(8,128)(2,1)S(1)}, bf16[64,8320]{1,0:T(8,128)(2,1)}, u32[]{:S(2)}, u32[]{:S(2)}) collective-permute-start(bf16[64,8320]{1,0:T(8,128)(2,1)S(1)} %pad_maximum_fusion.1.refs_9_), channel_id=1, source_target_pairs={{0,8},{8,16},{16,24},{24,32},{32,40},{40,48},{48,56},{56,0},{1,9},... | collective-permute-start | bytes 3194888 | tf_op jit(solution)/shard_map/ppermute | solution.py:304
  42.8 28.9 %collective-permute-start.10 = (bf16[64,8320]{1,0:T(8,128)(2,1)S(1)}, bf16[64,8320]{1,0:T(8,128)(2,1)}, u32[]{:S(2)}, u32[]{:S(2)}) collective-permute-start(bf16[64,8320]{1,0:T(8,128)(2,1)S(1)} %pad_maximum_fusion.1.refs_9_), channel_id=1, source_target_pairs={{0,56},{8,0},{16,8},{24,16},{32,24},{40,32},{48,40},{56,48},{1,57}... | collective-permute-start | bytes 3194888 | tf_op jit(solution)/shard_map/ppermute | solution.py:304
  48.1 8.2 %copy-start.11 = (s32[4]{0:T(128)S(1)}, s32[4]{0:T(128)}, u32[]{:S(2)}) copy-start(s32[4]{0:T(128)} %constant.147) | copy-start | bytes 52
  48.1 8.2 %copy-start.12 = (s32[4]{0:T(128)S(1)}, s32[4]{0:T(128)}, u32[]{:S(2)}) copy-start(s32[4]{0:T(128)} %constant.149) | copy-start | bytes 52
  49.2 28.6 %collective-permute-start.1 = (bf16[64,8320]{1,0:T(8,128)(2,1)}, bf16[64,8320]{1,0:T(8,128)(2,1)}, u32[]{:S(2)}, u32[]{:S(2)}) collective-permute-start(bf16[64,8320]{1,0:T(8,128)(2,1)} %pad_maximum_fusion.refs_0_), channel_id=1, source_target_pairs={{0,64},{64,128},{128,192},{192,256},{256,320},{320,384},{384,448},... | collective-permute-start | bytes 3194888 | tf_op jit(solution)/shard_map/ppermute | solution.py:304
  52.4 27.3 %collective-permute-start.2 = (bf16[64,8320]{1,0:T(8,128)(2,1)}, bf16[64,8320]{1,0:T(8,128)(2,1)}, u32[]{:S(2)}, u32[]{:S(2)}) collective-permute-start(bf16[64,8320]{1,0:T(8,128)(2,1)} %pad_maximum_fusion.refs_0_), channel_id=1, source_target_pairs={{0,448},{64,0},{128,64},{192,128},{256,192},{320,256},{384,320},{4... | collective-permute-start | bytes 3194888 | tf_op jit(solution)/shard_map/ppermute | solution.py:304
  69.8 27.5 %collective-permute-start.11 = (bf16[64,8320]{1,0:T(8,128)(2,1)}, bf16[64,8320]{1,0:T(8,128)(2,1)}, u32[]{:S(2)}, u32[]{:S(2)}) collective-permute-start(bf16[64,8320]{1,0:T(8,128)(2,1)} %collective-permute-done.9.refs_10_), channel_id=1, source_target_pairs={{0,8},{8,16},{16,24},{24,32},{32,40},{40,48},{48,56},{56,0},{1,9},... | collective-permute-start | bytes 3194888 | tf_op jit(solution)/shard_map/ppermute | solution.py:304
  71.7 27.5 %collective-permute-start.12 = (bf16[64,8320]{1,0:T(8,128)(2,1)}, bf16[64,8320]{1,0:T(8,128)(2,1)}, u32[]{:S(2)}, u32[]{:S(2)}) collective-permute-start(bf16[64,8320]{1,0:T(8,128)(2,1)} %collective-permute-done.10.refs_11_), channel_id=1, source_target_pairs={{0,56},{8,0},{16,8},{24,16},{32,24},{40,32},{48,40},{56,48},{1,57}... | collective-permute-start | bytes 3194888 | tf_op jit(solution)/shard_map/ppermute | solution.py:304
  77.8 27.3 %collective-permute-start.3 = (bf16[64,8320]{1,0:T(8,128)(2,1)}, bf16[64,8320]{1,0:T(8,128)(2,1)}, u32[]{:S(2)}, u32[]{:S(2)}) collective-permute-start(bf16[64,8320]{1,0:T(8,128)(2,1)} %collective-permute-done.1.refs_1_), channel_id=1, source_target_pairs={{0,64},{64,128},{128,192},{192,256},{256,320},{320,384},{384,448},... | collective-permute-start | bytes 3194888 | tf_op jit(solution)/shard_map/ppermute | solution.py:304
  79.8 27.3 %collective-permute-start.4 = (bf16[64,8320]{1,0:T(8,128)(2,1)}, bf16[64,8320]{1,0:T(8,128)(2,1)}, u32[]{:S(2)}, u32[]{:S(2)}) collective-permute-start(bf16[64,8320]{1,0:T(8,128)(2,1)} %collective-permute-done.2.refs_2_), channel_id=1, source_target_pairs={{0,448},{64,0},{128,64},{192,128},{256,192},{320,256},{384,320},{4... | collective-permute-start | bytes 3194888 | tf_op jit(solution)/shard_map/ppermute | solution.py:304
  97.3 26.6 %collective-permute-start.13 = (bf16[64,8320]{1,0:T(8,128)(2,1)}, bf16[64,8320]{1,0:T(8,128)(2,1)S(1)}, u32[]{:S(2)}, u32[]{:S(2)}) collective-permute-start(bf16[64,8320]{1,0:T(8,128)(2,1)} %collective-permute-done.11.refs_12_), channel_id=1, source_target_pairs={{0,8},{8,16},{16,24},{24,32},{32,40},{40,48},{48,56},{56,0},{1,9},... | collective-permute-start | bytes 3194888 | tf_op jit(solution)/shard_map/ppermute | solution.py:304
  99.3 26.6 %collective-permute-start.14 = (bf16[64,8320]{1,0:T(8,128)(2,1)}, bf16[64,8320]{1,0:T(8,128)(2,1)S(1)}, u32[]{:S(2)}, u32[]{:S(2)}) collective-permute-start(bf16[64,8320]{1,0:T(8,128)(2,1)} %collective-permute-done.12.refs_13_), channel_id=1, source_target_pairs={{0,56},{8,0},{16,8},{24,16},{32,24},{40,32},{48,40},{56,48},{1,57}... | collective-permute-start | bytes 3194888 | tf_op jit(solution)/shard_map/ppermute | solution.py:304
  105.1 26.3 %collective-permute-start.5 = (bf16[64,8320]{1,0:T(8,128)(2,1)}, bf16[64,8320]{1,0:T(8,128)(2,1)S(1)}, u32[]{:S(2)}, u32[]{:S(2)}) collective-permute-start(bf16[64,8320]{1,0:T(8,128)(2,1)} %collective-permute-done.3.refs_3_), channel_id=1, source_target_pairs={{0,64},{64,128},{128,192},{192,256},{256,320},{320,384},{384,448},... | collective-permute-start | bytes 3194888 | tf_op jit(solution)/shard_map/ppermute | solution.py:304
  107.1 26.7 %collective-permute-start.6 = (bf16[64,8320]{1,0:T(8,128)(2,1)}, bf16[64,8320]{1,0:T(8,128)(2,1)S(1)}, u32[]{:S(2)}, u32[]{:S(2)}) collective-permute-start(bf16[64,8320]{1,0:T(8,128)(2,1)} %collective-permute-done.4.refs_4_), channel_id=1, source_target_pairs={{0,448},{64,0},{128,64},{192,128},{256,192},{320,256},{384,320},{4... | collective-permute-start | bytes 3194888 | tf_op jit(solution)/shard_map/ppermute | solution.py:304
  123.9 14.3 %copy-start.3 = (bf16[64,8320]{1,0:T(8,128)(2,1)}, bf16[64,8320]{1,0:T(8,128)(2,1)S(1)}, u32[]{:S(2)}) copy-start(bf16[64,8320]{1,0:T(8,128)(2,1)S(1)} %collective-permute-done.13.refs_14_) | copy-start | bytes 3194884
  123.9 14.3 %collective-permute-start.15 = (bf16[32,8320]{1,0:T(8,128)(2,1)S(1)}, bf16[32,8320]{1,0:T(8,128)(2,1)S(1)}, u32[]{:S(2)}, u32[]{:S(2)}) collective-permute-start(bf16[32,8320]{1,0:T(8,128)(2,1)S(1)} %slice.161), channel_id=1, source_target_pairs={{0,8},{8,16},{16,24},{24,32},{32,40},{40,48},{48,56},{56,0},{1,9},... | collective-permute-start | bytes 1597448 | tf_op jit(solution)/shard_map/ppermute | solution.py:304
  125.9 12.3 %copy-start.4 = (bf16[64,8320]{1,0:T(8,128)(2,1)}, bf16[64,8320]{1,0:T(8,128)(2,1)S(1)}, u32[]{:S(2)}) copy-start(bf16[64,8320]{1,0:T(8,128)(2,1)S(1)} %collective-permute-done.14.refs_15_) | copy-start | bytes 3194884
  125.9 13.1 %collective-permute-start.16 = (bf16[32,8320]{1,0:T(8,128)(2,1)S(1)}, bf16[32,8320]{1,0:T(8,128)(2,1)S(1)}, u32[]{:S(2)}, u32[]{:S(2)}) collective-permute-start(bf16[32,8320]{1,0:T(8,128)(2,1)S(1)} %slice.162), channel_id=1, source_target_pairs={{0,56},{8,0},{16,8},{24,16},{32,24},{40,32},{48,40},{56,48},{1,57}... | collective-permute-start | bytes 1597448 | tf_op jit(solution)/shard_map/ppermute | solution.py:304
  131.4 6.8 %copy-start.5 = (bf16[64,8320]{1,0:T(8,128)(2,1)}, bf16[64,8320]{1,0:T(8,128)(2,1)S(1)}, u32[]{:S(2)}) copy-start(bf16[64,8320]{1,0:T(8,128)(2,1)S(1)} %collective-permute-done.5.refs_5_) | copy-start | bytes 3194884
  131.4 13.8 %collective-permute-start.7 = (bf16[32,8320]{1,0:T(8,128)(2,1)S(1)}, bf16[32,8320]{1,0:T(8,128)(2,1)S(1)}, u32[]{:S(2)}, u32[]{:S(2)}) collective-permute-start(bf16[32,8320]{1,0:T(8,128)(2,1)S(1)} %slice.158), channel_id=1, source_target_pairs={{0,64},{64,128},{128,192},{192,256},{256,320},{320,384},{384,448},... | collective-permute-start | bytes 1597448 | tf_op jit(solution)/shard_map/ppermute | solution.py:304
  133.8 12.4 %copy-start.6 = (bf16[64,8320]{1,0:T(8,128)(2,1)}, bf16[64,8320]{1,0:T(8,128)(2,1)S(1)}, u32[]{:S(2)}) copy-start(bf16[64,8320]{1,0:T(8,128)(2,1)S(1)} %collective-permute-done.6.refs_6_) | copy-start | bytes 3194884
  133.9 12.4 %collective-permute-start.8 = (bf16[32,8320]{1,0:T(8,128)(2,1)S(1)}, bf16[32,8320]{1,0:T(8,128)(2,1)S(1)}, u32[]{:S(2)}, u32[]{:S(2)}) collective-permute-start(bf16[32,8320]{1,0:T(8,128)(2,1)S(1)} %slice.159), channel_id=1, source_target_pairs={{0,448},{64,0},{128,64},{192,128},{256,192},{320,256},{384,320},{4... | collective-permute-start | bytes 1597448 | tf_op jit(solution)/shard_map/ppermute | solution.py:304
  138.3 7.9 %copy-start.15 = (bf16[32,8320]{1,0:T(8,128)(2,1)}, bf16[32,8320]{1,0:T(8,128)(2,1)S(1)}, u32[]{:S(2)}) copy-start(bf16[32,8320]{1,0:T(8,128)(2,1)S(1)} %collective-permute-done.15.refs_16_) | copy-start | bytes 1597444
  139.0 7.2 %copy-start.16 = (bf16[32,8320]{1,0:T(8,128)(2,1)}, bf16[32,8320]{1,0:T(8,128)(2,1)S(1)}, u32[]{:S(2)}) copy-start(bf16[32,8320]{1,0:T(8,128)(2,1)S(1)} %collective-permute-done.16.refs_17_) | copy-start | bytes 1597444
  139.0 8.0 %copy-start.9 = (bf16[512,128]{1,0:T(8,128)(2,1)}, bf16[512,128]{1,0:T(8,128)(2,1)S(1)}, u32[]{:S(2)}) copy-start(bf16[512,128]{1,0:T(8,128)(2,1)S(1)} %constant_dynamic-update-slice_fusion.9.refs_20_) | copy-start | bytes 393220
  145.2 1.0 copy-start.17
  146.2 0.8 copy-start.18
  147.1 0.7 copy-start.8
  224.9 11.8 %copy-start.7 = (f32[32,128]{1,0:T(8,128)S(1)}, f32[32,128]{1,0:T(8,128)}, u32[]{:S(2)}) copy-start(f32[32,128]{1,0:T(8,128)} %get-tuple-element.5) | copy-start | bytes 49156
  224.9 28.6 %all-to-all-start = ((f32[16,32,144]{2,1,0:T(8,128)}), f32[16,32,144]{2,1,0:T(8,128)S(1)}, u32[]{:S(2)}, u32[]{:S(2)}) async-start(f32[16,32,144]{2,1,0:T(8,128)} %bitcast.40), calls=%async_computation | async-start | bytes 1048576 | tf_op jit(solution)/shard_map/all_to_all | solution.py:383
  266.0 0.9 copy-start.14

commit v2 on v1

--- a/solution.py
+++ b/solution.py
@@ -23,7 +23,7 @@
 defocus_step = 500.0
 
 META = 128
-CHUNK = 512
+CHUNK = 1024
 PAIRS = ((5, 3, 0, 1), (7, 1, 1, 0), (8, 0, 1, 1), (6, 2, 1, -1))
 
 
@@ -73,7 +73,7 @@
 NT_DIMS = (((1,), (1,)), ((), ()))
 
 
-def prep_kernel(c_ref, xr, xi, qr, qi, w, ctf, binc, cx, sx, cy, sy, meta, out, energy, wc2_s, mag_s):
+def prep_kernel(c_ref, xr, xi, qr, qi, w, ctf, binc, cx, sx, cy, sy, meta, y_keep, z_keep, send, energy, wc2_s, mag_s):
     n, width = xr.shape
     half = width // 2
     c = c_ref[0]
@@ -81,6 +81,25 @@
     acc = jnp.zeros((n, BOX), jnp.float32)
     cyv = cy[...]
     syv = sy[...]
+
+    def put(mine, place, wr, wi, pr, pi):
+        a = pl.ds(place, BOX)
+        b = pl.ds(place + CHUNK, BOX)
+
+        @pl.when(mine)
+        def _():
+            y_keep[:, a] = wr
+            y_keep[:, b] = wi
+            z_keep[:, a] = pr
+            z_keep[:, b] = pi
+
+        @pl.when(jnp.logical_not(mine))
+        def _():
+            send[0:n, a] = wr
+            send[0:n, b] = wi
+            send[n : 2 * n, a] = pr
+            send[n : 2 * n, b] = pi
+
     for g in range(width // BOX):
         sl = pl.ds(g * BOX, BOX)
         wv = w[:, sl]
@@ -99,14 +118,12 @@
         h = (g * BOX) // half
         at = g * BOX - h * half
         place = (at // CHUNK) * 2 * CHUNK + at % CHUNK
-        d = (h + c) % 2
-        out[d, 0:n, pl.ds(place, BOX)] = (factor * (re * co + im * si)).astype(jnp.bfloat16)
-        out[d, 0:n, pl.ds(place + CHUNK, BOX)] = (factor * (im * co - re * si)).astype(jnp.bfloat16)
+        wr = (factor * (re * co + im * si)).astype(jnp.bfloat16)
+        wi = (factor * (im * co - re * si)).astype(jnp.bfloat16)
         acc = acc + wv * (re * re + im * im)
         pr = qr[:, sl]
         pi = qi[:, sl]
-        out[d, n : 2 * n, pl.ds(place, BOX)] = pr
-        out[d, n : 2 * n, pl.ds(place + CHUNK, BOX)] = pi
+        put(c == h, place, wr, wi, pr, pi)
         prf = pr.astype(jnp.float32)
         pif = pi.astype(jnp.float32)
         mag_s[:, sl] = prf * prf + pif * pif
@@ -120,9 +137,12 @@
     for k, part in enumerate(split3(power)):
         spot = jnp.where(lane == row + k * NBIN, 1.0, 0.0).astype(jnp.bfloat16)
         placed = placed + jnp.dot(part, spot, preferred_element_type=jnp.float32)
-    for d in range(2):
-        out[d, 0:n, pl.ds(width, META)] = meta[...]
-        out[d, n : 2 * n, pl.ds(width, META)] = placed.astype(jnp.bfloat16)
+    tail = pl.ds(width, META)
+    placed = placed.astype(jnp.bfloat16)
+    y_keep[:, tail] = meta[...]
+    z_keep[:, tail] = placed
+    send[0:n, tail] = meta[...]
+    send[n : 2 * n, tail] = placed
 
 
 def prepare(c, xr, xi, qr, qi, w, ctf, binc, cx, sx, cy, sy, meta):
@@ -131,39 +151,47 @@
     return pl.pallas_call(
         prep_kernel,
         out_shape=(
-            jax.ShapeDtypeStruct((2, 2 * n, width + META), jnp.bfloat16),
+            jax.ShapeDtypeStruct((n, width + META), jnp.bfloat16),
+            jax.ShapeDtypeStruct((n, width + META), jnp.bfloat16),
+            jax.ShapeDtypeStruct((2 * n, width + META), jnp.bfloat16),
             jax.ShapeDtypeStruct((n, META), jnp.float32),
         ),
         in_specs=[pl.BlockSpec(memory_space=pltpu.SMEM)] + [vm] * 12,
-        out_specs=(vm, vm),
+        out_specs=(vm, vm, vm, vm),
         scratch_shapes=[pltpu.VMEM((NBIN, width), jnp.float32), pltpu.VMEM((n, width), jnp.float32)],
         name="prep",
     )(c, xr, xi, qr, qi, w, ctf, binc, cx, sx, cy, sy, meta)
 
 
 def score_kernel(n_y, n_z, ids, *refs):
-    yb = refs[: n_y + 1]
-    zb = refs[n_y + 1 : n_y + n_z + 2]
-    tables, meta_y, meta_z, out, part_s, proj_s, rot_s, acc, w_s = refs[n_y + n_z + 2 :]
+    it = iter(refs)
+    take = lambda n: [next(it) for _ in range(n)]
+    yb = take(2 * n_y)
+    zb = take(2 * n_z)
+    z_next = take(4)
+    tables, tables_next = take(2)
+    meta_y = take(2 * n_y)
+    meta_z = take(2 * n_z)
+    out, part_s, proj_s, tab_s, rot_s, acc, w_s = take(7)
     step = pl.program_id(0)
     steps = pl.num_programs(0)
-    rows = yb[0].shape[0]
-    half_rows = rows // 2
+    piece = yb[0].shape[0]
+    rows = 2 * piece
+    wide = 2 * rows
+    pairs = n_z // 2
     np_ = n_y * rows
     offs_y = ring_offsets(n_y)
     offs_z = ring_offsets(n_z)
 
-    for k in range(n_y - 1):
-        part_s[k * rows : (k + 1) * rows, :] = yb[k][...]
-    part_s[(n_y - 1) * rows : (n_y - 1) * rows + half_rows, :] = yb[n_y - 1][...]
-    part_s[(n_y - 1) * rows + half_rows : n_y * rows, :] = yb[n_y][...]
-    for k in range(n_z - 1):
-        proj_s[k] = zb[k][...]
-    proj_s[n_z - 1, 0:half_rows, :] = zb[n_z - 1][...]
-    proj_s[n_z - 1, half_rows:rows, :] = zb[n_z][...]
-
-    def rotate(b, slot):
-        for s in range(rows // 16):
+    for k, ref in enumerate(yb):
+        part_s[k * piece : (k + 1) * piece, :] = ref[...]
+    for k, ref in enumerate(zb + z_next):
+        proj_s[k // 4, (k % 4) * piece : (k % 4 + 1) * piece, :] = ref[...]
+    tab_s[0] = tables[...]
+    tab_s[1] = tables_next[...]
+
+    def rotate(b, slot, later):
+        for s in range(wide // 16):
             sl = slice(s * 16, s * 16 + 16)
             for q in range(CHUNK // 256):
                 la = slice(q * 256, q * 256 + 256)
@@ -172,18 +200,18 @@
                 imb = proj_s[b, sl, lb]
                 re = reb.astype(jnp.float32)
                 im = imb.astype(jnp.float32)
-                base = 4 * rows + s * 16
+                base = 4 * wide + s * 16
                 rot_s[slot, base : base + 16, la] = reb
                 rot_s[slot, base : base + 16, lb] = imb
                 for k, (t1, t2, _, _) in enumerate(PAIRS):
-                    co = tables[k : k + 1, la]
-                    si = tables[4 + k : 5 + k, la]
+                    co = tab_s[later, k : k + 1, la]
+                    si = tab_s[later, 4 + k : 5 + k, la]
                     rc = re * co
                     is_ = im * si
                     ic = im * co
                     rs = re * si
-                    b1 = t1 * rows + s * 16
-                    b2 = t2 * rows + s * 16
+                    b1 = t1 * wide + s * 16
+                    b2 = t2 * wide + s * 16
                     rot_s[slot, b1 : b1 + 16, la] = (rc - is_).astype(jnp.bfloat16)
                     rot_s[slot, b1 : b1 + 16, lb] = (ic + rs).astype(jnp.bfloat16)
                     rot_s[slot, b2 : b2 + 16, la] = (rc + is_).astype(jnp.bfloat16)
@@ -192,51 +220,52 @@
     @pl.when(step == 0)
     def _():
         acc[...] = jnp.zeros_like(acc)
-
-    rotate(0, 0)
+        rotate(0, 0, 0)
 
     def body(b, carry):
         acc[b] += lax.dot_general(
             rot_s[b % 2], part_s[...], NT_DIMS, preferred_element_type=jnp.float32
         )
-        rotate(jnp.minimum(b + 1, n_z - 1), (b + 1) % 2)
+        rotate(b + 1, (b + 1) % 2, jnp.where(b + 1 == pairs, 1, 0))
         return carry
 
-    lax.fori_loop(0, n_z, body, 0)
+    lax.fori_loop(0, pairs, body, 0)
 
     @pl.when(step == steps - 1)
     def _():
         my_y = ids[0]
         my_z = ids[1]
         my_c = ids[2]
-        info = jnp.transpose(meta_y[...].astype(jnp.float32)).astype(jnp.int32)
+        info = jnp.concatenate([m[...].astype(jnp.float32) for m in meta_y], axis=0)
+        info = jnp.transpose(info).astype(jnp.int32)
         bins = info[8:9, :]
         r = lax.broadcasted_iota(jnp.int32, (META, np_), 0)
         spot = jnp.where((r % NBIN == bins) & (r < 3 * NBIN), -0.25, 0.0).astype(jnp.bfloat16)
-        power = jnp.dot(meta_z[...], spot, preferred_element_type=jnp.float32)
+        power_parts = jnp.concatenate([m[...] for m in meta_z], axis=0)
+        power = jnp.dot(power_parts, spot, preferred_element_type=jnp.float32)
         for lt in range(np_ // 128):
             la = slice(lt * 128, lt * 128 + 128)
             for t in range(NT):
-                sums = [jnp.zeros((half_rows, 128), jnp.float32) for _ in range(4)]
+                sums = [jnp.zeros((piece, 128), jnp.float32) for _ in range(4)]
                 for k in range(n_z):
                     z_abs = (my_z - offs_z[k] + n_z) % n_z
                     for u in range(2):
                         tile = (my_y * n_z + z_abs) * 2 + (my_c + u) % 2
-                        lo = t * rows + u * half_rows
-                        val = acc[k, lo : lo + half_rows, la]
-                        lo = k * rows + u * half_rows
-                        val = val + power[lo : lo + half_rows, la]
+                        lo = t * wide + (k % 2) * rows + u * piece
+                        val = acc[k // 2, lo : lo + piece, la]
+                        lo = k * rows + u * piece
+                        val = val + power[lo : lo + piece, la]
                         for j in range(4):
                             sums[j] = jnp.where(info[j : j + 1, la] // 2 == tile, val, sums[j])
                 for j in range(4):
                     x = sums[j]
                     start = info[4 + j : 5 + j, la]
                     for bit in (16, 8, 4, 2, 1):
-                        x = jnp.where((start & bit) != 0, pltpu.roll(x, half_rows - bit, 0), x)
+                        x = jnp.where((start & bit) != 0, pltpu.roll(x, piece - bit, 0), x)
                     w_s[j, t * 16 : t * 16 + 16, la] = x[0:16]
         lane = lax.broadcasted_iota(jnp.int32, (1, np_), 1)
         k_of = lane // rows
-        c_of = ((lane // half_rows) + my_c) % 2
+        c_of = ((lane // piece) + my_c) % 2
         y_of = jnp.zeros((1, np_), jnp.int32)
         for k in range(n_y):
             y_of = jnp.where(k_of == k, (my_y - offs_y[k] + n_y) % n_y, y_of)
@@ -249,39 +278,42 @@
             fits = (local >= 0) & (local < per_row)
             slot = jnp.where(fits, (y_of * 2 + c_of) * per_row + local, -1)
             pick = jnp.where(slot_row == slot, 1.0, 0.0).astype(jnp.bfloat16)
-            for piece in split3(w_s[j]):
-                total = total + lax.dot_general(pick, piece, NT_DIMS, preferred_element_type=jnp.float32)
+            for part in split3(w_s[j]):
+                total = total + lax.dot_general(pick, part, NT_DIMS, preferred_element_type=jnp.float32)
         out[...] = total
 
 
-def score(ids, y_blocks, z_blocks, tables, meta_y, meta_z):
-    n_y = len(y_blocks) - 1
-    n_z = len(z_blocks) - 1
-    rows = y_blocks[0].shape[0]
-    width = y_blocks[0].shape[1] - META
-    steps = width // (2 * CHUNK)
+def score(ids, y_pieces, z_pieces, tables):
+    n_y = len(y_pieces) // 2
+    n_z = len(z_pieces) // 2
+    piece = y_pieces[0].shape[0]
+    width = y_pieces[0].shape[1] - META
     span = 2 * CHUNK
-    blocks = [
-        pl.BlockSpec((a.shape[0], span), lambda i, s: (0, i)) for a in list(y_blocks) + list(z_blocks)
-    ]
-    full = lambda a: pl.BlockSpec(a.shape, lambda i, s: (0, 0))
+    steps = width // span
     n_slots = 2 * n_y * 4 * n_z
-    flops = 2 * NT * rows * n_z * rows * n_y * width
+    np_ = 2 * n_y * piece
+    now = pl.BlockSpec((piece, span), lambda i, s: (0, i))
+    later = pl.BlockSpec((piece, span), lambda i, s: (0, jnp.minimum(i + 1, steps - 1)))
+    table = pl.BlockSpec((8, CHUNK), lambda i, s: (0, i))
+    table_later = pl.BlockSpec((8, CHUNK), lambda i, s: (0, jnp.minimum(i + 1, steps - 1)))
+    tail = pl.BlockSpec((piece, META), lambda i, s: (0, width // META))
+    n_all = len(y_pieces) + len(z_pieces)
+    flops = 2 * NT * (2 * n_z * piece) * np_ * width
     return pl.pallas_call(
         functools.partial(score_kernel, n_y, n_z),
         out_shape=jax.ShapeDtypeStruct((n_slots, NT * 16), jnp.float32),
         grid_spec=pltpu.PrefetchScalarGridSpec(
             num_scalar_prefetch=1,
             grid=(steps,),
-            in_specs=blocks
-            + [pl.BlockSpec((8, CHUNK), lambda i, s: (0, i)), full(meta_y), full(meta_z)],
+            in_specs=[now] * n_all + [later] * 4 + [table, table_later] + [tail] * n_all,
             out_specs=pl.BlockSpec((n_slots, NT * 16), lambda i, s: (0, 0)),
             scratch_shapes=[
-                pltpu.VMEM((n_y * rows, span), jnp.bfloat16),
-                pltpu.VMEM((n_z, rows, span), jnp.bfloat16),
-                pltpu.VMEM((2, NT * rows, span), jnp.bfloat16),
-                pltpu.VMEM((n_z, NT * rows, n_y * rows), jnp.float32),
-                pltpu.VMEM((4, NT * 16, n_y * rows), jnp.float32),
+                pltpu.VMEM((np_, span), jnp.bfloat16),
+                pltpu.VMEM((n_z // 2 + 1, 4 * piece, span), jnp.bfloat16),
+                pltpu.VMEM((2, 8, CHUNK), jnp.float32),
+                pltpu.VMEM((2, NT * 4 * piece, span), jnp.bfloat16),
+                pltpu.VMEM((n_z // 2, NT * 4 * piece, np_), jnp.float32),
+                pltpu.VMEM((4, NT * 16, np_), jnp.float32),
             ],
         ),
         compiler_params=pltpu.CompilerParams(
@@ -289,31 +321,30 @@
         ),
         cost_estimate=pl.CostEstimate(flops=flops, transcendentals=0, bytes_accessed=17 * 1024 * 1024),
         name="score",
-    )(ids, *y_blocks, *z_blocks, tables, meta_y, meta_z)
-
-
-def both_rings(a, axis_a, b, axis_b):
-    found = {0: [a], 1: [b]}
-    axes = (axis_a, axis_b)
-    sizes = [lax.axis_size(x) for x in axes]
-    ahead = [a, b]
-    back = [a, b]
-
-    def shift(v, k, d):
-        n = sizes[k]
-        return lax.ppermute(v, axes[k], [(i, (i + d) % n) for i in range(n)])
-
-    for s in range(1, max(sizes) // 2 + 1):
-        for k in range(2):
-            n = sizes[k]
+    )(ids, *y_pieces, *z_pieces, *z_pieces[:4], tables, tables, *y_pieces, *z_pieces)
+
+
+def all_rings(pieces, axes):
+    n = lax.axis_size(axes[0])
+    ahead = list(pieces)
+    back = list(pieces)
+    found = [[p] for p in pieces]
+
+    def shift(v, axis, d):
+        return lax.ppermute(v, axis, [(i, (i + d) % n) for i in range(n)])
+
+    for s in range(1, n // 2 + 1):
+        for k, axis in enumerate(axes):
+            first = k < len(axes) // 2
             if s < n // 2:
-                ahead[k] = shift(ahead[k], k, 1)
-                back[k] = shift(back[k], k, -1)
+                ahead[k] = shift(ahead[k], axis, 1)
+                back[k] = shift(back[k], axis, -1)
                 found[k] += [ahead[k], back[k]]
-            elif s == n // 2:
-                h = a.shape[0] // 2
-                found[k] += [shift(ahead[k][:h], k, 1), shift(back[k][h:], k, -1)]
-    return found[0], found[1]
+            elif first:
+                found[k].append(shift(ahead[k], axis, 1))
+            else:
+                found[k].append(shift(back[k], axis, -1))
+    return found
 
 
 def slot_rank(tile_ids):
@@ -349,7 +380,7 @@
     key = tile_list * 2 + slot_rank(tile_list.reshape(-1)).reshape(count, windows)
     meta = jnp.concatenate([key, ori_start, defocus_bin[:, None]], axis=1)
     meta = jnp.pad(meta, ((0, 0), (0, META - meta.shape[1]))).astype(jnp.bfloat16)
-    sides, energy = prepare(
+    y_keep, z_keep, send, energy = prepare(
         my_c.reshape(1).astype(jnp.int32),
         particles[:, 0],
         particles[:, 1],
@@ -364,20 +395,17 @@
         sy,
         meta,
     )
-    kept = sides[0]
-    got = lax.ppermute(sides[1], TILE[2], [(0, 1), (1, 0)])
-    y_own = jnp.concatenate([kept[:count], got[:count]], axis=0)
-    z_own = jnp.concatenate([kept[count:], got[count:]], axis=0)
-    y_blocks, z_blocks = both_rings(y_own, TILE[0], z_own, TILE[1])
+    got = lax.ppermute(send, TILE[2], [(0, 1), (1, 0)])
+    found = all_rings([y_keep, z_keep, got[:count], got[count:]], [TILE[0], TILE[1], TILE[0], TILE[1]])
+    y_pieces = [p for both in zip(found[0], found[2]) for p in both]
+    z_pieces = [p for both in zip(found[1], found[3]) for p in both]
     mult = jnp.array([[a, b] for _, _, a, b in PAIRS], jnp.int32)
     fx = lax.dynamic_slice_in_dim(freq_x, my_c * half, half)
     fy = lax.dynamic_slice_in_dim(freq_y, my_c * half, half)
     co, si = turn(mult[:, 0:1] * fx[None, :] + mult[:, 1:2] * fy[None, :])
     tables = jnp.concatenate([co, si], axis=0)
-    meta_y = jnp.concatenate([b[:, half * 2 :] for b in y_blocks], axis=0)
-    meta_z = jnp.concatenate([b[:, half * 2 :] for b in z_blocks], axis=0)
     ids = jnp.stack([my_y, my_z, my_c]).astype(jnp.int32)
-    slots = score(ids, y_blocks, z_blocks, tables, meta_y, meta_z)
+    slots = score(ids, y_pieces, z_pieces, tables)
     n_y = lax.axis_size(TILE[0])
     slots = slots.reshape(2 * n_y, -1, NT * 16)
     slots = lax.all_to_all(slots, (TILE[0], TILE[2]), split_axis=0, concat_axis=0, tiled=True)

time: 268 us -> 266 us (level)
  starting transfers between devices: 73.5 us -> 108 us
  waiting for transfers between devices: 61.5 us -> 39.1 us
  local copies, waits for them, and re-layouts: 26.9 us -> 17.8 us
  Pallas kernels: 82.9 us -> 76.7 us
    ppermute x17 -> x29, starting transfers between devices: 62.1 us -> 98.5 us  [the longest x28 95.4 us: shift(): return lax.ppermute(v, axis, [(i, (i + d) % n) for i in range(n)])]
    ppermute x17 -> x29, waiting for transfers between devices: 44.8 us -> 22.4 us  [the longest x28 22.4 us: shift(): return lax.ppermute(v, axis, [(i, (i + d) % n) for i in range(n)])]
    pallas_call x1, Pallas kernels: 77.2 us -> 69.8 us  [score(): pl.pallas_call(functools.partial(score_kernel, n_y, n_z), out_shape=jax.S...]
    unnamed x54 -> x58, local copies, waits for them, and re-layouts: 8.97 us -> 3.42 us
    slice x1, local copies, waits for them, and re-layouts: 5.07 us -> 2.29 us  [per_device(): projections[:, 1]]
  transfers between devices with their start and end apart: 18 -> 30, of which waited for: 11 -> 7; matrix products, arithmetic and copies ran while one was open for 4% -> 1% of each run, Pallas kernels for 0% -> 0%
where the time goes in v2:
time: 266 us; the launch traced here: 264 us
  starting transfers between devices  108 us (41%)
  Pallas kernels  76.7 us (29%)
  waiting for transfers between devices  39.1 us (15%)
  local copies, waits for them, and re-layouts  17.8 us (7%)
  blocking collectives  11 us (4%)
  other arithmetic  10.1 us (4%)
    ppermute x28, starting transfers between devices, shift(): return lax.ppermute(v, axis, [(i, (i + d) % n) for i in range(n)])  95.4 us
    pallas_call x1, Pallas kernels, score(): pl.pallas_call(functools.partial(score_kernel, n_y, n_z), out_shape=jax.S...  69.8 us
    ppermute x28, waiting for transfers between devices, shift(): return lax.ppermute(v, axis, [(i, (i + d) % n) for i in range(n)])  22.4 us
    all_to_all x1, waiting for transfers between devices, per_device(): lax.all_to_all(slots, (TILE[0], TILE[2]), split_axis=0, concat_axis=0, ti...  16.7 us
    all_to_all x1, blocking collectives, per_device(): lax.all_to_all(copies, 'shell', split_axis=0, concat_axis=0, tiled=True)  11 us
    all_to_all x1, starting transfers between devices, per_device(): lax.all_to_all(slots, (TILE[0], TILE[2]), split_axis=0, concat_axis=0, ti...  9.5 us
    pallas_call x1, Pallas kernels, prepare(): pl.pallas_call(prep_kernel, out_shape=(jax.ShapeDtypeStruct((n, width + M...  6.94 us
  transfers between devices with their start and end apart: 30, of which 7 were waited for; matrix products, arithmetic and copies ran while one was open for 1% of the time, Pallas kernels for 0%

profile of v2, /device:TPU:1, one launch (start us, length us, event | category | flops | bytes accessed | tf_op | source)
XLA Modules:
  0.0 264.4 jit_solution(12127563326063146814)
XLA Ops:
  4.6 1.3 copy.53.binc
  6.4 3.8 %fusion.32 = (bf16[32,1,8192]{2,1,0:T(2,128)(2,1)S(1)}, bf16[32,1,8192]{2,1,0:T(2,128)(2,1)S(1)}) fusion(bf16[32,2,8192]{2,1,0:T(2,128)(2,1)} %param.8), kind=kLoop, calls=%fused_computation.83 | loop fusion | bytes 2097152 | tf_op jit(solution)/shard_map/slice | solution.py:386
  10.2 2.3 fusion.31
  13.3 0.8 fusion.22
  14.1 2.1 copy_bitcast_fusion.2
  16.2 2.1 copy_bitcast_fusion
  19.0 3.0 %negate_multiply_fusion.ctf = f32[16,8192]{1,0:T(8,128)} fusion(f32[8192]{0:T(1024)S(1)} %get-tuple-element.38, f32[8192]{0:T(1024)S(1)} %get-tuple-element.39, f32[8192]{0:T(1024)S(1)} %multiply_add_fusion, f32[16]{0:T(128)S(1)} %add_multiply_fusion), kind=kLoop, calls=%fused_computation.6 | loop fusion | flops 917504 | bytes 622656 | tf_op jit(solution)/shard_map/mul | solution.py:55
  22.0 6.9 %prep.1 = (bf16[32,8320]{1,0:T(8,128)(2,1)}, bf16[32,8320]{1,0:T(8,128)(2,1)}, bf16[64,8320]{1,0:T(8,128)(2,1)}, f32[32,128]{1,0:T(8,128)}) custom-call(s32[1]{0:T(128)} %bitcast.2.c_ref, bf16[32,8192]{1,0:T(8,128)(2,1)} %get-tuple-element.33.xr, bf16[32,8192]{1,0:T(8,128)(2,1)} %get-tuple-element.32.xi, bf16[32,8192]{1,0:T(8,128)(2,1)} %get-tuple-element.35.qr, ...), custom_call_target="tpu_custom_call" | custom-call | tf_op jit(solution)/shard_map/prep/pallas_call | solution.py:151
  28.9 5.9 %collective-permute-start.3 = (bf16[32,8320]{1,0:T(8,128)(2,1)}, bf16[32,8320]{1,0:T(8,128)(2,1)S(1)}, u32[]{:S(2)}, u32[]{:S(2)}) collective-permute-start(bf16[32,8320]{1,0:T(8,128)(2,1)} %get-tuple-element.6.refs_0_.refs_38_), channel_id=1, source_target_pairs={{0,448},{64,0},{128,64},{192,128},{256,192},{320,256},{384,320},{4... | collective-permute-start | bytes 1597448 | tf_op jit(solution)/shard_map/ppermute | solution.py:334
  34.9 1.9 collective-permute-start.1
  36.8 10.7 %collective-permute-start.17 = (bf16[32,8320]{1,0:T(8,128)(2,1)}, bf16[32,8320]{1,0:T(8,128)(2,1)S(1)}, u32[]{:S(2)}, u32[]{:S(2)}) collective-permute-start(bf16[32,8320]{1,0:T(8,128)(2,1)} %get-tuple-element.8.refs_16_.refs_32_.refs_54_), channel_id=1, source_target_pairs={{0,56},{8,0},{16,8},{24,16},{32,24},{40,32},{48,40},{56,48},{1,57}... | collective-permute-start | bytes 1597448 | tf_op jit(solution)/shard_map/ppermute | solution.py:334
  47.5 3.1 %collective-permute-start = (bf16[64,8320]{1,0:T(8,128)(2,1)}, bf16[64,8320]{1,0:T(8,128)(2,1)S(1)}, u32[]{:S(2)}, u32[]{:S(2)}) collective-permute-start(bf16[64,8320]{1,0:T(8,128)(2,1)} %get-tuple-element.7), channel_id=1, source_target_pairs={{0,4},{4,0},{1,5},{5,1},{2,6},{6,2},{3,7},{7,3},{8,12},{12,8},{9,1... | collective-permute-start | bytes 3194888 | tf_op jit(solution)/shard_map/ppermute | solution.py:398
  50.6 1.9 collective-permute-start.15
  52.6 4.9 %collective-permute-start.7 = (bf16[32,8320]{1,0:T(8,128)(2,1)S(1)}, bf16[32,8320]{1,0:T(8,128)(2,1)S(1)}, u32[]{:S(2)}, u32[]{:S(2)}) collective-permute-start(bf16[32,8320]{1,0:T(8,128)(2,1)S(1)} %collective-permute-done.3.refs_4_.refs_42_), channel_id=1, source_target_pairs={{0,448},{64,0},{128,64},{192,128},{256,192},{320,256},{384,320},{4... | collective-permute-start | bytes 1597448 | tf_op jit(solution)/shard_map/ppermute | solution.py:334
  57.5 1.9 collective-permute-start.5
  59.4 4.6 %collective-permute-start.21 = (bf16[32,8320]{1,0:T(8,128)(2,1)S(1)}, bf16[32,8320]{1,0:T(8,128)(2,1)S(1)}, u32[]{:S(2)}, u32[]{:S(2)}) collective-permute-start(bf16[32,8320]{1,0:T(8,128)(2,1)S(1)} %collective-permute-done.17.refs_20_.refs_58_), channel_id=1, source_target_pairs={{0,56},{8,0},{16,8},{24,16},{32,24},{40,32},{48,40},{56,48},{1,57}... | collective-permute-start | bytes 1597448 | tf_op jit(solution)/shard_map/ppermute | solution.py:334
  64.0 3.6 %collective-permute-done.15.refs_18_.refs_34_.refs_56_ = bf16[32,8320]{1,0:T(8,128)(2,1)S(1)} collective-permute-done((bf16[32,8320]{1,0:T(8,128)(2,1)}, bf16[32,8320]{1,0:T(8,128)(2,1)S(1)}, u32[]{:S(2)}, u32[]{:S(2)}) %collective-permute-start.15) | collective-permute-done | bytes 532512 | tf_op jit(solution)/shard_map/ppermute | solution.py:334
  67.6 1.9 collective-permute-start.19
  69.5 4.9 %collective-permute-start.11 = (bf16[32,8320]{1,0:T(8,128)(2,1)S(1)}, bf16[32,8320]{1,0:T(8,128)(2,1)S(1)}, u32[]{:S(2)}, u32[]{:S(2)}) collective-permute-start(bf16[32,8320]{1,0:T(8,128)(2,1)S(1)} %collective-permute-done.7.refs_8_.refs_46_), channel_id=1, source_target_pairs={{0,448},{64,0},{128,64},{192,128},{256,192},{320,256},{384,320},{4... | collective-permute-start | bytes 1597448 | tf_op jit(solution)/shard_map/ppermute | solution.py:334
  74.4 1.9 collective-permute-start.9
  76.4 4.6 %collective-permute-start.25 = (bf16[32,8320]{1,0:T(8,128)(2,1)S(1)}, bf16[32,8320]{1,0:T(8,128)(2,1)S(1)}, u32[]{:S(2)}, u32[]{:S(2)}) collective-permute-start(bf16[32,8320]{1,0:T(8,128)(2,1)S(1)} %collective-permute-done.21.refs_24_.refs_62_), channel_id=1, source_target_pairs={{0,56},{8,0},{16,8},{24,16},{32,24},{40,32},{48,40},{56,48},{1,57}... | collective-permute-start | bytes 1597448 | tf_op jit(solution)/shard_map/ppermute | solution.py:334
  81.1 1.9 collective-permute-start.18
  83.6 4.8 %collective-permute-start.4 = (bf16[32,8320]{1,0:T(8,128)(2,1)S(1)}, bf16[32,8320]{1,0:T(8,128)(2,1)S(1)}, u32[]{:S(2)}, u32[]{:S(2)}) collective-permute-start(bf16[32,8320]{1,0:T(8,128)(2,1)S(1)} %get-tuple-element.19.refs_1_.refs_39_), channel_id=1, source_target_pairs={{0,448},{64,0},{128,64},{192,128},{256,192},{320,256},{384,320},{4... | collective-permute-start | bytes 1597448 | tf_op jit(solution)/shard_map/ppermute | solution.py:334
  88.5 2.5 collective-permute-start.23
  91.0 1.9 collective-permute-start.16
  93.0 1.9 collective-permute-start.2
  94.9 7.5 %collective-permute-done.18.refs_21_.refs_59_ = bf16[32,8320]{1,0:T(8,128)(2,1)S(1)} collective-permute-done((bf16[32,8320]{1,0:T(8,128)(2,1)S(1)}, bf16[32,8320]{1,0:T(8,128)(2,1)S(1)}, u32[]{:S(2)}, u32[]{:S(2)}) %collective-permute-start.18) | collective-permute-done | bytes 532512 | tf_op jit(solution)/shard_map/ppermute | solution.py:334
  102.4 5.4 %collective-permute-start.22 = (bf16[32,8320]{1,0:T(8,128)(2,1)S(1)}, bf16[32,8320]{1,0:T(8,128)(2,1)}, u32[]{:S(2)}, u32[]{:S(2)}) collective-permute-start(bf16[32,8320]{1,0:T(8,128)(2,1)S(1)} %collective-permute-done.18.refs_21_.refs_59_), channel_id=1, source_target_pairs={{0,56},{8,0},{16,8},{24,16},{32,24},{40,32},{48,40},{56,48},{1,57}... | collective-permute-start | bytes 1597448 | tf_op jit(solution)/shard_map/ppermute | solution.py:334
  107.8 4.2 %collective-permute-start.8 = (bf16[32,8320]{1,0:T(8,128)(2,1)S(1)}, bf16[32,8320]{1,0:T(8,128)(2,1)}, u32[]{:S(2)}, u32[]{:S(2)}) collective-permute-start(bf16[32,8320]{1,0:T(8,128)(2,1)S(1)} %collective-permute-done.4.refs_5_.refs_43_), channel_id=1, source_target_pairs={{0,448},{64,0},{128,64},{192,128},{256,192},{320,256},{384,320},{4... | collective-permute-start | bytes 1597448 | tf_op jit(solution)/shard_map/ppermute | solution.py:334
  112.1 1.9 collective-permute-start.13
  114.1 0.9 collective-permute-done.16.refs_19_.refs_35_.refs_57_
  114.9 1.9 collective-permute-start.20
  116.9 1.9 collective-permute-start.6
  118.8 4.6 %collective-permute-start.26 = (bf16[32,8320]{1,0:T(8,128)(2,1)}, bf16[32,8320]{1,0:T(8,128)(2,1)S(1)}, u32[]{:S(2)}, u32[]{:S(2)}) collective-permute-start(bf16[32,8320]{1,0:T(8,128)(2,1)} %collective-permute-done.22.refs_25_.refs_63_), channel_id=1, source_target_pairs={{0,56},{8,0},{16,8},{24,16},{32,24},{40,32},{48,40},{56,48},{1,57}... | collective-permute-start | bytes 1597448 | tf_op jit(solution)/shard_map/ppermute | solution.py:334
  123.4 4.8 %collective-permute-start.12 = (bf16[32,8320]{1,0:T(8,128)(2,1)}, bf16[32,8320]{1,0:T(8,128)(2,1)S(1)}, u32[]{:S(2)}, u32[]{:S(2)}) collective-permute-start(bf16[32,8320]{1,0:T(8,128)(2,1)} %collective-permute-done.8.refs_9_.refs_47_), channel_id=1, source_target_pairs={{0,448},{64,0},{128,64},{192,128},{256,192},{320,256},{384,320},{4... | collective-permute-start | bytes 1597448 | tf_op jit(solution)/shard_map/ppermute | solution.py:334
  128.8 1.9 collective-permute-start.27
  130.7 1.9 collective-permute-start.24
  132.7 4.5 %collective-permute-done.6.refs_7_.refs_45_ = bf16[32,8320]{1,0:T(8,128)(2,1)S(1)} collective-permute-done((bf16[32,8320]{1,0:T(8,128)(2,1)}, bf16[32,8320]{1,0:T(8,128)(2,1)S(1)}, u32[]{:S(2)}, u32[]{:S(2)}) %collective-permute-start.6) | collective-permute-done | bytes 532512 | tf_op jit(solution)/shard_map/ppermute | solution.py:334
  137.2 1.9 collective-permute-start.10
  139.1 2.2 collective-permute-start.28
  141.4 4.6 %collective-permute-start.14 = (bf16[32,8320]{1,0:T(8,128)(2,1)S(1)}, bf16[32,8320]{1,0:T(8,128)(2,1)}, u32[]{:S(2)}, u32[]{:S(2)}) collective-permute-start(bf16[32,8320]{1,0:T(8,128)(2,1)S(1)} %collective-permute-done.12.refs_13_.refs_51_), channel_id=1, source_target_pairs={{0,448},{64,0},{128,64},{192,128},{256,192},{320,256},{384,320},{4... | collective-permute-start | bytes 1597448 | tf_op jit(solution)/shard_map/ppermute | solution.py:334
  147.3 5.4 %collective-permute-done.24.refs_27_.refs_65_ = bf16[32,8320]{1,0:T(8,128)(2,1)S(1)} collective-permute-done((bf16[32,8320]{1,0:T(8,128)(2,1)S(1)}, bf16[32,8320]{1,0:T(8,128)(2,1)S(1)}, u32[]{:S(2)}, u32[]{:S(2)}) %collective-permute-start.24) | collective-permute-done | bytes 532512 | tf_op jit(solution)/shard_map/ppermute | solution.py:334
  153.7 0.8 copy-done.27
  154.5 69.8 %score.1 = f32[512,144]{1,0:T(8,128)} custom-call(s32[3]{0:T(128)} %pad_add_fusion.ids, bf16[32,8320]{1,0:T(8,128)(2,1)} %get-tuple-element.6.refs_0_.refs_38_, bf16[32,8320]{1,0:T(8,128)(2,1)} %copy-done.2, bf16[32,8320]{1,0:T(8,128)(2,1)} %copy-done.8, bf16[32,8320]{1,0:T(8,128)(2,1)} %collective-permute-done.2.refs_3_.refs_41_, ...), custom_call_target="tpu_custom_call" | custom-call | flops 38654705664 | bytes 17825792 | tf_op jit(solution)/shard_map/score/pallas_call | solution.py:302
  224.3 9.5 %all-to-all-start = ((f32[16,32,144]{2,1,0:T(8,128)}), f32[16,32,144]{2,1,0:T(8,128)S(1)}, u32[]{:S(2)}, u32[]{:S(2)}) async-start(f32[16,32,144]{2,1,0:T(8,128)} %bitcast.34), calls=%async_computation | async-start | bytes 1048576 | tf_op jit(solution)/shard_map/all_to_all | solution.py:411
  234.3 16.7 %all-to-all-done = f32[16,32,144]{2,1,0:T(8,128)S(1)} async-done(((f32[16,32,144]{2,1,0:T(8,128)}), f32[16,32,144]{2,1,0:T(8,128)S(1)}, u32[]{:S(2)}, u32[]{:S(2)}) %all-to-all-start) | async-done | bytes 294944 | tf_op jit(solution)/shard_map/all_to_all | solution.py:411
  252.0 11.0 %all_to_all.10 = f32[4,32,576]{2,1,0:T(8,128)S(1)} all-to-all(f32[4,32,576]{2,1,0:T(8,128)S(1)} %broadcast_in_dim.39), channel_id=1, replica_groups=mesh['tile_0'=8,'tile_1'=8,'tile_2'=2,'shell'=4] {'shell'}, dimensions={0} | all-to-all | bytes 589824 | tf_op jit(solution)/shard_map/all_to_all | solution.py:417
  263.6 0.8 copy.56
  (124 shorter events, 11.5 us)
Async XLA Ops:
  28.9 23.6 %collective-permute-start.3 = (bf16[32,8320]{1,0:T(8,128)(2,1)}, bf16[32,8320]{1,0:T(8,128)(2,1)S(1)}, u32[]{:S(2)}, u32[]{:S(2)}) collective-permute-start(bf16[32,8320]{1,0:T(8,128)(2,1)} %get-tuple-element.6.refs_0_.refs_38_), channel_id=1, source_target_pairs={{0,448},{64,0},{128,64},{192,128},{256,192},{320,256},{384,320},{4... | collective-permute-start | bytes 1597448 | tf_op jit(solution)/shard_map/ppermute | solution.py:334
  34.9 22.6 %collective-permute-start.1 = (bf16[32,8320]{1,0:T(8,128)(2,1)}, bf16[32,8320]{1,0:T(8,128)(2,1)S(1)}, u32[]{:S(2)}, u32[]{:S(2)}) collective-permute-start(bf16[32,8320]{1,0:T(8,128)(2,1)} %get-tuple-element.6.refs_0_.refs_38_), channel_id=1, source_target_pairs={{0,64},{64,128},{128,192},{192,256},{256,320},{320,384},{384,448},... | collective-permute-start | bytes 1597448 | tf_op jit(solution)/shard_map/ppermute | solution.py:334
  36.8 22.6 %collective-permute-start.17 = (bf16[32,8320]{1,0:T(8,128)(2,1)}, bf16[32,8320]{1,0:T(8,128)(2,1)S(1)}, u32[]{:S(2)}, u32[]{:S(2)}) collective-permute-start(bf16[32,8320]{1,0:T(8,128)(2,1)} %get-tuple-element.8.refs_16_.refs_32_.refs_54_), channel_id=1, source_target_pairs={{0,56},{8,0},{16,8},{24,16},{32,24},{40,32},{48,40},{56,48},{1,57}... | collective-permute-start | bytes 1597448 | tf_op jit(solution)/shard_map/ppermute | solution.py:334
  47.5 80.7 %copy-start.4 = (s32[4]{0:T(128)S(1)}, s32[4]{0:T(128)}, u32[]{:S(2)}) copy-start(s32[4]{0:T(128)} %constant.149) | copy-start | bytes 52
  47.5 80.7 %copy-start.5 = (s32[4]{0:T(128)S(1)}, s32[4]{0:T(128)}, u32[]{:S(2)}) copy-start(s32[4]{0:T(128)} %constant.147) | copy-start | bytes 52
  47.5 33.5 %collective-permute-start = (bf16[64,8320]{1,0:T(8,128)(2,1)}, bf16[64,8320]{1,0:T(8,128)(2,1)S(1)}, u32[]{:S(2)}, u32[]{:S(2)}) collective-permute-start(bf16[64,8320]{1,0:T(8,128)(2,1)} %get-tuple-element.7), channel_id=1, source_target_pairs={{0,4},{4,0},{1,5},{5,1},{2,6},{6,2},{3,7},{7,3},{8,12},{12,8},{9,1... | collective-permute-start | bytes 3194888 | tf_op jit(solution)/shard_map/ppermute | solution.py:398
  50.6 17.0 %collective-permute-start.15 = (bf16[32,8320]{1,0:T(8,128)(2,1)}, bf16[32,8320]{1,0:T(8,128)(2,1)S(1)}, u32[]{:S(2)}, u32[]{:S(2)}) collective-permute-start(bf16[32,8320]{1,0:T(8,128)(2,1)} %get-tuple-element.8.refs_16_.refs_32_.refs_54_), channel_id=1, source_target_pairs={{0,8},{8,16},{16,24},{24,32},{32,40},{40,48},{48,56},{56,0},{1,9},... | collective-permute-start | bytes 1597448 | tf_op jit(solution)/shard_map/ppermute | solution.py:334
  52.6 28.5 %copy-start.7 = (bf16[32,8320]{1,0:T(8,128)(2,1)}, bf16[32,8320]{1,0:T(8,128)(2,1)S(1)}, u32[]{:S(2)}) copy-start(bf16[32,8320]{1,0:T(8,128)(2,1)S(1)} %collective-permute-done.3.refs_4_.refs_42_) | copy-start | bytes 1597444
  52.6 16.9 %collective-permute-start.7 = (bf16[32,8320]{1,0:T(8,128)(2,1)S(1)}, bf16[32,8320]{1,0:T(8,128)(2,1)S(1)}, u32[]{:S(2)}, u32[]{:S(2)}) collective-permute-start(bf16[32,8320]{1,0:T(8,128)(2,1)S(1)} %collective-permute-done.3.refs_4_.refs_42_), channel_id=1, source_target_pairs={{0,448},{64,0},{128,64},{192,128},{256,192},{320,256},{384,320},{4... | collective-permute-start | bytes 1597448 | tf_op jit(solution)/shard_map/ppermute | solution.py:334
  57.5 23.6 %copy-start.8 = (bf16[32,8320]{1,0:T(8,128)(2,1)}, bf16[32,8320]{1,0:T(8,128)(2,1)S(1)}, u32[]{:S(2)}) copy-start(bf16[32,8320]{1,0:T(8,128)(2,1)S(1)} %collective-permute-done.1.refs_2_.refs_40_) | copy-start | bytes 1597444
  57.5 16.9 %collective-permute-start.5 = (bf16[32,8320]{1,0:T(8,128)(2,1)S(1)}, bf16[32,8320]{1,0:T(8,128)(2,1)S(1)}, u32[]{:S(2)}, u32[]{:S(2)}) collective-permute-start(bf16[32,8320]{1,0:T(8,128)(2,1)S(1)} %collective-permute-done.1.refs_2_.refs_40_), channel_id=1, source_target_pairs={{0,64},{64,128},{128,192},{192,256},{256,320},{320,384},{384,448},... | collective-permute-start | bytes 1597448 | tf_op jit(solution)/shard_map/ppermute | solution.py:334
  59.4 21.7 %copy-start.9 = (bf16[32,8320]{1,0:T(8,128)(2,1)}, bf16[32,8320]{1,0:T(8,128)(2,1)S(1)}, u32[]{:S(2)}) copy-start(bf16[32,8320]{1,0:T(8,128)(2,1)S(1)} %collective-permute-done.17.refs_20_.refs_58_) | copy-start | bytes 1597444
  59.4 16.9 %collective-permute-start.21 = (bf16[32,8320]{1,0:T(8,128)(2,1)S(1)}, bf16[32,8320]{1,0:T(8,128)(2,1)S(1)}, u32[]{:S(2)}, u32[]{:S(2)}) collective-permute-start(bf16[32,8320]{1,0:T(8,128)(2,1)S(1)} %collective-permute-done.17.refs_20_.refs_58_), channel_id=1, source_target_pairs={{0,56},{8,0},{16,8},{24,16},{32,24},{40,32},{48,40},{56,48},{1,57}... | collective-permute-start | bytes 1597448 | tf_op jit(solution)/shard_map/ppermute | solution.py:334
  67.6 16.0 %collective-permute-start.19 = (bf16[32,8320]{1,0:T(8,128)(2,1)S(1)}, bf16[32,8320]{1,0:T(8,128)(2,1)}, u32[]{:S(2)}, u32[]{:S(2)}) collective-permute-start(bf16[32,8320]{1,0:T(8,128)(2,1)S(1)} %collective-permute-done.15.refs_18_.refs_34_.refs_56_), channel_id=1, source_target_pairs={{0,8},{8,16},{16,24},{24,32},{32,40},{40,48},{48,56},{56,0},{1,9},... | collective-permute-start | bytes 1597448 | tf_op jit(solution)/shard_map/ppermute | solution.py:334
  69.5 38.3 %copy-start.11 = (bf16[32,8320]{1,0:T(8,128)(2,1)}, bf16[32,8320]{1,0:T(8,128)(2,1)S(1)}, u32[]{:S(2)}) copy-start(bf16[32,8320]{1,0:T(8,128)(2,1)S(1)} %collective-permute-done.7.refs_8_.refs_46_) | copy-start | bytes 1597444
  69.5 18.9 %collective-permute-start.11 = (bf16[32,8320]{1,0:T(8,128)(2,1)S(1)}, bf16[32,8320]{1,0:T(8,128)(2,1)S(1)}, u32[]{:S(2)}, u32[]{:S(2)}) collective-permute-start(bf16[32,8320]{1,0:T(8,128)(2,1)S(1)} %collective-permute-done.7.refs_8_.refs_46_), channel_id=1, source_target_pairs={{0,448},{64,0},{128,64},{192,128},{256,192},{320,256},{384,320},{4... | collective-permute-start | bytes 1597448 | tf_op jit(solution)/shard_map/ppermute | solution.py:334
  74.4 33.4 %copy-start.12 = (bf16[32,8320]{1,0:T(8,128)(2,1)}, bf16[32,8320]{1,0:T(8,128)(2,1)S(1)}, u32[]{:S(2)}) copy-start(bf16[32,8320]{1,0:T(8,128)(2,1)S(1)} %collective-permute-done.5.refs_6_.refs_44_) | copy-start | bytes 1597444
  74.4 16.6 %collective-permute-start.9 = (bf16[32,8320]{1,0:T(8,128)(2,1)S(1)}, bf16[32,8320]{1,0:T(8,128)(2,1)S(1)}, u32[]{:S(2)}, u32[]{:S(2)}) collective-permute-start(bf16[32,8320]{1,0:T(8,128)(2,1)S(1)} %collective-permute-done.5.refs_6_.refs_44_), channel_id=1, source_target_pairs={{0,64},{64,128},{128,192},{192,256},{256,320},{320,384},{384,448},... | collective-permute-start | bytes 1597448 | tf_op jit(solution)/shard_map/ppermute | solution.py:334
  76.4 31.5 %copy-start.13 = (bf16[32,8320]{1,0:T(8,128)(2,1)}, bf16[32,8320]{1,0:T(8,128)(2,1)S(1)}, u32[]{:S(2)}) copy-start(bf16[32,8320]{1,0:T(8,128)(2,1)S(1)} %collective-permute-done.21.refs_24_.refs_62_) | copy-start | bytes 1597444
  76.4 16.6 %collective-permute-start.25 = (bf16[32,8320]{1,0:T(8,128)(2,1)S(1)}, bf16[32,8320]{1,0:T(8,128)(2,1)S(1)}, u32[]{:S(2)}, u32[]{:S(2)}) collective-permute-start(bf16[32,8320]{1,0:T(8,128)(2,1)S(1)} %collective-permute-done.21.refs_24_.refs_62_), channel_id=1, source_target_pairs={{0,56},{8,0},{16,8},{24,16},{32,24},{40,32},{48,40},{56,48},{1,57}... | collective-permute-start | bytes 1597448 | tf_op jit(solution)/shard_map/ppermute | solution.py:334
  81.1 73.4 %copy-start.1 = (bf16[32,8320]{1,0:T(8,128)(2,1)}, bf16[32,8320]{1,0:T(8,128)(2,1)S(1)}, u32[]{:S(2)}) copy-start(bf16[32,8320]{1,0:T(8,128)(2,1)S(1)} %get-tuple-element.18.refs_17_.refs_33_.refs_55_) | copy-start | bytes 1597444
  81.1 73.4 %copy-start.2 = (bf16[32,8320]{1,0:T(8,128)(2,1)}, bf16[32,8320]{1,0:T(8,128)(2,1)S(1)}, u32[]{:S(2)}) copy-start(bf16[32,8320]{1,0:T(8,128)(2,1)S(1)} %get-tuple-element.19.refs_1_.refs_39_) | copy-start | bytes 1597444
  81.1 21.3 %collective-permute-start.18 = (bf16[32,8320]{1,0:T(8,128)(2,1)S(1)}, bf16[32,8320]{1,0:T(8,128)(2,1)S(1)}, u32[]{:S(2)}, u32[]{:S(2)}) collective-permute-start(bf16[32,8320]{1,0:T(8,128)(2,1)S(1)} %get-tuple-element.18.refs_17_.refs_33_.refs_55_), channel_id=1, source_target_pairs={{0,56},{8,0},{16,8},{24,16},{32,24},{40,32},{48,40},{56,48},{1,57}... | collective-permute-start | bytes 1597448 | tf_op jit(solution)/shard_map/ppermute | solution.py:334
  83.6 24.2 %collective-permute-start.4 = (bf16[32,8320]{1,0:T(8,128)(2,1)S(1)}, bf16[32,8320]{1,0:T(8,128)(2,1)S(1)}, u32[]{:S(2)}, u32[]{:S(2)}) collective-permute-start(bf16[32,8320]{1,0:T(8,128)(2,1)S(1)} %get-tuple-element.19.refs_1_.refs_39_), channel_id=1, source_target_pairs={{0,448},{64,0},{128,64},{192,128},{256,192},{320,256},{384,320},{4... | collective-permute-start | bytes 1597448 | tf_op jit(solution)/shard_map/ppermute | solution.py:334
  88.4 19.4 %copy-start.14 = (bf16[32,8320]{1,0:T(8,128)(2,1)}, bf16[32,8320]{1,0:T(8,128)(2,1)S(1)}, u32[]{:S(2)}) copy-start(bf16[32,8320]{1,0:T(8,128)(2,1)S(1)} %collective-permute-done.11.refs_12_.refs_50_) | copy-start | bytes 1597444
  88.5 23.7 %collective-permute-start.23 = (bf16[32,8320]{1,0:T(8,128)(2,1)}, bf16[32,8320]{1,0:T(8,128)(2,1)}, u32[]{:S(2)}, u32[]{:S(2)}) collective-permute-start(bf16[32,8320]{1,0:T(8,128)(2,1)} %collective-permute-done.19.refs_22_.refs_60_), channel_id=1, source_target_pairs={{0,8},{8,16},{16,24},{24,32},{32,40},{40,48},{48,56},{56,0},{1,9},... | collective-permute-start | bytes 1597448 | tf_op jit(solution)/shard_map/ppermute | solution.py:334
  91.0 63.4 %copy-start.15 = (bf16[32,8320]{1,0:T(8,128)(2,1)}, bf16[32,8320]{1,0:T(8,128)(2,1)S(1)}, u32[]{:S(2)}) copy-start(bf16[32,8320]{1,0:T(8,128)(2,1)S(1)} %collective-permute-done.9.refs_10_.refs_48_) | copy-start | bytes 1597444
  91.0 23.9 %collective-permute-start.16 = (bf16[32,8320]{1,0:T(8,128)(2,1)S(1)}, bf16[32,8320]{1,0:T(8,128)(2,1)}, u32[]{:S(2)}, u32[]{:S(2)}) collective-permute-start(bf16[32,8320]{1,0:T(8,128)(2,1)S(1)} %get-tuple-element.18.refs_17_.refs_33_.refs_55_), channel_id=1, source_target_pairs={{0,8},{8,16},{16,24},{24,32},{32,40},{40,48},{48,56},{56,0},{1,9},... | collective-permute-start | bytes 1597448 | tf_op jit(solution)/shard_map/ppermute | solution.py:334
  93.0 61.5 %copy-start.16 = (bf16[32,8320]{1,0:T(8,128)(2,1)}, bf16[32,8320]{1,0:T(8,128)(2,1)S(1)}, u32[]{:S(2)}) copy-start(bf16[32,8320]{1,0:T(8,128)(2,1)S(1)} %collective-permute-done.25.refs_28_.refs_66_) | copy-start | bytes 1597444
  93.0 23.9 %collective-permute-start.2 = (bf16[32,8320]{1,0:T(8,128)(2,1)S(1)}, bf16[32,8320]{1,0:T(8,128)(2,1)}, u32[]{:S(2)}, u32[]{:S(2)}) collective-permute-start(bf16[32,8320]{1,0:T(8,128)(2,1)S(1)} %get-tuple-element.19.refs_1_.refs_39_), channel_id=1, source_target_pairs={{0,64},{64,128},{128,192},{192,256},{256,320},{320,384},{384,448},... | collective-permute-start | bytes 1597448 | tf_op jit(solution)/shard_map/ppermute | solution.py:334
  102.4 52.1 %copy-start.17 = (bf16[32,8320]{1,0:T(8,128)(2,1)}, bf16[32,8320]{1,0:T(8,128)(2,1)S(1)}, u32[]{:S(2)}) copy-start(bf16[32,8320]{1,0:T(8,128)(2,1)S(1)} %collective-permute-done.18.refs_21_.refs_59_) | copy-start | bytes 1597444
  102.4 16.4 %collective-permute-start.22 = (bf16[32,8320]{1,0:T(8,128)(2,1)S(1)}, bf16[32,8320]{1,0:T(8,128)(2,1)}, u32[]{:S(2)}, u32[]{:S(2)}) collective-permute-start(bf16[32,8320]{1,0:T(8,128)(2,1)S(1)} %collective-permute-done.18.refs_21_.refs_59_), channel_id=1, source_target_pairs={{0,56},{8,0},{16,8},{24,16},{32,24},{40,32},{48,40},{56,48},{1,57}... | collective-permute-start | bytes 1597448 | tf_op jit(solution)/shard_map/ppermute | solution.py:334
  107.8 46.7 %copy-start.18 = (bf16[32,8320]{1,0:T(8,128)(2,1)}, bf16[32,8320]{1,0:T(8,128)(2,1)S(1)}, u32[]{:S(2)}) copy-start(bf16[32,8320]{1,0:T(8,128)(2,1)S(1)} %collective-permute-done.4.refs_5_.refs_43_) | copy-start | bytes 1597444
  107.8 15.5 %collective-permute-start.8 = (bf16[32,8320]{1,0:T(8,128)(2,1)S(1)}, bf16[32,8320]{1,0:T(8,128)(2,1)}, u32[]{:S(2)}, u32[]{:S(2)}) collective-permute-start(bf16[32,8320]{1,0:T(8,128)(2,1)S(1)} %collective-permute-done.4.refs_5_.refs_43_), channel_id=1, source_target_pairs={{0,448},{64,0},{128,64},{192,128},{256,192},{320,256},{384,320},{4... | collective-permute-start | bytes 1597448 | tf_op jit(solution)/shard_map/ppermute | solution.py:334
  112.1 16.6 %collective-permute-start.13 = (bf16[32,8320]{1,0:T(8,128)(2,1)S(1)}, bf16[32,8320]{1,0:T(8,128)(2,1)S(1)}, u32[]{:S(2)}, u32[]{:S(2)}) collective-permute-start(bf16[32,8320]{1,0:T(8,128)(2,1)S(1)} %collective-permute-done.9.refs_10_.refs_48_), channel_id=1, source_target_pairs={{0,64},{64,128},{128,192},{192,256},{256,320},{320,384},{384,448},... | collective-permute-start | bytes 1597448 | tf_op jit(solution)/shard_map/ppermute | solution.py:334
  114.9 15.8 %collective-permute-start.20 = (bf16[32,8320]{1,0:T(8,128)(2,1)}, bf16[32,8320]{1,0:T(8,128)(2,1)S(1)}, u32[]{:S(2)}, u32[]{:S(2)}) collective-permute-start(bf16[32,8320]{1,0:T(8,128)(2,1)} %collective-permute-done.16.refs_19_.refs_35_.refs_57_), channel_id=1, source_target_pairs={{0,8},{8,16},{16,24},{24,32},{32,40},{40,48},{48,56},{56,0},{1,9},... | collective-permute-start | bytes 1597448 | tf_op jit(solution)/shard_map/ppermute | solution.py:334
  116.9 20.3 %collective-permute-start.6 = (bf16[32,8320]{1,0:T(8,128)(2,1)}, bf16[32,8320]{1,0:T(8,128)(2,1)S(1)}, u32[]{:S(2)}, u32[]{:S(2)}) collective-permute-start(bf16[32,8320]{1,0:T(8,128)(2,1)} %collective-permute-done.2.refs_3_.refs_41_), channel_id=1, source_target_pairs={{0,64},{64,128},{128,192},{192,256},{256,320},{320,384},{384,448},... | collective-permute-start | bytes 1597448 | tf_op jit(solution)/shard_map/ppermute | solution.py:334
  118.8 20.3 %collective-permute-start.26 = (bf16[32,8320]{1,0:T(8,128)(2,1)}, bf16[32,8320]{1,0:T(8,128)(2,1)S(1)}, u32[]{:S(2)}, u32[]{:S(2)}) collective-permute-start(bf16[32,8320]{1,0:T(8,128)(2,1)} %collective-permute-done.22.refs_25_.refs_63_), channel_id=1, source_target_pairs={{0,56},{8,0},{16,8},{24,16},{32,24},{40,32},{48,40},{56,48},{1,57}... | collective-permute-start | bytes 1597448 | tf_op jit(solution)/shard_map/ppermute | solution.py:334
  123.4 17.9 %collective-permute-start.12 = (bf16[32,8320]{1,0:T(8,128)(2,1)}, bf16[32,8320]{1,0:T(8,128)(2,1)S(1)}, u32[]{:S(2)}, u32[]{:S(2)}) collective-permute-start(bf16[32,8320]{1,0:T(8,128)(2,1)} %collective-permute-done.8.refs_9_.refs_47_), channel_id=1, source_target_pairs={{0,448},{64,0},{128,64},{192,128},{256,192},{320,256},{384,320},{4... | collective-permute-start | bytes 1597448 | tf_op jit(solution)/shard_map/ppermute | solution.py:334
  128.8 25.7 %copy-start.19 = (bf16[32,8320]{1,0:T(8,128)(2,1)}, bf16[32,8320]{1,0:T(8,128)(2,1)S(1)}, u32[]{:S(2)}) copy-start(bf16[32,8320]{1,0:T(8,128)(2,1)S(1)} %collective-permute-done.13.refs_14_.refs_52_) | copy-start | bytes 1597444
  128.8 18.5 %collective-permute-start.27 = (bf16[32,8320]{1,0:T(8,128)(2,1)}, bf16[32,8320]{1,0:T(8,128)(2,1)S(1)}, u32[]{:S(2)}, u32[]{:S(2)}) collective-permute-start(bf16[32,8320]{1,0:T(8,128)(2,1)} %collective-permute-done.23.refs_26_.refs_64_), channel_id=1, source_target_pairs={{0,8},{8,16},{16,24},{24,32},{32,40},{40,48},{48,56},{56,0},{1,9},... | collective-permute-start | bytes 1597448 | tf_op jit(solution)/shard_map/ppermute | solution.py:334
  130.7 16.5 %copy-start.20 = (bf16[32,8320]{1,0:T(8,128)(2,1)}, bf16[32,8320]{1,0:T(8,128)(2,1)S(1)}, u32[]{:S(2)}) copy-start(bf16[32,8320]{1,0:T(8,128)(2,1)S(1)} %collective-permute-done.20.refs_23_.refs_61_) | copy-start | bytes 1597444
  130.7 21.9 %collective-permute-start.24 = (bf16[32,8320]{1,0:T(8,128)(2,1)S(1)}, bf16[32,8320]{1,0:T(8,128)(2,1)S(1)}, u32[]{:S(2)}, u32[]{:S(2)}) collective-permute-start(bf16[32,8320]{1,0:T(8,128)(2,1)S(1)} %collective-permute-done.20.refs_23_.refs_61_), channel_id=1, source_target_pairs={{0,8},{8,16},{16,24},{24,32},{32,40},{40,48},{48,56},{56,0},{1,9},... | collective-permute-start | bytes 1597448 | tf_op jit(solution)/shard_map/ppermute | solution.py:334
  137.2 15.5 %copy-start.21 = (bf16[32,8320]{1,0:T(8,128)(2,1)}, bf16[32,8320]{1,0:T(8,128)(2,1)S(1)}, u32[]{:S(2)}) copy-start(bf16[32,8320]{1,0:T(8,128)(2,1)S(1)} %collective-permute-done.6.refs_7_.refs_45_) | copy-start | bytes 1597444
  137.2 15.5 %collective-permute-start.10 = (bf16[32,8320]{1,0:T(8,128)(2,1)S(1)}, bf16[32,8320]{1,0:T(8,128)(2,1)S(1)}, u32[]{:S(2)}, u32[]{:S(2)}) collective-permute-start(bf16[32,8320]{1,0:T(8,128)(2,1)S(1)} %collective-permute-done.6.refs_7_.refs_45_), channel_id=1, source_target_pairs={{0,64},{64,128},{128,192},{192,256},{256,320},{320,384},{384,448},... | collective-permute-start | bytes 1597448 | tf_op jit(solution)/shard_map/ppermute | solution.py:334
  139.1 13.5 %collective-permute-start.28 = (bf16[32,8320]{1,0:T(8,128)(2,1)S(1)}, bf16[32,8320]{1,0:T(8,128)(2,1)S(1)}, u32[]{:S(2)}, u32[]{:S(2)}) collective-permute-start(bf16[32,8320]{1,0:T(8,128)(2,1)S(1)} %collective-permute-done.26.refs_29_.refs_67_), channel_id=1, source_target_pairs={{0,56},{8,0},{16,8},{24,16},{32,24},{40,32},{48,40},{56,48},{1,57}... | collective-permute-start | bytes 1597448 | tf_op jit(solution)/shard_map/ppermute | solution.py:334
  141.4 13.1 %collective-permute-start.14 = (bf16[32,8320]{1,0:T(8,128)(2,1)S(1)}, bf16[32,8320]{1,0:T(8,128)(2,1)}, u32[]{:S(2)}, u32[]{:S(2)}) collective-permute-start(bf16[32,8320]{1,0:T(8,128)(2,1)S(1)} %collective-permute-done.12.refs_13_.refs_51_), channel_id=1, source_target_pairs={{0,448},{64,0},{128,64},{192,128},{256,192},{320,256},{384,320},{4... | collective-permute-start | bytes 1597448 | tf_op jit(solution)/shard_map/ppermute | solution.py:334
  224.3 26.7 %all-to-all-start = ((f32[16,32,144]{2,1,0:T(8,128)}), f32[16,32,144]{2,1,0:T(8,128)S(1)}, u32[]{:S(2)}, u32[]{:S(2)}) async-start(f32[16,32,144]{2,1,0:T(8,128)} %bitcast.34), calls=%async_computation | async-start | bytes 1048576 | tf_op jit(solution)/shard_map/all_to_all | solution.py:411
  (10 other events, 60.9 us)

commit v3 on v2

--- a/solution.py
+++ b/solution.py
@@ -73,7 +73,7 @@
 NT_DIMS = (((1,), (1,)), ((), ()))
 
 
-def prep_kernel(c_ref, xr, xi, qr, qi, w, ctf, binc, cx, sx, cy, sy, meta, y_keep, z_keep, send, energy, wc2_s, mag_s):
+def prep_kernel(c_ref, xr, xi, qr, qi, w, ctf, binc, cx, sx, cy, sy, meta, own_a, own_b, send, energy, wc2_s, mag_s):
     n, width = xr.shape
     half = width // 2
     c = c_ref[0]
@@ -82,23 +82,21 @@
     cyv = cy[...]
     syv = sy[...]
 
-    def put(mine, place, wr, wi, pr, pi):
-        a = pl.ds(place, BOX)
-        b = pl.ds(place + CHUNK, BOX)
-
-        @pl.when(mine)
-        def _():
-            y_keep[:, a] = wr
-            y_keep[:, b] = wi
-            z_keep[:, a] = pr
-            z_keep[:, b] = pi
-
-        @pl.when(jnp.logical_not(mine))
-        def _():
-            send[0:n, a] = wr
-            send[0:n, b] = wi
-            send[n : 2 * n, a] = pr
-            send[n : 2 * n, b] = pi
+    first = c == 0
+
+    def put(mine, place, own, other):
+        for k in range(2):
+            a = pl.ds(place + k * CHUNK, BOX)
+
+            @pl.when(mine)
+            def _(k=k, a=a):
+                own_a[:, a] = own[k]
+                send[n : 2 * n, a] = other[k]
+
+            @pl.when(jnp.logical_not(mine))
+            def _(k=k, a=a):
+                own_b[:, a] = own[k]
+                send[0:n, a] = other[k]
 
     for g in range(width // BOX):
         sl = pl.ds(g * BOX, BOX)
@@ -123,7 +121,9 @@
         acc = acc + wv * (re * re + im * im)
         pr = qr[:, sl]
         pi = qi[:, sl]
-        put(c == h, place, wr, wi, pr, pi)
+        own = (jnp.where(first, wr, pr), jnp.where(first, wi, pi))
+        other = (jnp.where(first, pr, wr), jnp.where(first, pi, wi))
+        put(c == h, place, own, other)
         prf = pr.astype(jnp.float32)
         pif = pi.astype(jnp.float32)
         mag_s[:, sl] = prf * prf + pif * pif
@@ -139,10 +139,12 @@
         placed = placed + jnp.dot(part, spot, preferred_element_type=jnp.float32)
     tail = pl.ds(width, META)
     placed = placed.astype(jnp.bfloat16)
-    y_keep[:, tail] = meta[...]
-    z_keep[:, tail] = placed
-    send[0:n, tail] = meta[...]
-    send[n : 2 * n, tail] = placed
+    own = jnp.where(first, meta[...], placed)
+    other = jnp.where(first, placed, meta[...])
+    own_a[:, tail] = own
+    own_b[:, tail] = own
+    send[0:n, tail] = other
+    send[n : 2 * n, tail] = other
 
 
 def prepare(c, xr, xi, qr, qi, w, ctf, binc, cx, sx, cy, sy, meta):
@@ -163,36 +165,57 @@
     )(c, xr, xi, qr, qi, w, ctf, binc, cx, sx, cy, sy, meta)
 
 
-def score_kernel(n_y, n_z, ids, *refs):
+def score_kernel(n_pos, ids, *refs):
     it = iter(refs)
     take = lambda n: [next(it) for _ in range(n)]
-    yb = take(2 * n_y)
-    zb = take(2 * n_z)
-    z_next = take(4)
+    mine = take(n_pos + 1)
+    theirs = take(n_pos + 1)
+    mine_next = take(2)
+    theirs_next = take(2)
     tables, tables_next = take(2)
-    meta_y = take(2 * n_y)
-    meta_z = take(2 * n_z)
+    mine_meta = take(n_pos + 1)
+    theirs_meta = take(n_pos + 1)
     out, part_s, proj_s, tab_s, rot_s, acc, w_s = take(7)
     step = pl.program_id(0)
     steps = pl.num_programs(0)
-    piece = yb[0].shape[0]
-    rows = 2 * piece
-    wide = 2 * rows
+    rows = mine[0].shape[0]
+    piece = rows // 2
+    n_y = n_z = n_pos
     pairs = n_z // 2
     np_ = n_y * rows
     offs_y = ring_offsets(n_y)
     offs_z = ring_offsets(n_z)
-
-    for k, ref in enumerate(yb):
-        part_s[k * piece : (k + 1) * piece, :] = ref[...]
-    for k, ref in enumerate(zb + z_next):
-        proj_s[k // 4, (k % 4) * piece : (k % 4 + 1) * piece, :] = ref[...]
+    my_y = ids[0]
+    my_z = ids[1]
+    my_c = ids[2]
+
+    def spread(y_refs, z_refs, z_later):
+        at = 0
+        for ref in y_refs:
+            part_s[at : at + ref.shape[0], :] = ref[...]
+            at += ref.shape[0]
+        at = 0
+        for ref in list(z_refs) + list(z_later):
+            lo = at % (2 * rows)
+            proj_s[at // (2 * rows), lo : lo + ref.shape[0], :] = ref[...]
+            at += ref.shape[0]
+
+    @pl.when(my_c == 0)
+    def _():
+        spread(mine, theirs, theirs_next)
+
+    @pl.when(my_c != 0)
+    def _():
+        spread(theirs, mine, mine_next)
+
     tab_s[0] = tables[...]
     tab_s[1] = tables_next[...]
 
     def rotate(b, slot, later):
-        for s in range(wide // 16):
+        for s in range(2 * rows // 16):
             sl = slice(s * 16, s * 16 + 16)
+            i = s * 16 // rows
+            at = s * 16 % rows
             for q in range(CHUNK // 256):
                 la = slice(q * 256, q * 256 + 256)
                 lb = slice(CHUNK + q * 256, CHUNK + q * 256 + 256)
@@ -200,9 +223,9 @@
                 imb = proj_s[b, sl, lb]
                 re = reb.astype(jnp.float32)
                 im = imb.astype(jnp.float32)
-                base = 4 * wide + s * 16
-                rot_s[slot, base : base + 16, la] = reb
-                rot_s[slot, base : base + 16, lb] = imb
+                base = 4 * rows + at
+                rot_s[slot, i, base : base + 16, la] = reb
+                rot_s[slot, i, base : base + 16, lb] = imb
                 for k, (t1, t2, _, _) in enumerate(PAIRS):
                     co = tab_s[later, k : k + 1, la]
                     si = tab_s[later, 4 + k : 5 + k, la]
@@ -210,12 +233,12 @@
                     is_ = im * si
                     ic = im * co
                     rs = re * si
-                    b1 = t1 * wide + s * 16
-                    b2 = t2 * wide + s * 16
-                    rot_s[slot, b1 : b1 + 16, la] = (rc - is_).astype(jnp.bfloat16)
-                    rot_s[slot, b1 : b1 + 16, lb] = (ic + rs).astype(jnp.bfloat16)
-                    rot_s[slot, b2 : b2 + 16, la] = (rc + is_).astype(jnp.bfloat16)
-                    rot_s[slot, b2 : b2 + 16, lb] = (ic - rs).astype(jnp.bfloat16)
+                    b1 = t1 * rows + at
+                    b2 = t2 * rows + at
+                    rot_s[slot, i, b1 : b1 + 16, la] = (rc - is_).astype(jnp.bfloat16)
+                    rot_s[slot, i, b1 : b1 + 16, lb] = (ic + rs).astype(jnp.bfloat16)
+                    rot_s[slot, i, b2 : b2 + 16, la] = (rc + is_).astype(jnp.bfloat16)
+                    rot_s[slot, i, b2 : b2 + 16, lb] = (ic - rs).astype(jnp.bfloat16)
 
     @pl.when(step == 0)
     def _():
@@ -223,9 +246,10 @@
         rotate(0, 0, 0)
 
     def body(b, carry):
-        acc[b] += lax.dot_general(
-            rot_s[b % 2], part_s[...], NT_DIMS, preferred_element_type=jnp.float32
-        )
+        for i in range(2):
+            acc[2 * b + i] += lax.dot_general(
+                rot_s[b % 2, i], part_s[...], NT_DIMS, preferred_element_type=jnp.float32
+            )
         rotate(b + 1, (b + 1) % 2, jnp.where(b + 1 == pairs, 1, 0))
         return carry
 
@@ -233,15 +257,14 @@
 
     @pl.when(step == steps - 1)
     def _():
-        my_y = ids[0]
-        my_z = ids[1]
-        my_c = ids[2]
-        info = jnp.concatenate([m[...].astype(jnp.float32) for m in meta_y], axis=0)
+        a_meta = jnp.concatenate([m[...] for m in mine_meta], axis=0)
+        b_meta = jnp.concatenate([m[...] for m in theirs_meta], axis=0)
+        info = jnp.where(my_c == 0, a_meta, b_meta).astype(jnp.float32)
+        power_parts = jnp.where(my_c == 0, b_meta, a_meta)
         info = jnp.transpose(info).astype(jnp.int32)
         bins = info[8:9, :]
         r = lax.broadcasted_iota(jnp.int32, (META, np_), 0)
         spot = jnp.where((r % NBIN == bins) & (r < 3 * NBIN), -0.25, 0.0).astype(jnp.bfloat16)
-        power_parts = jnp.concatenate([m[...] for m in meta_z], axis=0)
         power = jnp.dot(power_parts, spot, preferred_element_type=jnp.float32)
         for lt in range(np_ // 128):
             la = slice(lt * 128, lt * 128 + 128)
@@ -250,9 +273,9 @@
                 for k in range(n_z):
                     z_abs = (my_z - offs_z[k] + n_z) % n_z
                     for u in range(2):
-                        tile = (my_y * n_z + z_abs) * 2 + (my_c + u) % 2
-                        lo = t * wide + (k % 2) * rows + u * piece
-                        val = acc[k // 2, lo : lo + piece, la]
+                        tile = (my_y * n_z + z_abs) * 2 + 1 - u
+                        lo = t * rows + u * piece
+                        val = acc[k, lo : lo + piece, la]
                         lo = k * rows + u * piece
                         val = val + power[lo : lo + piece, la]
                         for j in range(4):
@@ -265,7 +288,7 @@
                     w_s[j, t * 16 : t * 16 + 16, la] = x[0:16]
         lane = lax.broadcasted_iota(jnp.int32, (1, np_), 1)
         k_of = lane // rows
-        c_of = ((lane // piece) + my_c) % 2
+        c_of = (lane // piece) % 2
         y_of = jnp.zeros((1, np_), jnp.int32)
         for k in range(n_y):
             y_of = jnp.where(k_of == k, (my_y - offs_y[k] + n_y) % n_y, y_of)
@@ -283,36 +306,35 @@
         out[...] = total
 
 
-def score(ids, y_pieces, z_pieces, tables):
-    n_y = len(y_pieces) // 2
-    n_z = len(z_pieces) // 2
-    piece = y_pieces[0].shape[0]
-    width = y_pieces[0].shape[1] - META
+def score(ids, mine, theirs, tables):
+    n_pos = len(mine) - 1
+    rows = mine[0].shape[0]
+    width = mine[0].shape[1] - META
     span = 2 * CHUNK
     steps = width // span
-    n_slots = 2 * n_y * 4 * n_z
-    np_ = 2 * n_y * piece
-    now = pl.BlockSpec((piece, span), lambda i, s: (0, i))
-    later = pl.BlockSpec((piece, span), lambda i, s: (0, jnp.minimum(i + 1, steps - 1)))
+    n_slots = 2 * n_pos * 4 * n_pos
+    np_ = n_pos * rows
+    after = lambda i, s: (0, jnp.minimum(i + 1, steps - 1))
+    now = [pl.BlockSpec((a.shape[0], span), lambda i, s: (0, i)) for a in mine]
+    later = pl.BlockSpec((rows, span), after)
     table = pl.BlockSpec((8, CHUNK), lambda i, s: (0, i))
-    table_later = pl.BlockSpec((8, CHUNK), lambda i, s: (0, jnp.minimum(i + 1, steps - 1)))
-    tail = pl.BlockSpec((piece, META), lambda i, s: (0, width // META))
-    n_all = len(y_pieces) + len(z_pieces)
-    flops = 2 * NT * (2 * n_z * piece) * np_ * width
+    table_later = pl.BlockSpec((8, CHUNK), after)
+    tail = [pl.BlockSpec((a.shape[0], META), lambda i, s: (0, width // META)) for a in mine]
+    flops = 2 * NT * np_ * np_ * width
     return pl.pallas_call(
-        functools.partial(score_kernel, n_y, n_z),
+        functools.partial(score_kernel, n_pos),
         out_shape=jax.ShapeDtypeStruct((n_slots, NT * 16), jnp.float32),
         grid_spec=pltpu.PrefetchScalarGridSpec(
             num_scalar_prefetch=1,
             grid=(steps,),
-            in_specs=[now] * n_all + [later] * 4 + [table, table_later] + [tail] * n_all,
+            in_specs=now + now + [later] * 4 + [table, table_later] + tail + tail,
             out_specs=pl.BlockSpec((n_slots, NT * 16), lambda i, s: (0, 0)),
             scratch_shapes=[
                 pltpu.VMEM((np_, span), jnp.bfloat16),
-                pltpu.VMEM((n_z // 2 + 1, 4 * piece, span), jnp.bfloat16),
+                pltpu.VMEM((n_pos // 2 + 1, 2 * rows, span), jnp.bfloat16),
                 pltpu.VMEM((2, 8, CHUNK), jnp.float32),
-                pltpu.VMEM((2, NT * 4 * piece, span), jnp.bfloat16),
-                pltpu.VMEM((n_z // 2, NT * 4 * piece, np_), jnp.float32),
+                pltpu.VMEM((2, 2, NT * rows, span), jnp.bfloat16),
+                pltpu.VMEM((n_pos, NT * rows, np_), jnp.float32),
                 pltpu.VMEM((4, NT * 16, np_), jnp.float32),
             ],
         ),
@@ -321,30 +343,38 @@
         ),
         cost_estimate=pl.CostEstimate(flops=flops, transcendentals=0, bytes_accessed=17 * 1024 * 1024),
         name="score",
-    )(ids, *y_pieces, *z_pieces, *z_pieces[:4], tables, tables, *y_pieces, *z_pieces)
-
-
-def all_rings(pieces, axes):
-    n = lax.axis_size(axes[0])
-    ahead = list(pieces)
-    back = list(pieces)
-    found = [[p] for p in pieces]
-
-    def shift(v, axis, d):
-        return lax.ppermute(v, axis, [(i, (i + d) % n) for i in range(n)])
-
+    )(ids, *mine, *theirs, *mine[:2], *theirs[:2], tables, tables, *mine, *theirs)
+
+
+def core_rings(first, second, n):
+    spot = lambda y, z, c: (y % n * n + z % n) * 2 + c
+    cells = [(y, z) for y in range(n) for z in range(n)]
+
+    def shift(v, d):
+        pairs = [(spot(y, z, 0), spot(y + d, z, 0)) for y, z in cells]
+        pairs += [(spot(y, z, 1), spot(y, z + d, 1)) for y, z in cells]
+        return lax.ppermute(v, TILE, pairs)
+
+    def swap(v):
+        return lax.ppermute(v, TILE[2], [(0, 1), (1, 0)])
+
+    ahead = [first, second]
+    back = [first, second]
+    theirs, mine = [swap(first)], [second]
+    h = first.shape[0] // 2
     for s in range(1, n // 2 + 1):
-        for k, axis in enumerate(axes):
-            first = k < len(axes) // 2
+        for k in range(2):
             if s < n // 2:
-                ahead[k] = shift(ahead[k], axis, 1)
-                back[k] = shift(back[k], axis, -1)
-                found[k] += [ahead[k], back[k]]
-            elif first:
-                found[k].append(shift(ahead[k], axis, 1))
+                ahead[k] = shift(ahead[k], 1)
+                back[k] = shift(back[k], -1)
+                new = [ahead[k], back[k]]
             else:
-                found[k].append(shift(back[k], axis, -1))
-    return found
+                new = [shift(ahead[k][:h], 1), shift(back[k][h:], -1)]
+            if k == 0:
+                theirs += [swap(v) for v in new]
+            else:
+                mine += new
+    return mine, theirs
 
 
 def slot_rank(tile_ids):
@@ -380,7 +410,7 @@
     key = tile_list * 2 + slot_rank(tile_list.reshape(-1)).reshape(count, windows)
     meta = jnp.concatenate([key, ori_start, defocus_bin[:, None]], axis=1)
     meta = jnp.pad(meta, ((0, 0), (0, META - meta.shape[1]))).astype(jnp.bfloat16)
-    y_keep, z_keep, send, energy = prepare(
+    own_a, own_b, send, energy = prepare(
         my_c.reshape(1).astype(jnp.int32),
         particles[:, 0],
         particles[:, 1],
@@ -396,16 +426,16 @@
         meta,
     )
     got = lax.ppermute(send, TILE[2], [(0, 1), (1, 0)])
-    found = all_rings([y_keep, z_keep, got[:count], got[count:]], [TILE[0], TILE[1], TILE[0], TILE[1]])
-    y_pieces = [p for both in zip(found[0], found[2]) for p in both]
-    z_pieces = [p for both in zip(found[1], found[3]) for p in both]
+    kept = jnp.concatenate([own_a, got[:count]], axis=0)
+    passed = jnp.concatenate([own_b, got[count:]], axis=0)
+    mine, theirs = core_rings(passed, kept, lax.axis_size(TILE[0]))
     mult = jnp.array([[a, b] for _, _, a, b in PAIRS], jnp.int32)
     fx = lax.dynamic_slice_in_dim(freq_x, my_c * half, half)
     fy = lax.dynamic_slice_in_dim(freq_y, my_c * half, half)
     co, si = turn(mult[:, 0:1] * fx[None, :] + mult[:, 1:2] * fy[None, :])
     tables = jnp.concatenate([co, si], axis=0)
     ids = jnp.stack([my_y, my_z, my_c]).astype(jnp.int32)
-    slots = score(ids, y_pieces, z_pieces, tables)
+    slots = score(ids, mine, theirs, tables)
     n_y = lax.axis_size(TILE[0])
     slots = slots.reshape(2 * n_y, -1, NT * 16)
     slots = lax.all_to_all(slots, (TILE[0], TILE[2]), split_axis=0, concat_axis=0, tiled=True)

time: 266 us -> 259 us (0.974)
  starting transfers between devices: 108 us -> 90.6 us
  waiting for transfers between devices: 39.1 us -> 47.8 us
  local copies, waits for them, and re-layouts: 17.8 us -> 21.9 us
    ppermute x28 -> x25, starting transfers between devices: 95.4 us -> 74.7 us  [the longest x16 53.8 us: shift(): return lax.ppermute(v, TILE, pairs)]
    ppermute x28 -> x25, waiting for transfers between devices: 22.4 us -> 28.5 us  [the longest x16 28.5 us: shift(): return lax.ppermute(v, TILE, pairs)]
    ppermute x1, starting transfers between devices: 3.14 us -> 8.87 us  [per_device(): got = lax.ppermute(send, TILE[2], [(0, 1), (1, 0)])]
    slice x1, local copies, waits for them, and re-layouts: 2.29 us -> 5.07 us  [per_device(): projections[:, 1]]
  transfers between devices with their start and end apart: 30 -> 27, of which waited for: 7 -> 10; matrix products, arithmetic and copies ran while one was open for 1% -> 1% of each run, Pallas kernels for 0% -> 0%
where the time goes in v3:
time: 259 us; the launch traced here: 258 us
  starting transfers between devices  90.6 us (35%)
  Pallas kernels  76.6 us (30%)
  waiting for transfers between devices  47.8 us (18%)
  local copies, waits for them, and re-layouts  21.9 us (8%)
  blocking collectives  11 us (4%)
  other arithmetic  8.96 us (3%)
    pallas_call x1, Pallas kernels, score(): pl.pallas_call(functools.partial(score_kernel, n_pos), out_shape=jax.Shap...  69.2 us
    ppermute x16, starting transfers between devices, shift(): return lax.ppermute(v, TILE, pairs)  53.8 us
    ppermute x16, waiting for transfers between devices, shift(): return lax.ppermute(v, TILE, pairs)  28.5 us
    ppermute x9, starting transfers between devices, swap(): return lax.ppermute(v, TILE[2], [(0, 1), (1, 0)])  20.9 us
    all_to_all x1, waiting for transfers between devices, per_device(): lax.all_to_all(slots, (TILE[0], TILE[2]), split_axis=0, concat_axis=0, ti...  16.7 us
    all_to_all x1, blocking collectives, per_device(): lax.all_to_all(copies, 'shell', split_axis=0, concat_axis=0, tiled=True)  11 us
    ppermute x1, starting transfers between devices, per_device(): got = lax.ppermute(send, TILE[2], [(0, 1), (1, 0)])  8.87 us
    pallas_call x1, Pallas kernels, prepare(): pl.pallas_call(prep_kernel, out_shape=(jax.ShapeDtypeStruct((n, width + M...  7.37 us
  transfers between devices with their start and end apart: 27, of which 10 were waited for; matrix products, arithmetic and copies ran while one was open for 1% of the time, Pallas kernels for 0%

profile of v3, /device:TPU:1, one launch (start us, length us, event | category | flops | bytes accessed | tf_op | source)
XLA Modules:
  0.0 258.1 jit_solution(6231632383519839972)
XLA Ops:
  3.0 5.1 %fusion.31 = (bf16[32,1,8192]{2,1,0:T(2,128)(2,1)S(1)}, bf16[32,1,8192]{2,1,0:T(2,128)(2,1)}) fusion(bf16[32,2,8192]{2,1,0:T(2,128)(2,1)} %param.9), kind=kLoop, calls=%fused_computation.84 | loop fusion | bytes 2097152 | tf_op jit(solution)/shard_map/slice | solution.py:418
  8.1 2.3 fusion.32
  12.5 3.3 %copy_bitcast_fusion = (bf16[32,8192]{1,0:T(8,128)(2,1)}, bf16[32,8192]{1,0:T(8,128)(2,1)}) fusion(bf16[32,1,8192]{2,1,0:T(2,128)(2,1)S(1)} %get-tuple-element.20, bf16[32,1,8192]{2,1,0:T(2,128)(2,1)} %get-tuple-element.21), kind=kLoop, calls=%fused_computation.3 | loop fusion | bytes 2097152 | tf_op jit(solution)/shard_map/squeeze | solution.py:418
  15.8 2.1 copy_bitcast_fusion.2
  17.9 0.8 fusion.22
  19.5 3.0 %negate_multiply_fusion.ctf = f32[16,8192]{1,0:T(8,128)} fusion(f32[8192]{0:T(1024)S(1)} %get-tuple-element.38, f32[8192]{0:T(1024)S(1)} %get-tuple-element.39, f32[8192]{0:T(1024)S(1)} %multiply_add_fusion, f32[16]{0:T(128)S(1)} %add_multiply_fusion), kind=kLoop, calls=%fused_computation.8 | loop fusion | flops 917504 | bytes 622656 | tf_op jit(solution)/shard_map/mul | solution.py:55
  22.5 7.4 %prep.1 = (bf16[32,8320]{1,0:T(8,128)(2,1)}, bf16[32,8320]{1,0:T(8,128)(2,1)}, bf16[64,8320]{1,0:T(8,128)(2,1)}, f32[32,128]{1,0:T(8,128)}) custom-call(s32[1]{0:T(128)} %bitcast.2.c_ref, bf16[32,8192]{1,0:T(8,128)(2,1)} %get-tuple-element.33.xr, bf16[32,8192]{1,0:T(8,128)(2,1)} %get-tuple-element.32.xi, bf16[32,8192]{1,0:T(8,128)(2,1)} %get-tuple-element.35.qr, ...), custom_call_target="tpu_custom_call" | custom-call | tf_op jit(solution)/shard_map/prep/pallas_call | solution.py:153
  29.9 8.9 %collective-permute-start = (bf16[64,8320]{1,0:T(8,128)(2,1)}, bf16[64,8320]{1,0:T(8,128)(2,1)S(1)}, u32[]{:S(2)}, u32[]{:S(2)}) collective-permute-start(bf16[64,8320]{1,0:T(8,128)(2,1)} %get-tuple-element.7), channel_id=1, source_target_pairs={{0,4},{4,0},{1,5},{5,1},{2,6},{6,2},{3,7},{7,3},{8,12},{12,8},{9,1... | collective-permute-start | bytes 3194888 | tf_op jit(solution)/shard_map/ppermute | solution.py:428
  38.7 2.5 collective-permute-done
  41.4 2.1 collective-permute-start.10
  43.5 5.3 %collective-permute-start.12 = (bf16[64,8320]{1,0:T(8,128)(2,1)S(1)}, bf16[64,8320]{1,0:T(8,128)(2,1)}, u32[]{:S(2)}, u32[]{:S(2)}) collective-permute-start(bf16[64,8320]{1,0:T(8,128)(2,1)S(1)} %pad_maximum_fusion.1), channel_id=1, source_target_pairs={{0,448},{8,456},{16,464},{24,472},{32,480},{40,488},{48,496},{56,5... | collective-permute-start | bytes 3194888 | tf_op jit(solution)/shard_map/ppermute | solution.py:356
  48.9 1.9 collective-permute-start.1
  50.8 4.6 %collective-permute-start.2 = (bf16[64,8320]{1,0:T(8,128)(2,1)S(1)}, bf16[64,8320]{1,0:T(8,128)(2,1)S(1)}, u32[]{:S(2)}, u32[]{:S(2)}) collective-permute-start(bf16[64,8320]{1,0:T(8,128)(2,1)S(1)} %pad_maximum_fusion.refs_0_.refs_18_.refs_24_), channel_id=1, source_target_pairs={{0,448},{8,456},{16,464},{24,472},{32,480},{40,488},{48,496},{56,5... | collective-permute-start | bytes 3194888 | tf_op jit(solution)/shard_map/ppermute | solution.py:356
  55.4 4.2 %collective-permute-done.10 = bf16[64,8320]{1,0:T(8,128)(2,1)} collective-permute-done((bf16[64,8320]{1,0:T(8,128)(2,1)S(1)}, bf16[64,8320]{1,0:T(8,128)(2,1)}, u32[]{:S(2)}, u32[]{:S(2)}) %collective-permute-start.10) | collective-permute-done | bytes 1064992 | tf_op jit(solution)/shard_map/ppermute | solution.py:356
  59.6 1.9 collective-permute-start.14
  61.6 4.6 %collective-permute-start.16 = (bf16[64,8320]{1,0:T(8,128)(2,1)}, bf16[64,8320]{1,0:T(8,128)(2,1)}, u32[]{:S(2)}, u32[]{:S(2)}) collective-permute-start(bf16[64,8320]{1,0:T(8,128)(2,1)} %collective-permute-done.12), channel_id=1, source_target_pairs={{0,448},{8,456},{16,464},{24,472},{32,480},{40,488},{48,496},{56,5... | collective-permute-start | bytes 3194888 | tf_op jit(solution)/shard_map/ppermute | solution.py:356
  66.1 4.8 %collective-permute-done.1.refs_1_.refs_19_.refs_25_ = bf16[64,8320]{1,0:T(8,128)(2,1)S(1)} collective-permute-done((bf16[64,8320]{1,0:T(8,128)(2,1)S(1)}, bf16[64,8320]{1,0:T(8,128)(2,1)S(1)}, u32[]{:S(2)}, u32[]{:S(2)}) %collective-permute-start.1) | collective-permute-done | bytes 1064992 | tf_op jit(solution)/shard_map/ppermute | solution.py:356
  70.9 1.9 collective-permute-start.3
  72.9 2.4 collective-permute-start.9
  75.3 5.7 %collective-permute-start.4 = (bf16[64,8320]{1,0:T(8,128)(2,1)S(1)}, bf16[64,8320]{1,0:T(8,128)(2,1)}, u32[]{:S(2)}, u32[]{:S(2)}) collective-permute-start(bf16[64,8320]{1,0:T(8,128)(2,1)S(1)} %collective-permute-done.2.refs_2_.refs_26_), channel_id=1, source_target_pairs={{0,448},{8,456},{16,464},{24,472},{32,480},{40,488},{48,496},{56,5... | collective-permute-start | bytes 3194888 | tf_op jit(solution)/shard_map/ppermute | solution.py:356
  81.0 1.5 collective-permute-done.14
  82.5 1.9 collective-permute-start.18
  84.4 4.6 %collective-permute-start.20 = (bf16[64,8320]{1,0:T(8,128)(2,1)}, bf16[64,8320]{1,0:T(8,128)(2,1)S(1)}, u32[]{:S(2)}, u32[]{:S(2)}) collective-permute-start(bf16[64,8320]{1,0:T(8,128)(2,1)} %collective-permute-done.16), channel_id=1, source_target_pairs={{0,448},{8,456},{16,464},{24,472},{32,480},{40,488},{48,496},{56,5... | collective-permute-start | bytes 3194888 | tf_op jit(solution)/shard_map/ppermute | solution.py:356
  89.0 4.8 %collective-permute-done.3.refs_3_.refs_27_ = bf16[64,8320]{1,0:T(8,128)(2,1)S(1)} collective-permute-done((bf16[64,8320]{1,0:T(8,128)(2,1)S(1)}, bf16[64,8320]{1,0:T(8,128)(2,1)S(1)}, u32[]{:S(2)}, u32[]{:S(2)}) %collective-permute-start.3) | collective-permute-done | bytes 1064992 | tf_op jit(solution)/shard_map/ppermute | solution.py:356
  93.8 1.9 collective-permute-start.5
  95.7 2.4 collective-permute-start.11
  98.1 1.9 collective-permute-start.13
  100.1 5.1 %collective-permute-done.18 = bf16[64,8320]{1,0:T(8,128)(2,1)S(1)} collective-permute-done((bf16[64,8320]{1,0:T(8,128)(2,1)}, bf16[64,8320]{1,0:T(8,128)(2,1)S(1)}, u32[]{:S(2)}, u32[]{:S(2)}) %collective-permute-start.18) | collective-permute-done | bytes 1064992 | tf_op jit(solution)/shard_map/ppermute | solution.py:356
  105.2 2.4 collective-permute-start.15
  107.6 1.9 collective-permute-start.17
  109.5 7.1 %collective-permute-done.5.refs_5_.refs_29_ = bf16[64,8320]{1,0:T(8,128)(2,1)S(1)} collective-permute-done((bf16[64,8320]{1,0:T(8,128)(2,1)S(1)}, bf16[64,8320]{1,0:T(8,128)(2,1)S(1)}, u32[]{:S(2)}, u32[]{:S(2)}) %collective-permute-start.5) | collective-permute-done | bytes 1064992 | tf_op jit(solution)/shard_map/ppermute | solution.py:356
  116.6 3.5 %collective-permute-start.6 = (bf16[64,8320]{1,0:T(8,128)(2,1)}, bf16[64,8320]{1,0:T(8,128)(2,1)}, u32[]{:S(2)}, u32[]{:S(2)}) collective-permute-start(bf16[64,8320]{1,0:T(8,128)(2,1)} %collective-permute-done.4.refs_4_.refs_28_), channel_id=1, source_target_pairs={{0,448},{8,456},{16,464},{24,472},{32,480},{40,488},{48,496},{56,5... | collective-permute-start | bytes 3194888 | tf_op jit(solution)/shard_map/ppermute | solution.py:356
  120.3 1.2 copy-done.6
  121.6 1.9 collective-permute-start.22
  123.5 4.6 %collective-permute-start.24 = (bf16[32,8320]{1,0:T(8,128)(2,1)S(1)}, bf16[32,8320]{1,0:T(8,128)(2,1)S(1)}, u32[]{:S(2)}, u32[]{:S(2)}) collective-permute-start(bf16[32,8320]{1,0:T(8,128)(2,1)S(1)} %slice.67), channel_id=1, source_target_pairs={{0,448},{8,456},{16,464},{24,472},{32,480},{40,488},{48,496},{56,5... | collective-permute-start | bytes 1597448 | tf_op jit(solution)/shard_map/ppermute | solution.py:356
  128.1 1.9 collective-permute-start.7
  130.1 2.3 collective-permute-start.19
  132.9 3.2 %collective-permute-start.21 = (bf16[64,8320]{1,0:T(8,128)(2,1)S(1)}, bf16[64,8320]{1,0:T(8,128)(2,1)S(1)}, u32[]{:S(2)}, u32[]{:S(2)}) collective-permute-start(bf16[64,8320]{1,0:T(8,128)(2,1)S(1)} %copy-done.6), channel_id=1, source_target_pairs={{0,4},{4,0},{1,5},{5,1},{2,6},{6,2},{3,7},{7,3},{8,12},{12,8},{9,1... | collective-permute-start | bytes 3194888 | tf_op jit(solution)/shard_map/ppermute | solution.py:359
  136.8 1.1 slice.64
  137.9 5.6 %collective-permute-start.8 = (bf16[32,8320]{1,0:T(8,128)(2,1)S(1)}, bf16[32,8320]{1,0:T(8,128)(2,1)S(1)}, u32[]{:S(2)}, u32[]{:S(2)}) collective-permute-start(bf16[32,8320]{1,0:T(8,128)(2,1)S(1)} %slice.64), channel_id=1, source_target_pairs={{0,448},{8,456},{16,464},{24,472},{32,480},{40,488},{48,496},{56,5... | collective-permute-start | bytes 1597448 | tf_op jit(solution)/shard_map/ppermute | solution.py:356
  143.5 1.9 collective-permute-start.23
  145.4 2.4 collective-permute-start.25
  150.5 0.9 copy-done.21
  151.3 69.2 %score.1 = f32[512,144]{1,0:T(8,128)} custom-call(s32[3]{0:T(128)} %pad_add_fusion.ids, bf16[64,8320]{1,0:T(8,128)(2,1)} %copy-done.1, bf16[64,8320]{1,0:T(8,128)(2,1)} %copy-done.13, bf16[64,8320]{1,0:T(8,128)(2,1)} %copy-done.14, bf16[64,8320]{1,0:T(8,128)(2,1)} %copy-done.15, bf16[64,8320]{1,0:T(8,128)(2,1)} %collective-permute-done.4.refs_4_.refs_28_, ...), custom_call_target="tpu_custom_call" | custom-call | flops 38654705664 | bytes 17825792 | tf_op jit(solution)/shard_map/score/pallas_call | solution.py:324
  220.6 7.0 %all-to-all-start = ((f32[16,32,144]{2,1,0:T(8,128)}), f32[16,32,144]{2,1,0:T(8,128)S(1)}, u32[]{:S(2)}, u32[]{:S(2)}) async-start(f32[16,32,144]{2,1,0:T(8,128)} %bitcast.34), calls=%async_computation | async-start | bytes 1048576 | tf_op jit(solution)/shard_map/all_to_all | solution.py:441
  228.1 16.7 %all-to-all-done = f32[16,32,144]{2,1,0:T(8,128)S(1)} async-done(((f32[16,32,144]{2,1,0:T(8,128)}), f32[16,32,144]{2,1,0:T(8,128)S(1)}, u32[]{:S(2)}, u32[]{:S(2)}) %all-to-all-start) | async-done | bytes 294944 | tf_op jit(solution)/shard_map/all_to_all | solution.py:441
  245.8 11.0 %all_to_all.10 = f32[4,32,576]{2,1,0:T(8,128)S(1)} all-to-all(f32[4,32,576]{2,1,0:T(8,128)S(1)} %broadcast_in_dim.39), channel_id=1, replica_groups=mesh['tile_0'=8,'tile_1'=8,'tile_2'=2,'shell'=4] {'shell'}, dimensions={0} | all-to-all | bytes 589824 | tf_op jit(solution)/shard_map/all_to_all | solution.py:447
  257.3 0.8 copy.56
  (112 shorter events, 11.4 us)
Async XLA Ops:
  3.0 5.1 %copy-start = (bf16[32,2,8192]{2,1,0:T(2,128)(2,1)S(1)}, bf16[32,2,8192]{2,1,0:T(2,128)(2,1)}, u32[]{:S(2)}) copy-start(bf16[32,2,8192]{2,1,0:T(2,128)(2,1)} %param.8) | copy-start | bytes 3145732
  8.1 2.8 %copy-start.8 = (s32[32,4]{0,1:T(4,128)S(1)}, s32[32,4]{0,1:T(4,128)}, u32[]{:S(2)}) copy-start(s32[32,4]{0,1:T(4,128)} %param.12) | copy-start | bytes 1540
  8.1 2.9 %copy-start.11 = (s32[32]{0:T(128)S(1)}, s32[32]{0:T(128)}, u32[]{:S(2)}) copy-start(s32[32]{0:T(128)} %param.14) | copy-start | bytes 388
  29.9 11.5 %copy-start.3 = (bf16[32,8320]{1,0:T(8,128)(2,1)S(1)}, bf16[32,8320]{1,0:T(8,128)(2,1)}, u32[]{:S(2)}) copy-start(bf16[32,8320]{1,0:T(8,128)(2,1)} %get-tuple-element.8) | copy-start | bytes 1597444
  29.9 11.4 %collective-permute-start = (bf16[64,8320]{1,0:T(8,128)(2,1)}, bf16[64,8320]{1,0:T(8,128)(2,1)S(1)}, u32[]{:S(2)}, u32[]{:S(2)}) collective-permute-start(bf16[64,8320]{1,0:T(8,128)(2,1)} %get-tuple-element.7), channel_id=1, source_target_pairs={{0,4},{4,0},{1,5},{5,1},{2,6},{6,2},{3,7},{7,3},{8,12},{12,8},{9,1... | collective-permute-start | bytes 3194888 | tf_op jit(solution)/shard_map/ppermute | solution.py:428
  41.3 7.5 %copy-start.2 = (bf16[32,8320]{1,0:T(8,128)(2,1)S(1)}, bf16[32,8320]{1,0:T(8,128)(2,1)}, u32[]{:S(2)}) copy-start(bf16[32,8320]{1,0:T(8,128)(2,1)} %get-tuple-element.6) | copy-start | bytes 1597444
  41.4 18.2 %collective-permute-start.10 = (bf16[64,8320]{1,0:T(8,128)(2,1)S(1)}, bf16[64,8320]{1,0:T(8,128)(2,1)}, u32[]{:S(2)}, u32[]{:S(2)}) collective-permute-start(bf16[64,8320]{1,0:T(8,128)(2,1)S(1)} %pad_maximum_fusion.1), channel_id=1, source_target_pairs={{0,64},{8,72},{16,80},{24,88},{32,96},{40,104},{48,112},{56,120},{... | collective-permute-start | bytes 3194888 | tf_op jit(solution)/shard_map/ppermute | solution.py:356
  43.5 18.1 %collective-permute-start.12 = (bf16[64,8320]{1,0:T(8,128)(2,1)S(1)}, bf16[64,8320]{1,0:T(8,128)(2,1)}, u32[]{:S(2)}, u32[]{:S(2)}) collective-permute-start(bf16[64,8320]{1,0:T(8,128)(2,1)S(1)} %pad_maximum_fusion.1), channel_id=1, source_target_pairs={{0,448},{8,456},{16,464},{24,472},{32,480},{40,488},{48,496},{56,5... | collective-permute-start | bytes 3194888 | tf_op jit(solution)/shard_map/ppermute | solution.py:356
  48.9 72.6 %copy-start.1 = (bf16[64,8320]{1,0:T(8,128)(2,1)}, bf16[64,8320]{1,0:T(8,128)(2,1)S(1)}, u32[]{:S(2)}) copy-start(bf16[64,8320]{1,0:T(8,128)(2,1)S(1)} %pad_maximum_fusion.refs_0_.refs_18_.refs_24_) | copy-start | bytes 3194884
  48.9 22.0 %collective-permute-start.1 = (bf16[64,8320]{1,0:T(8,128)(2,1)S(1)}, bf16[64,8320]{1,0:T(8,128)(2,1)S(1)}, u32[]{:S(2)}, u32[]{:S(2)}) collective-permute-start(bf16[64,8320]{1,0:T(8,128)(2,1)S(1)} %pad_maximum_fusion.refs_0_.refs_18_.refs_24_), channel_id=1, source_target_pairs={{0,64},{8,72},{16,80},{24,88},{32,96},{40,104},{48,112},{56,120},{... | collective-permute-start | bytes 3194888 | tf_op jit(solution)/shard_map/ppermute | solution.py:356
  50.8 24.4 %collective-permute-start.2 = (bf16[64,8320]{1,0:T(8,128)(2,1)S(1)}, bf16[64,8320]{1,0:T(8,128)(2,1)S(1)}, u32[]{:S(2)}, u32[]{:S(2)}) collective-permute-start(bf16[64,8320]{1,0:T(8,128)(2,1)S(1)} %pad_maximum_fusion.refs_0_.refs_18_.refs_24_), channel_id=1, source_target_pairs={{0,448},{8,456},{16,464},{24,472},{32,480},{40,488},{48,496},{56,5... | collective-permute-start | bytes 3194888 | tf_op jit(solution)/shard_map/ppermute | solution.py:356
  59.6 22.8 %collective-permute-start.14 = (bf16[64,8320]{1,0:T(8,128)(2,1)}, bf16[64,8320]{1,0:T(8,128)(2,1)}, u32[]{:S(2)}, u32[]{:S(2)}) collective-permute-start(bf16[64,8320]{1,0:T(8,128)(2,1)} %collective-permute-done.10), channel_id=1, source_target_pairs={{0,64},{8,72},{16,80},{24,88},{32,96},{40,104},{48,112},{56,120},{... | collective-permute-start | bytes 3194888 | tf_op jit(solution)/shard_map/ppermute | solution.py:356
  61.6 22.8 %collective-permute-start.16 = (bf16[64,8320]{1,0:T(8,128)(2,1)}, bf16[64,8320]{1,0:T(8,128)(2,1)}, u32[]{:S(2)}, u32[]{:S(2)}) collective-permute-start(bf16[64,8320]{1,0:T(8,128)(2,1)} %collective-permute-done.12), channel_id=1, source_target_pairs={{0,448},{8,456},{16,464},{24,472},{32,480},{40,488},{48,496},{56,5... | collective-permute-start | bytes 3194888 | tf_op jit(solution)/shard_map/ppermute | solution.py:356
  70.9 18.0 %copy-start.13 = (bf16[64,8320]{1,0:T(8,128)(2,1)}, bf16[64,8320]{1,0:T(8,128)(2,1)S(1)}, u32[]{:S(2)}) copy-start(bf16[64,8320]{1,0:T(8,128)(2,1)S(1)} %collective-permute-done.1.refs_1_.refs_19_.refs_25_) | copy-start | bytes 3194884
  70.9 22.8 %collective-permute-start.3 = (bf16[64,8320]{1,0:T(8,128)(2,1)S(1)}, bf16[64,8320]{1,0:T(8,128)(2,1)S(1)}, u32[]{:S(2)}, u32[]{:S(2)}) collective-permute-start(bf16[64,8320]{1,0:T(8,128)(2,1)S(1)} %collective-permute-done.1.refs_1_.refs_19_.refs_25_), channel_id=1, source_target_pairs={{0,64},{8,72},{16,80},{24,88},{32,96},{40,104},{48,112},{56,120},{... | collective-permute-start | bytes 3194888 | tf_op jit(solution)/shard_map/ppermute | solution.py:356
  72.9 22.8 %collective-permute-start.9 = (bf16[64,8320]{1,0:T(8,128)(2,1)S(1)}, bf16[64,8320]{1,0:T(8,128)(2,1)S(1)}, u32[]{:S(2)}, u32[]{:S(2)}) collective-permute-start(bf16[64,8320]{1,0:T(8,128)(2,1)S(1)} %pad_maximum_fusion.1), channel_id=1, source_target_pairs={{0,4},{4,0},{1,5},{5,1},{2,6},{6,2},{3,7},{7,3},{8,12},{12,8},{9,1... | collective-permute-start | bytes 3194888 | tf_op jit(solution)/shard_map/ppermute | solution.py:359
  75.3 41.3 %copy-start.14 = (bf16[64,8320]{1,0:T(8,128)(2,1)}, bf16[64,8320]{1,0:T(8,128)(2,1)S(1)}, u32[]{:S(2)}) copy-start(bf16[64,8320]{1,0:T(8,128)(2,1)S(1)} %collective-permute-done.2.refs_2_.refs_26_) | copy-start | bytes 3194884
  75.3 22.8 %collective-permute-start.4 = (bf16[64,8320]{1,0:T(8,128)(2,1)S(1)}, bf16[64,8320]{1,0:T(8,128)(2,1)}, u32[]{:S(2)}, u32[]{:S(2)}) collective-permute-start(bf16[64,8320]{1,0:T(8,128)(2,1)S(1)} %collective-permute-done.2.refs_2_.refs_26_), channel_id=1, source_target_pairs={{0,448},{8,456},{16,464},{24,472},{32,480},{40,488},{48,496},{56,5... | collective-permute-start | bytes 3194888 | tf_op jit(solution)/shard_map/ppermute | solution.py:356
  82.5 22.7 %collective-permute-start.18 = (bf16[64,8320]{1,0:T(8,128)(2,1)}, bf16[64,8320]{1,0:T(8,128)(2,1)S(1)}, u32[]{:S(2)}, u32[]{:S(2)}) collective-permute-start(bf16[64,8320]{1,0:T(8,128)(2,1)} %collective-permute-done.14), channel_id=1, source_target_pairs={{0,64},{8,72},{16,80},{24,88},{32,96},{40,104},{48,112},{56,120},{... | collective-permute-start | bytes 3194888 | tf_op jit(solution)/shard_map/ppermute | solution.py:356
  84.4 23.2 %collective-permute-start.20 = (bf16[64,8320]{1,0:T(8,128)(2,1)}, bf16[64,8320]{1,0:T(8,128)(2,1)S(1)}, u32[]{:S(2)}, u32[]{:S(2)}) collective-permute-start(bf16[64,8320]{1,0:T(8,128)(2,1)} %collective-permute-done.16), channel_id=1, source_target_pairs={{0,448},{8,456},{16,464},{24,472},{32,480},{40,488},{48,496},{56,5... | collective-permute-start | bytes 3194888 | tf_op jit(solution)/shard_map/ppermute | solution.py:356
  93.8 22.8 %copy-start.15 = (bf16[64,8320]{1,0:T(8,128)(2,1)}, bf16[64,8320]{1,0:T(8,128)(2,1)S(1)}, u32[]{:S(2)}) copy-start(bf16[64,8320]{1,0:T(8,128)(2,1)S(1)} %collective-permute-done.3.refs_3_.refs_27_) | copy-start | bytes 3194884
  93.8 22.8 %collective-permute-start.5 = (bf16[64,8320]{1,0:T(8,128)(2,1)S(1)}, bf16[64,8320]{1,0:T(8,128)(2,1)S(1)}, u32[]{:S(2)}, u32[]{:S(2)}) collective-permute-start(bf16[64,8320]{1,0:T(8,128)(2,1)S(1)} %collective-permute-done.3.refs_3_.refs_27_), channel_id=1, source_target_pairs={{0,64},{8,72},{16,80},{24,88},{32,96},{40,104},{48,112},{56,120},{... | collective-permute-start | bytes 3194888 | tf_op jit(solution)/shard_map/ppermute | solution.py:356
  95.7 20.9 %copy-start.16 = (bf16[64,8320]{1,0:T(8,128)(2,1)}, bf16[64,8320]{1,0:T(8,128)(2,1)S(1)}, u32[]{:S(2)}) copy-start(bf16[64,8320]{1,0:T(8,128)(2,1)S(1)} %collective-permute-done.9.refs_9_.refs_20_.refs_33_) | copy-start | bytes 3194884
  95.7 25.9 %collective-permute-start.11 = (bf16[64,8320]{1,0:T(8,128)(2,1)}, bf16[64,8320]{1,0:T(8,128)(2,1)}, u32[]{:S(2)}, u32[]{:S(2)}) collective-permute-start(bf16[64,8320]{1,0:T(8,128)(2,1)} %collective-permute-done.10), channel_id=1, source_target_pairs={{0,4},{4,0},{1,5},{5,1},{2,6},{6,2},{3,7},{7,3},{8,12},{12,8},{9,1... | collective-permute-start | bytes 3194888 | tf_op jit(solution)/shard_map/ppermute | solution.py:359
  98.1 25.4 %collective-permute-start.13 = (bf16[64,8320]{1,0:T(8,128)(2,1)}, bf16[64,8320]{1,0:T(8,128)(2,1)}, u32[]{:S(2)}, u32[]{:S(2)}) collective-permute-start(bf16[64,8320]{1,0:T(8,128)(2,1)} %collective-permute-done.12), channel_id=1, source_target_pairs={{0,4},{4,0},{1,5},{5,1},{2,6},{6,2},{3,7},{7,3},{8,12},{12,8},{9,1... | collective-permute-start | bytes 3194888 | tf_op jit(solution)/shard_map/ppermute | solution.py:359
  105.2 23.0 %collective-permute-start.15 = (bf16[64,8320]{1,0:T(8,128)(2,1)}, bf16[64,8320]{1,0:T(8,128)(2,1)}, u32[]{:S(2)}, u32[]{:S(2)}) collective-permute-start(bf16[64,8320]{1,0:T(8,128)(2,1)} %collective-permute-done.14), channel_id=1, source_target_pairs={{0,4},{4,0},{1,5},{5,1},{2,6},{6,2},{3,7},{7,3},{8,12},{12,8},{9,1... | collective-permute-start | bytes 3194888 | tf_op jit(solution)/shard_map/ppermute | solution.py:359
  107.6 9.0 %copy-start.5 = (bf16[64,8320]{1,0:T(8,128)(2,1)}, bf16[64,8320]{1,0:T(8,128)(2,1)S(1)}, u32[]{:S(2)}) copy-start(bf16[64,8320]{1,0:T(8,128)(2,1)S(1)} %collective-permute-done.20) | copy-start | bytes 3194884
  107.6 22.5 %collective-permute-start.17 = (bf16[64,8320]{1,0:T(8,128)(2,1)}, bf16[64,8320]{1,0:T(8,128)(2,1)}, u32[]{:S(2)}, u32[]{:S(2)}) collective-permute-start(bf16[64,8320]{1,0:T(8,128)(2,1)} %collective-permute-done.16), channel_id=1, source_target_pairs={{0,4},{4,0},{1,5},{5,1},{2,6},{6,2},{3,7},{7,3},{8,12},{12,8},{9,1... | collective-permute-start | bytes 3194888 | tf_op jit(solution)/shard_map/ppermute | solution.py:359
  116.6 4.9 %copy-start.4 = (bf16[64,8320]{1,0:T(8,128)(2,1)}, bf16[64,8320]{1,0:T(8,128)(2,1)S(1)}, u32[]{:S(2)}) copy-start(bf16[64,8320]{1,0:T(8,128)(2,1)S(1)} %collective-permute-done.5.refs_5_.refs_29_) | copy-start | bytes 3194884
  116.6 16.3 %collective-permute-start.6 = (bf16[64,8320]{1,0:T(8,128)(2,1)}, bf16[64,8320]{1,0:T(8,128)(2,1)}, u32[]{:S(2)}, u32[]{:S(2)}) collective-permute-start(bf16[64,8320]{1,0:T(8,128)(2,1)} %collective-permute-done.4.refs_4_.refs_28_), channel_id=1, source_target_pairs={{0,448},{8,456},{16,464},{24,472},{32,480},{40,488},{48,496},{56,5... | collective-permute-start | bytes 3194888 | tf_op jit(solution)/shard_map/ppermute | solution.py:356
  120.3 1.2 copy-start.6
  121.5 14.7 %copy-start.9 = (s32[4]{0:T(128)S(1)}, s32[4]{0:T(128)}, u32[]{:S(2)}) copy-start(s32[4]{0:T(128)} %constant.147) | copy-start | bytes 52
  121.5 14.7 %copy-start.10 = (s32[4]{0:T(128)S(1)}, s32[4]{0:T(128)}, u32[]{:S(2)}) copy-start(s32[4]{0:T(128)} %constant.149) | copy-start | bytes 52
  121.6 16.3 %collective-permute-start.22 = (bf16[32,8320]{1,0:T(8,128)(2,1)S(1)}, bf16[32,8320]{1,0:T(8,128)(2,1)S(1)}, u32[]{:S(2)}, u32[]{:S(2)}) collective-permute-start(bf16[32,8320]{1,0:T(8,128)(2,1)S(1)} %slice.66), channel_id=1, source_target_pairs={{0,64},{8,72},{16,80},{24,88},{32,96},{40,104},{48,112},{56,120},{... | collective-permute-start | bytes 1597448 | tf_op jit(solution)/shard_map/ppermute | solution.py:356
  123.5 19.9 %collective-permute-start.24 = (bf16[32,8320]{1,0:T(8,128)(2,1)S(1)}, bf16[32,8320]{1,0:T(8,128)(2,1)S(1)}, u32[]{:S(2)}, u32[]{:S(2)}) collective-permute-start(bf16[32,8320]{1,0:T(8,128)(2,1)S(1)} %slice.67), channel_id=1, source_target_pairs={{0,448},{8,456},{16,464},{24,472},{32,480},{40,488},{48,496},{56,5... | collective-permute-start | bytes 1597448 | tf_op jit(solution)/shard_map/ppermute | solution.py:356
  128.1 17.3 %collective-permute-start.7 = (bf16[32,8320]{1,0:T(8,128)(2,1)S(1)}, bf16[32,8320]{1,0:T(8,128)(2,1)S(1)}, u32[]{:S(2)}, u32[]{:S(2)}) collective-permute-start(bf16[32,8320]{1,0:T(8,128)(2,1)S(1)} %slice.63), channel_id=1, source_target_pairs={{0,64},{8,72},{16,80},{24,88},{32,96},{40,104},{48,112},{56,120},{... | collective-permute-start | bytes 1597448 | tf_op jit(solution)/shard_map/ppermute | solution.py:356
  130.1 19.6 %collective-permute-start.19 = (bf16[64,8320]{1,0:T(8,128)(2,1)S(1)}, bf16[64,8320]{1,0:T(8,128)(2,1)S(1)}, u32[]{:S(2)}, u32[]{:S(2)}) collective-permute-start(bf16[64,8320]{1,0:T(8,128)(2,1)S(1)} %collective-permute-done.18), channel_id=1, source_target_pairs={{0,4},{4,0},{1,5},{5,1},{2,6},{6,2},{3,7},{7,3},{8,12},{12,8},{9,1... | collective-permute-start | bytes 3194888 | tf_op jit(solution)/shard_map/ppermute | solution.py:359
  132.9 16.7 %collective-permute-start.21 = (bf16[64,8320]{1,0:T(8,128)(2,1)S(1)}, bf16[64,8320]{1,0:T(8,128)(2,1)S(1)}, u32[]{:S(2)}, u32[]{:S(2)}) collective-permute-start(bf16[64,8320]{1,0:T(8,128)(2,1)S(1)} %copy-done.6), channel_id=1, source_target_pairs={{0,4},{4,0},{1,5},{5,1},{2,6},{6,2},{3,7},{7,3},{8,12},{12,8},{9,1... | collective-permute-start | bytes 3194888 | tf_op jit(solution)/shard_map/ppermute | solution.py:359
  137.9 11.8 %collective-permute-start.8 = (bf16[32,8320]{1,0:T(8,128)(2,1)S(1)}, bf16[32,8320]{1,0:T(8,128)(2,1)S(1)}, u32[]{:S(2)}, u32[]{:S(2)}) collective-permute-start(bf16[32,8320]{1,0:T(8,128)(2,1)S(1)} %slice.64), channel_id=1, source_target_pairs={{0,448},{8,456},{16,464},{24,472},{32,480},{40,488},{48,496},{56,5... | collective-permute-start | bytes 1597448 | tf_op jit(solution)/shard_map/ppermute | solution.py:356
  143.5 6.2 %collective-permute-start.23 = (bf16[32,8320]{1,0:T(8,128)(2,1)S(1)}, bf16[32,8320]{1,0:T(8,128)(2,1)S(1)}, u32[]{:S(2)}, u32[]{:S(2)}) collective-permute-start(bf16[32,8320]{1,0:T(8,128)(2,1)S(1)} %collective-permute-done.22), channel_id=1, source_target_pairs={{0,4},{4,0},{1,5},{5,1},{2,6},{6,2},{3,7},{7,3},{8,12},{12,8},{9,1... | collective-permute-start | bytes 1597448 | tf_op jit(solution)/shard_map/ppermute | solution.py:359
  145.4 5.9 %copy-start.19 = (bf16[32,8320]{1,0:T(8,128)(2,1)}, bf16[32,8320]{1,0:T(8,128)(2,1)S(1)}, u32[]{:S(2)}) copy-start(bf16[32,8320]{1,0:T(8,128)(2,1)S(1)} %collective-permute-done.7.refs_7_.refs_31_) | copy-start | bytes 1597444
  145.4 5.9 %collective-permute-start.25 = (bf16[32,8320]{1,0:T(8,128)(2,1)S(1)}, bf16[32,8320]{1,0:T(8,128)(2,1)}, u32[]{:S(2)}, u32[]{:S(2)}) collective-permute-start(bf16[32,8320]{1,0:T(8,128)(2,1)S(1)} %collective-permute-done.24), channel_id=1, source_target_pairs={{0,4},{4,0},{1,5},{5,1},{2,6},{6,2},{3,7},{7,3},{8,12},{12,8},{9,1... | collective-permute-start | bytes 1597448 | tf_op jit(solution)/shard_map/ppermute | solution.py:359
  149.7 1.7 copy-start.17
  149.7 1.7 copy-start.18
  150.5 0.9 copy-start.21
  220.6 7.4 %copy-start.7 = (f32[32,128]{1,0:T(8,128)S(1)}, f32[32,128]{1,0:T(8,128)}, u32[]{:S(2)}) copy-start(f32[32,128]{1,0:T(8,128)} %get-tuple-element.9) | copy-start | bytes 49156
  220.6 24.2 %all-to-all-start = ((f32[16,32,144]{2,1,0:T(8,128)}), f32[16,32,144]{2,1,0:T(8,128)S(1)}, u32[]{:S(2)}, u32[]{:S(2)}) async-start(f32[16,32,144]{2,1,0:T(8,128)} %bitcast.34), calls=%async_computation | async-start | bytes 1048576 | tf_op jit(solution)/shard_map/all_to_all | solution.py:441
  257.3 0.9 copy-start.12
  (1 other events, 0.8 us)
